TPU v7x, 32 devices: a whole 2x2x4 slice. The times are simulated.
32 devices in a mesh: gx: 4 (over y, x), gy: 4 (over z), gz: 2 (over core).
Axes of the slice: x: 2, y: 2, z: 4, core: 2. Of those that a mesh axis runs over, the one named last changes fastest.
Arguments:
- hidden: bfloat16 [4096, 2, 4096], P(('gx', 'gy', 'gz')), may hold values from -6 to 6
- norm_gain: float32 [4096], replicated, may hold values from 0.25 to 1.75
- prompt_of: int32 [4096], P(('gx', 'gy', 'gz')), may hold values from 0 to 255, as said below
- lengths: int32 [4096], P(('gx', 'gy', 'gz')), may hold values from 1 to 2
- reward_level: int32 [4096], P(('gx', 'gy', 'gz')), may hold values from 0 to 15
Outputs:
- weighted: bfloat16 [4096, 2, 4096], P(('gx', 'gy', 'gz'))
- advantages: float32 [4096], P(('gx', 'gy', 'gz'))
Inputs may be any that keep to these rules, and one draw needn't show every extreme that they name: `prompt_of`: each of the 256 prompts has exactly 16 completions; prompt p is owned by the device p // 8 in mesh order; the completions of one device include at most 5 whose prompts one owner holds, and exactly 5 for some owner.
All inputs are finite; a program needn't handle non-finite values.
Results may differ from a plain program's by a relative error of at most 0.0085.
Values may be sent and summed in bfloat16 or wider, within the bound.
No kernel may reach another device: no remote copies, remote signals or barrier semaphores. Data moves between devices by JAX's collectives and lax.ppermute only.
A program may use at most 64 MiB of HBM per device.

v0:
```python
import jax
import jax.numpy as jnp
from jax import lax
from jax.sharding import PartitionSpec as P

G = 16


norm_eps = 1e-05


def rms_scale(values_in, norm_gain):
    values = values_in.astype(jnp.float32)
    meansq = jnp.mean(values * values, axis=-1, keepdims=True)
    return (values * lax.rsqrt(meansq + norm_eps) * norm_gain).astype(jnp.bfloat16)


def on_device(hidden, norm_gain, prompt_of, lengths, reward_level):
    count_here, window, features = hidden.shape
    owners = lax.axis_size("gx") * lax.axis_size("gy") * lax.axis_size("gz")
    slot_count = max(2, count_here // owners + 1)
    groups = count_here // G
    owner_of = prompt_of // groups
    position = jnp.arange(count_here, dtype=jnp.int32)
    before_me = position[None, :] < position[:, None]
    same_owner = owner_of[:, None] == owner_of[None, :]
    send_slot = jnp.sum(same_owner & before_me, axis=1)
    member = prompt_of % groups
    labels = member + 1
    headers = jnp.stack([labels, reward_level, lengths], axis=1)
    slot_index = owner_of * slot_count + send_slot
    arrived = owners * slot_count
    outgoing = jnp.zeros((arrived, window, features), jnp.bfloat16).at[slot_index].set(hidden)
    header_out = jnp.zeros((arrived, 3), jnp.int32).at[slot_index].set(headers)
    incoming, header_in = (
        lax.all_to_all(outgoing, ("gx", "gy", "gz"), split_axis=0, concat_axis=0, tiled=True),
        lax.all_to_all(header_out, ("gx", "gy", "gz"), split_axis=0, concat_axis=0, tiled=True),
    )
    label_in = header_in[:, 0]
    filled = label_in > 0
    group_in = label_in - 1
    arrival = jnp.arange(arrived, dtype=jnp.int32)
    earlier_in = arrival[None, :] < arrival[:, None]
    same_group = (group_in[:, None] == group_in[None, :]) & filled[None, :]
    ranking_in = jnp.sum(same_group & earlier_in, axis=1)
    target = group_in * G + ranking_in
    target = jnp.where(filled, target, count_here)
    source = (
        jnp.zeros((count_here,), jnp.int32)
        .at[target]
        .set(jnp.arange(arrived, dtype=jnp.int32), mode="drop")
    )
    gathered = incoming[source]
    normed = rms_scale(gathered, norm_gain)
    levels = header_in[source, 1].astype(jnp.float32).reshape(groups, G)
    lengths_in = header_in[source, 2]
    average = jnp.mean(levels, axis=1, keepdims=True)
    centered = levels - average
    spread = jnp.sqrt(jnp.mean(centered * centered, axis=1, keepdims=True))
    advantages = (centered / jnp.maximum(spread, 1.0)).reshape(count_here)
    tokens_at = jnp.arange(window, dtype=jnp.int32)
    weight = jnp.where(
        tokens_at[None, :] < lengths_in[:, None],
        advantages[:, None] / lengths_in[:, None].astype(jnp.float32),
        0.0,
    )
    weighted = (normed.astype(jnp.float32) * weight[:, :, None]).astype(jnp.bfloat16)
    return (weighted, advantages)


def solution(mesh):
    in_specs = (
        P(("gx", "gy", "gz"), None, None),
        P(),
        P(("gx", "gy", "gz")),
        P(("gx", "gy", "gz")),
        P(("gx", "gy", "gz")),
    )
    out_specs = (P(("gx", "gy", "gz"), None, None), P(("gx", "gy", "gz")))
    return jax.shard_map(
        on_device, mesh=mesh, in_specs=in_specs, out_specs=out_specs, check_vma=False
    )
```

profile of v0, /device:TPU:0, one launch (start us, length us, event | category | flops | bytes accessed | tf_op | source)
XLA Modules:
  0.0 115.8 jit_solution(13540634410701664714)
XLA Ops:
  0.6 0.8 fusion.9
  1.5 0.2 convert_reduce_fusion.1
  1.6 0.7 pad_add_fusion
  2.3 0.1 copy.26
  2.4 0.9 scatter_custom_fusion.1
  3.3 0.1 copy.27
  3.4 0.1 all_to_all.12
  3.5 0.7 copy.28
  4.2 7.3 %all-to-all-start.1 = ((s32[32,5,3]{1,2,0:T(4,128)}), s32[32,5,3]{1,2,0:T(4,128)S(1)}, u32[]{:S(2)}, u32[]{:S(2)}) async-start(s32[32,5,3]{1,2,0:T(4,128)} %copy.28), calls=%async_computation.1 | async-start | bytes 131072 | tf_op jit(solution)/shard_map/all_to_all | solution.py:37
  11.5 4.2 %broadcast_in_dim.20 = bf16[160,2,4096]{2,1,0:T(2,128)(2,1)} broadcast(bf16[]{:T(256)} %constant.20.clone.1), dimensions={} | broadcast | bytes 2621442 | tf_op jit(solution)/shard_map/broadcast_in_dim | solution.py:33
  15.7 15.9 %scatter_fusion = bf16[160,2,4096]{2,1,0:T(2,128)(2,1)} fusion(bf16[160,2,4096]{2,1,0:T(2,128)(2,1)} %broadcast_in_dim.20, s32[128]{0:T(128)S(1)} %compare_select_fusion.2, bf16[128,2,4096]{2,1,0:T(2,128)(2,1)S(1)} %copy-done), kind=kCustom, calls=%fused_computation.3 | custom fusion | bytes 6291968 | tf_op jit(solution)/shard_map/scatter | solution.py:33
  31.6 0.0 all-to-all-done.1
  31.6 5.9 %all-to-all-start = ((bf16[160,2,4096]{2,1,0:T(2,128)(2,1)}), bf16[160,2,4096]{2,1,0:T(2,128)(2,1)}, u32[]{:S(2)}, u32[]{:S(2)}) async-start(bf16[160,2,4096]{2,1,0:T(2,128)(2,1)} %scatter_fusion), calls=%async_computation | async-start | bytes 5242880 | tf_op jit(solution)/shard_map/all_to_all | solution.py:36
  37.5 0.1 all_to_all.14
  37.7 0.2 convert_reduce_fusion
  37.9 1.3 %scatter_custom_fusion.2 = s32[128]{0:T(128)S(1)} fusion(s32[160]{0:T(256)S(1)} %bitcast.13, s32[160]{0:T(256)S(1)} %iota.24, s32[]{:T(128)} %constant.24.clone.1), kind=kCustom, calls=%fused_computation.45 | custom fusion | bytes 516 | tf_op jit(solution)/shard_map/scatter | solution.py:51
  39.2 1.5 %gather_fusion.2 = s32[128]{0:T(128)S(1)} fusion(s32[160,3]{0,1:T(4,128)S(1)} %all_to_all.14, s32[128]{0:T(128)S(1)} %broadcast_or_fusion), kind=kCustom, calls=%fused_computation.2 | custom fusion | bytes 2048 | tf_op jit(solution)/shard_map/gather | solution.py:55
  40.8 0.1 convert_element_type.45
  40.8 0.1 reduce_sum.51
  41.0 0.2 multiply_reduce_fusion
  41.2 0.1 div.53
  41.2 0.1 div.54
  41.3 0.1 sub.30
  41.4 0.1 sub.31
  41.5 1.6 %gather_fusion.1 = s32[128]{0:T(128)S(1)} fusion(s32[160,3]{0,1:T(4,128)S(1)} %all_to_all.14, s32[128]{0:T(128)S(1)} %get-tuple-element.2), kind=kCustom, calls=%fused_computation.1 | custom fusion | bytes 2048 | tf_op jit(solution)/shard_map/gather | solution.py:56
  43.0 0.5 subtract_divide_fusion
  43.6 0.1 fusion.5
  43.7 0.0 copy-start.1
  43.7 55.1 %all-to-all-done = bf16[160,2,4096]{2,1,0:T(2,128)(2,1)} async-done(((bf16[160,2,4096]{2,1,0:T(2,128)(2,1)}), bf16[160,2,4096]{2,1,0:T(2,128)(2,1)}, u32[]{:S(2)}, u32[]{:S(2)}) %all-to-all-start) | async-done | bytes 2621472 | tf_op jit(solution)/shard_map/all_to_all | solution.py:36
  98.8 9.3 %gather_fusion = bf16[128,2,4096]{2,1,0:T(2,128)(2,1)S(1)} fusion(bf16[160,2,4096]{2,1,0:T(2,128)(2,1)} %all-to-all-done, s32[1024]{0:T(1024)S(1)} %pad_clamp_fusion), kind=kCustom, calls=%fused_computation | custom fusion | bytes 4194816 | tf_op jit(solution)/shard_map/gather | solution.py:53
  108.1 2.2 %fusion = f32[128,2]{1,0:T(8,128)S(1)} fusion(bf16[128,2,4096]{2,1,0:T(2,128)(2,1)S(1)} %gather_fusion), kind=kLoop, calls=%fused_computation.8 | loop fusion | flops 3145472 | bytes 2098176 | tf_op jit(solution)/shard_map/reduce_sum | solution.py:14
  110.4 5.4 %multiply_convert_fusion = bf16[128,2,4096]{2,1,0:T(2,128)(2,1)} fusion(bf16[128,2,4096]{2,1,0:T(2,128)(2,1)S(1)} %gather_fusion, f32[128,2]{1,0:T(8,128)S(1)} %fusion.5, f32[4096]{0:T(1024)S(1)} %copy-done.1, f32[128,2]{1,0:T(8,128)S(1)} %add_rsqrt_fusion), kind=kLoop, calls=%fused_computation.11 | loop fusion | flops 7340032 | bytes 4212736 | tf_op jit(solution)/shard_map/convert_element_type | solution.py:67
  (16 shorter events, 0.1 us)
Async XLA Ops:
  0.6 15.1 %copy-start = (bf16[128,2,4096]{2,1,0:T(2,128)(2,1)S(1)}, bf16[128,2,4096]{2,1,0:T(2,128)(2,1)}, u32[]{:S(2)}) copy-start(bf16[128,2,4096]{2,1,0:T(2,128)(2,1)} %param.5) | copy-start | bytes 6291460
  4.2 27.4 %all-to-all-start.1 = ((s32[32,5,3]{1,2,0:T(4,128)}), s32[32,5,3]{1,2,0:T(4,128)S(1)}, u32[]{:S(2)}, u32[]{:S(2)}) async-start(s32[32,5,3]{1,2,0:T(4,128)} %copy.28), calls=%async_computation.1 | async-start | bytes 131072 | tf_op jit(solution)/shard_map/all_to_all | solution.py:37
  31.6 67.2 %all-to-all-start = ((bf16[160,2,4096]{2,1,0:T(2,128)(2,1)}), bf16[160,2,4096]{2,1,0:T(2,128)(2,1)}, u32[]{:S(2)}, u32[]{:S(2)}) async-start(bf16[160,2,4096]{2,1,0:T(2,128)(2,1)} %scatter_fusion), calls=%async_computation | async-start | bytes 5242880 | tf_op jit(solution)/shard_map/all_to_all | solution.py:36
  43.7 66.7 %copy-start.1 = (f32[4096]{0:T(1024)S(1)}, f32[4096]{0:T(1024)}, u32[]{:S(2)}) copy-start(f32[4096]{0:T(1024)} %param.6) | copy-start | bytes 49156
where the time goes:
time: 117 us; the launch traced here: 116 us
  waiting for transfers between devices  55.1 us (47%)
  local copies, waits for them, and re-layouts  36.1 us (31%)
  starting transfers between devices  13.2 us (11%)
  other arithmetic  10.5 us (9%)
    all_to_all x1, waiting for transfers between devices, on_device(): lax.all_to_all(outgoing, ('gx', 'gy', 'gz'), split_axis=0, concat_axis=0,...  55.1 us
    scatter x1, local copies, waits for them, and re-layouts, on_device(): jnp.zeros((arrived, window, features), jnp.bfloat16).at[slot_index]  15.9 us
    gather x1, local copies, waits for them, and re-layouts, on_device(): gathered = incoming[source]  9.33 us
    all_to_all x1, starting transfers between devices, on_device(): lax.all_to_all(header_out, ('gx', 'gy', 'gz'), split_axis=0, concat_axis=...  7.33 us
    all_to_all x1, starting transfers between devices, on_device(): lax.all_to_all(outgoing, ('gx', 'gy', 'gz'), split_axis=0, concat_axis=0,...  5.92 us
    convert_element_type x1, other arithmetic, on_device(): (normed.astype(jnp.float32) * weight[:, :, None]).astype(jnp.bfloat16)  5.38 us
    broadcast_in_dim x1, local copies, waits for them, and re-layouts, on_device(): jnp.zeros((arrived, window, features), jnp.bfloat16).at[slot_index]  4.16 us
  transfers between devices with their start and end apart: 2, of which 1 were waited for; matrix products, arithmetic and copies ran while one was open for 22% of the time, Pallas kernels for 0%

commit v1 on v0

v1 whole, which is shorter than its diff:
```python
import functools
import jax
import jax.numpy as jnp
from jax import lax
from jax.experimental import pallas as pl
from jax.experimental.pallas import tpu as pltpu
from jax.sharding import PartitionSpec as P

G = 16
AXES = ("gx", "gy", "gz")
STAGES = ("gz", "gx", "gy")
LANES = 128
norm_eps = 1e-05


def pack_body(cap, groups, prompt_ref, length_ref, gain_ref, rows_ref, out_ref,
              rows, wide, tokens, src, dst, count, first, in_sems, out_sem):
    total, pieces = rows.shape[0], in_sems.shape[0]
    piece = total // pieces
    half = wide.shape[1] // 2
    features = half * LANES
    for k in range(pieces):
        part = pl.ds(k * piece, piece)
        pltpu.make_async_copy(rows_ref.at[part], rows.at[part], in_sems.at[k]).start()

    def clear(o, _):
        count[o] = 0
        return 0
    lax.fori_loop(0, count.shape[0], clear, 0)

    def place(i, _):
        o = prompt_ref[i] // groups
        at = count[o]
        two = length_ref[i] > 1
        count[o] = at + jnp.where(two, 2, 1)
        base = o * cap

        @pl.when(at == 0)
        def _():
            first[o] = 2 * i
        head = first[o]
        ok0 = at < cap
        src[2 * i] = jnp.where(ok0, 2 * i, head)
        dst[2 * i] = base + jnp.where(ok0, at, 0)
        ok1 = two & (at + 1 < cap)
        src[2 * i + 1] = jnp.where(ok1, 2 * i + 1, src[2 * i])
        dst[2 * i + 1] = jnp.where(ok1, base + at + 1, dst[2 * i])
        return 0
    lax.fori_loop(0, total, place, 0)

    gain = gain_ref[...]
    batch = wide.shape[0]

    def work(j, _):
        for b in range(batch):
            i = j * batch + b
            wide[b] = rows[i].astype(jnp.float32)
            for t in range(2):
                x = wide[b, pl.ds(t, half, stride=2), :]
                s = jnp.sum(jnp.sum((x * x).reshape(half // 8, 8, LANES), axis=0), axis=1, keepdims=True)
                s = jnp.sum(s, axis=0, keepdims=True)
                r = lax.rsqrt(s * (1.0 / features) + norm_eps)
                tokens[2 * i + t] = (x * r * gain).astype(jnp.bfloat16)
        return 0

    def send(i, _):
        pltpu.make_async_copy(tokens.at[src[i]], out_ref.at[dst[i]], out_sem).start()
        return 0

    for k in range(pieces):
        part = pl.ds(k * piece, piece)
        pltpu.make_async_copy(rows_ref.at[part], rows.at[part], in_sems.at[k]).wait()
        lax.fori_loop(k * (piece // batch), (k + 1) * (piece // batch), work, 0)
        lax.fori_loop(k * 2 * piece, (k + 1) * 2 * piece, send, 0, unroll=8)
    pltpu.make_async_copy(tokens, tokens, out_sem).wait()


def unpack_body(slot_ref, weight_ref, tokens_ref, out_ref, tokens, wide, out, in_sem, out_sems):
    total, pieces = out.shape[0], out_sems.shape[0]
    piece = total // pieces
    half = wide.shape[1] // 2
    batch = wide.shape[0]
    pltpu.make_async_copy(tokens_ref, tokens, in_sem).start()
    pltpu.make_async_copy(tokens_ref, tokens, in_sem).wait()

    def work(j, _):
        for b in range(batch):
            i = j * batch + b
            for t in range(2):
                x = tokens[slot_ref[2 * i + t]].astype(jnp.float32)
                wide[b, pl.ds(t, half, stride=2), :] = x * weight_ref[2 * i + t]
            out[i] = wide[b].astype(jnp.bfloat16)
        return 0

    for k in range(pieces):
        part = pl.ds(k * piece, piece)
        lax.fori_loop(k * (piece // batch), (k + 1) * (piece // batch), work, 0)
        pltpu.make_async_copy(out.at[part], out_ref.at[part], out_sems.at[k]).start()
    for k in range(pieces):
        part = pl.ds(k * piece, piece)
        pltpu.make_async_copy(out.at[part], out_ref.at[part], out_sems.at[k]).wait()


def pack(rows, gain, prompt_of, lengths, owners, cap, groups):
    total, width, _ = rows.shape
    half = width // 2
    smem, vmem = pl.BlockSpec(memory_space=pltpu.SMEM), pl.BlockSpec(memory_space=pltpu.VMEM)
    return pl.pallas_call(
        functools.partial(pack_body, cap, groups),
        out_shape=jax.ShapeDtypeStruct((owners * cap, half, LANES), jnp.bfloat16),
        in_specs=[smem, smem, vmem, pl.BlockSpec(memory_space=pl.ANY)],
        out_specs=pl.BlockSpec(memory_space=pl.ANY),
        scratch_shapes=[
            pltpu.VMEM(rows.shape, jnp.bfloat16),
            pltpu.VMEM((4, width, LANES), jnp.float32),
            pltpu.VMEM((2 * total, half, LANES), jnp.bfloat16),
            pltpu.SMEM((2 * total,), jnp.int32),
            pltpu.SMEM((2 * total,), jnp.int32),
            pltpu.SMEM((owners,), jnp.int32),
            pltpu.SMEM((owners,), jnp.int32),
            pltpu.SemaphoreType.DMA((8,)),
            pltpu.SemaphoreType.DMA,
        ],
        name="pack",
    )(prompt_of, lengths, gain, rows)


def unpack(slots, weights, tokens, total):
    count, half, _ = tokens.shape
    smem, hbm = pl.BlockSpec(memory_space=pltpu.SMEM), pl.BlockSpec(memory_space=pl.ANY)
    return pl.pallas_call(
        unpack_body,
        out_shape=jax.ShapeDtypeStruct((total, 2 * half, LANES), jnp.bfloat16),
        in_specs=[smem, smem, hbm],
        out_specs=hbm,
        scratch_shapes=[
            pltpu.VMEM(tokens.shape, jnp.bfloat16),
            pltpu.VMEM((4, 2 * half, LANES), jnp.float32),
            pltpu.VMEM((total, 2 * half, LANES), jnp.bfloat16),
            pltpu.SemaphoreType.DMA,
            pltpu.SemaphoreType.DMA((8,)),
        ],
        name="unpack",
    )(slots, weights, tokens)


def partner(size, index, step):
    return index ^ step if size & (size - 1) == 0 else (index + step) % size


def origin(size, index, step):
    return index ^ step if size & (size - 1) == 0 else (index + size - step) % size


def on_device(hidden, norm_gain, prompt_of, lengths, reward_level):
    count_here, window, features = hidden.shape
    sizes = {a: lax.axis_size(a) for a in AXES}
    owners = sizes["gx"] * sizes["gy"] * sizes["gz"]
    slot_count = max(2, count_here // owners + 1)
    cap = window * slot_count
    groups = count_here // G
    half = features // LANES
    coord = {a: lax.axis_index(a) for a in AXES}
    me = (coord["gx"] * sizes["gy"] + coord["gy"]) * sizes["gz"] + coord["gz"]

    rows = hidden.reshape(count_here, window, half, LANES).transpose(0, 2, 1, 3)
    rows = rows.reshape(count_here, window * half, LANES)
    sent = pack(rows, norm_gain.reshape(half, LANES), prompt_of, lengths, owners, cap, groups)
    came = lax.all_to_all(sent, AXES, split_axis=0, concat_axis=0, tiled=True)

    known = jnp.stack([prompt_of, lengths, reward_level])[None]
    source = me[None]
    weight_of = {"gx": sizes["gy"] * sizes["gz"], "gy": sizes["gz"], "gz": 1}
    for a in STAGES:
        blocks, ids = [known], [source]
        for k in range(1, sizes[a]):
            pairs = [(i, partner(sizes[a], i, k)) for i in range(sizes[a])]
            blocks.append(lax.ppermute(known, a, pairs))
            ids.append(source + (origin(sizes[a], coord[a], k) - coord[a]) * weight_of[a])
        known, source = jnp.concatenate(blocks), jnp.concatenate(ids)

    f32 = jnp.float32
    prompts, lens, levels = known[:, 0], known[:, 1], known[:, 2]
    mine = prompts // groups == me
    spot = jnp.arange(count_here)
    before = (spot[:, None] < spot[None, :]).astype(f32)
    group = jnp.arange(groups)
    same = (prompts[None] == me * groups + group[:, None, None]).astype(f32)
    within = jnp.einsum("gsj,jk->gsk", same, before, preferred_element_type=f32)
    earlier = (source[:, None] < source[None, :]).astype(f32)
    ahead = jnp.einsum("gs,sr->gr", jnp.sum(same, axis=2), earlier, precision=lax.Precision.HIGHEST)
    target = jnp.sum(same * (within + ahead[:, :, None] + (G * group + 1).astype(f32)[:, None, None]), axis=0) - 1
    live = jnp.where(mine, lens, 0)
    at = jnp.dot(live.astype(f32), before, preferred_element_type=f32).astype(jnp.int32)
    code = ((source[:, None] * cap + at) * 16 + levels) * 4 + lens
    hit = target.astype(jnp.int32)[None] == spot[:, None, None]
    code = jnp.sum(jnp.where(hit, code[None], 0), axis=(1, 2))
    size, level, slot = code % 4, (code // 4) % 16, code // 64

    levels = level.astype(f32).reshape(groups, G)
    average = jnp.mean(levels, axis=1, keepdims=True)
    centered = levels - average
    spread = jnp.sqrt(jnp.mean(centered * centered, axis=1, keepdims=True))
    advantages = (centered / jnp.maximum(spread, 1.0)).reshape(count_here)
    t = jnp.arange(window)
    alive = t[None, :] < size[:, None]
    weight = jnp.where(alive, advantages[:, None] / size[:, None].astype(f32), 0.0)
    slots = slot[:, None] + jnp.where(alive, t[None, :], 0)
    out = unpack(slots.reshape(-1), weight.reshape(-1), came, count_here)
    out = out.reshape(count_here, half, window, LANES).transpose(0, 2, 1, 3)
    return out.reshape(count_here, window, features), advantages


def solution(mesh):
    many = P(AXES)
    return jax.shard_map(
        on_device, mesh=mesh,
        in_specs=(P(AXES, None, None), P(), many, many, many),
        out_specs=(P(AXES, None, None), many), check_vma=False,
    )
```

time: 117 us -> 90.8 us (0.78)
  local copies, waits for them, and re-layouts: 36.1 us -> 2.94 us
  Pallas kernels: 0 us -> 13.3 us
  other arithmetic: 10.5 us -> 4.83 us
  waiting for transfers between devices: 55.1 us -> 50.7 us
  starting transfers between devices: 13.2 us -> 17.5 us
    all_to_all x2 -> x1, waiting for transfers between devices: 55.1 us -> 0.01 us  [on_device(): came = lax.all_to_all(sent, AXES, split_axis=0, concat_axis=0, tiled=True)]
    ppermute x0 -> x7, waiting for transfers between devices: none -> 50.7 us  [on_device(): blocks.append(lax.ppermute(known, a, pairs))]
    scatter x4 -> x0, local copies, waits for them, and re-layouts: 18.1 us -> none  [the longest x1 15.9 us: on_device(): jnp.zeros((arrived, window, features), jnp.bfloat16).at[slot_index]]
    pallas_call x0 -> x2, Pallas kernels: none -> 13.3 us  [the longest x1 9.25 us: pack(): pl.pallas_call(functools.partial(pack_body, cap, groups), out_shape=jax.S...]
    gather x3 -> x0, local copies, waits for them, and re-layouts: 12.4 us -> none  [the longest x1 9.33 us: on_device(): gathered = incoming[source]]
    ppermute x0 -> x7, starting transfers between devices: none -> 10.1 us  [on_device(): blocks.append(lax.ppermute(known, a, pairs))]
    all_to_all x2 -> x1, starting transfers between devices: 13.2 us -> 7.34 us  [on_device(): came = lax.all_to_all(sent, AXES, split_axis=0, concat_axis=0, tiled=True)]
    convert_element_type x2, other arithmetic: 5.38 us -> 0.01 us  [the longest x1 0.01 us: on_device(): hit = target.astype(jnp.int32)[None] == spot[:, None, None]]
  transfers between devices with their start and end apart: 2 -> 8, of which waited for: 1 -> 4; matrix products, arithmetic and copies ran while one was open for 22% -> 8% of each run, Pallas kernels for 0% -> 0%
where the time goes in v1:
time: 90.8 us; the launch traced here: 90.5 us
  waiting for transfers between devices  50.7 us (56%)
  starting transfers between devices  17.5 us (19%)
  Pallas kernels  13.3 us (15%)
  other arithmetic  4.83 us (5%)
  local copies, waits for them, and re-layouts  2.94 us (3%)
    ppermute x7, waiting for transfers between devices, on_device(): blocks.append(lax.ppermute(known, a, pairs))  50.7 us
    ppermute x7, starting transfers between devices, on_device(): blocks.append(lax.ppermute(known, a, pairs))  10.1 us
    pallas_call x1, Pallas kernels, pack(): pl.pallas_call(functools.partial(pack_body, cap, groups), out_shape=jax.S...  9.25 us
    all_to_all x1, starting transfers between devices, on_device(): came = lax.all_to_all(sent, AXES, split_axis=0, concat_axis=0, tiled=True)  7.34 us
    pallas_call x1, Pallas kernels, unpack(): pl.pallas_call(unpack_body, out_shape=jax.ShapeDtypeStruct((total, 2 * ha...  4.05 us
    reduce_sum x1, other arithmetic, on_device(): code = jnp.sum(jnp.where(hit, code[None], 0), axis=(1, 2))  2.36 us
  transfers between devices with their start and end apart: 8, of which 4 were waited for; matrix products, arithmetic and copies ran while one was open for 8% of the time, Pallas kernels for 0%

profile of v1, /device:TPU:0, one launch (start us, length us, event | category | flops | bytes accessed | tf_op | source)
XLA Modules:
  0.0 90.5 jit_solution(5058601125481710751)
XLA Ops:
  0.6 9.2 %pack.1 = bf16[320,32,128]{2,1,0:T(8,128)(2,1)} custom-call(s32[128]{0:T(128)} %prompt_ref.1, s32[128]{0:T(128)} %length_ref.1, f32[32,128]{1,0:T(8,128)} %bitcast.43, bf16[128,64,128]{2,1,0:T(8,128)(2,1)} %bitcast.42), custom_call_target="tpu_custom_call" | custom-call | tf_op jit(solution)/shard_map/pack/pallas_call | solution.py:108
  9.9 7.3 %all-to-all-start = ((bf16[320,32,128]{2,1,0:T(8,128)(2,1)}), bf16[320,32,128]{2,1,0:T(8,128)(2,1)S(1)}, u32[]{:S(2)}, u32[]{:S(2)}) async-start(bf16[320,32,128]{2,1,0:T(8,128)(2,1)} %pack.1), calls=%async_computation | async-start | bytes 5242880 | tf_op jit(solution)/shard_map/all_to_all | solution.py:169
  17.3 0.3 collective-permute-start
  17.9 0.1 concatenate.43
  18.0 0.6 collective-permute-done
  18.6 2.7 %collective-permute-start.3 = (s32[2,3,128]{2,0,1:T(2,128)S(1)}, s32[2,3,128]{2,0,1:T(2,128)S(1)}, u32[]{:S(2)}, u32[]{:S(2)}) collective-permute-start(s32[2,3,128]{2,0,1:T(2,128)S(1)} %pad_add_fusion), channel_id=1, source_target_pairs={{0,24},{8,16},{16,8},{24,0},{1,25},{9,17},{17,9},{25,1},{2,26},{10... | collective-permute-start | bytes 9224 | tf_op jit(solution)/shard_map/ppermute | solution.py:178
  21.3 0.6 collective-permute-start.2
  21.9 0.3 collective-permute-start.1
  22.1 12.1 %collective-permute-done.3 = s32[2,3,128]{2,0,1:T(2,128)S(1)} collective-permute-done((s32[2,3,128]{2,0,1:T(2,128)S(1)}, s32[2,3,128]{2,0,1:T(2,128)S(1)}, u32[]{:S(2)}, u32[]{:S(2)}) %collective-permute-start.3) | collective-permute-done | bytes 3104 | tf_op jit(solution)/shard_map/ppermute | solution.py:178
  34.2 5.6 %collective-permute-start.6 = (s32[8,3,128]{2,0,1:T(8,128)S(1)}, s32[8,3,128]{2,0,1:T(8,128)S(1)}, u32[]{:S(2)}, u32[]{:S(2)}) collective-permute-start(s32[8,3,128]{2,0,1:T(8,128)S(1)} %concatenate.39), channel_id=1, source_target_pairs={{0,6},{2,4},{4,2},{6,0},{1,7},{3,5},{5,3},{7,1},{8,14},{10,12},{12... | collective-permute-start | bytes 36872 | tf_op jit(solution)/shard_map/ppermute | solution.py:178
  39.8 0.6 collective-permute-start.4
  40.5 0.1 lt.74
  40.6 24.3 %collective-permute-done.6 = s32[8,3,128]{2,0,1:T(8,128)S(1)} collective-permute-done((s32[8,3,128]{2,0,1:T(8,128)S(1)}, s32[8,3,128]{2,0,1:T(8,128)S(1)}, u32[]{:S(2)}, u32[]{:S(2)}) %collective-permute-start.6) | collective-permute-done | bytes 12320 | tf_op jit(solution)/shard_map/ppermute | solution.py:178
  65.0 13.7 %collective-permute-done.5 = s32[8,3,128]{2,0,1:T(8,128)S(1)} collective-permute-done((s32[8,3,128]{2,0,1:T(8,128)S(1)}, s32[8,3,128]{2,0,1:T(8,128)S(1)}, u32[]{:S(2)}, u32[]{:S(2)}) %collective-permute-start.5) | collective-permute-done | bytes 12320 | tf_op jit(solution)/shard_map/ppermute | solution.py:178
  78.7 0.2 fusion.6
  78.9 0.2 fusion.24
  79.0 0.2 fusion.2
  79.3 0.1 fusion.15
  79.4 2.4 %select_reduce_fusion = s32[128]{0:T(128)S(1)} fusion(s32[32,128]{1,0:T(8,128)S(1)} %fusion.15, s32[32,128]{1,0:T(8,128)S(1)} %add_convert_fusion), kind=kLoop, calls=%fused_computation | loop fusion | flops 1572736 | bytes 33280 | tf_op jit(solution)/shard_map/reduce_sum | solution.py:197
  81.8 0.1 reduce_sum.50
  81.9 0.1 fusion.48
  82.0 0.2 multiply_reduce_fusion
  82.3 0.1 div.88
  82.4 0.1 sub.74
  82.5 0.6 fusion.46
  83.2 0.2 broadcast_in_dim.68
  83.4 0.1 add.192
  83.6 0.2 lt.77
  83.8 0.6 select_add_fusion.slot_ref
  84.4 0.6 broadcast_select_fusion.weight_ref
  85.0 1.5 %copy-done = bf16[320,32,128]{2,1,0:T(8,128)(2,1)} copy-done((bf16[320,32,128]{2,1,0:T(8,128)(2,1)}, bf16[320,32,128]{2,1,0:T(8,128)(2,1)S(1)}, u32[]{:S(2)}) %copy-start) | copy-done | bytes 2621464
  86.5 4.1 %unpack.1 = bf16[128,64,128]{2,1,0:T(8,128)(2,1)} custom-call(s32[256]{0:T(256)} %select_add_fusion.slot_ref, f32[256]{0:T(256)} %broadcast_select_fusion.weight_ref, bf16[320,32,128]{2,1,0:T(8,128)(2,1)} %copy-done), custom_call_target="tpu_custom_call" | custom-call | tf_op jit(solution)/shard_map/unpack/pallas_call | solution.py:131
  (35 shorter events, 0.8 us)
Async XLA Ops:
  9.9 7.4 %copy-start.1 = (s32[128]{0:T(128)S(1)}, s32[128]{0:T(128)}, u32[]{:S(2)}) copy-start(s32[128]{0:T(128)} %length_ref.1) | copy-start | bytes 1540
  9.9 7.4 %copy-start.2 = (s32[128]{0:T(128)S(1)}, s32[128]{0:T(128)}, u32[]{:S(2)}) copy-start(s32[128]{0:T(128)} %prompt_ref.1) | copy-start | bytes 1540
  9.9 7.4 %copy-start.3 = (s32[128]{0:T(128)S(1)}, s32[128]{0:T(128)}, u32[]{:S(2)}) copy-start(s32[128]{0:T(128)} %param.9) | copy-start | bytes 1540
  9.9 75.1 %all-to-all-start = ((bf16[320,32,128]{2,1,0:T(8,128)(2,1)}), bf16[320,32,128]{2,1,0:T(8,128)(2,1)S(1)}, u32[]{:S(2)}, u32[]{:S(2)}) async-start(bf16[320,32,128]{2,1,0:T(8,128)(2,1)} %pack.1), calls=%async_computation | async-start | bytes 5242880 | tf_op jit(solution)/shard_map/all_to_all | solution.py:169
  17.3 1.2 %collective-permute-start = (s32[1,3,128]{2,0,1:T(1,128)S(1)}, s32[1,3,128]{2,0,1:T(1,128)S(1)}, u32[]{:S(2)}, u32[]{:S(2)}) collective-permute-start(s32[1,3,128]{2,0,1:T(1,128)S(1)} %broadcast_in_dim.38), channel_id=1, source_target_pairs={{0,1},{1,0},{2,3},{3,2},{4,5},{5,4},{6,7},{7,6},{8,9},{9,8},{10,11... | collective-permute-start | bytes 4616 | tf_op jit(solution)/shard_map/ppermute | solution.py:178
  18.6 15.6 %collective-permute-start.3 = (s32[2,3,128]{2,0,1:T(2,128)S(1)}, s32[2,3,128]{2,0,1:T(2,128)S(1)}, u32[]{:S(2)}, u32[]{:S(2)}) collective-permute-start(s32[2,3,128]{2,0,1:T(2,128)S(1)} %pad_add_fusion), channel_id=1, source_target_pairs={{0,24},{8,16},{16,8},{24,0},{1,25},{9,17},{17,9},{25,1},{2,26},{10... | collective-permute-start | bytes 9224 | tf_op jit(solution)/shard_map/ppermute | solution.py:178
  21.3 12.9 %collective-permute-start.2 = (s32[2,3,128]{2,0,1:T(2,128)S(1)}, s32[2,3,128]{2,0,1:T(2,128)S(1)}, u32[]{:S(2)}, u32[]{:S(2)}) collective-permute-start(s32[2,3,128]{2,0,1:T(2,128)S(1)} %pad_add_fusion), channel_id=1, source_target_pairs={{0,16},{8,24},{16,0},{24,8},{1,17},{9,25},{17,1},{25,9},{2,18},{10... | collective-permute-start | bytes 9224 | tf_op jit(solution)/shard_map/ppermute | solution.py:178
  21.9 12.3 %collective-permute-start.1 = (s32[2,3,128]{2,0,1:T(2,128)S(1)}, s32[2,3,128]{2,0,1:T(2,128)S(1)}, u32[]{:S(2)}, u32[]{:S(2)}) collective-permute-start(s32[2,3,128]{2,0,1:T(2,128)S(1)} %pad_add_fusion), channel_id=1, source_target_pairs={{0,8},{8,0},{16,24},{24,16},{1,9},{9,1},{17,25},{25,17},{2,10},{10... | collective-permute-start | bytes 9224 | tf_op jit(solution)/shard_map/ppermute | solution.py:178
  34.2 30.8 %collective-permute-start.6 = (s32[8,3,128]{2,0,1:T(8,128)S(1)}, s32[8,3,128]{2,0,1:T(8,128)S(1)}, u32[]{:S(2)}, u32[]{:S(2)}) collective-permute-start(s32[8,3,128]{2,0,1:T(8,128)S(1)} %concatenate.39), channel_id=1, source_target_pairs={{0,6},{2,4},{4,2},{6,0},{1,7},{3,5},{5,3},{7,1},{8,14},{10,12},{12... | collective-permute-start | bytes 36872 | tf_op jit(solution)/shard_map/ppermute | solution.py:178
  39.8 38.8 %collective-permute-start.5 = (s32[8,3,128]{2,0,1:T(8,128)S(1)}, s32[8,3,128]{2,0,1:T(8,128)S(1)}, u32[]{:S(2)}, u32[]{:S(2)}) collective-permute-start(s32[8,3,128]{2,0,1:T(8,128)S(1)} %concatenate.39), channel_id=1, source_target_pairs={{0,4},{2,6},{4,0},{6,2},{1,5},{3,7},{5,1},{7,3},{8,12},{10,14},{12... | collective-permute-start | bytes 36872 | tf_op jit(solution)/shard_map/ppermute | solution.py:178
  39.8 38.8 %collective-permute-start.4 = (s32[8,3,128]{2,0,1:T(8,128)S(1)}, s32[8,3,128]{2,0,1:T(8,128)S(1)}, u32[]{:S(2)}, u32[]{:S(2)}) collective-permute-start(s32[8,3,128]{2,0,1:T(8,128)S(1)} %concatenate.39), channel_id=1, source_target_pairs={{0,2},{2,0},{4,6},{6,4},{1,3},{3,1},{5,7},{7,5},{8,10},{10,8},{12,... | collective-permute-start | bytes 36872 | tf_op jit(solution)/shard_map/ppermute | solution.py:178
  85.0 1.5 %copy-start = (bf16[320,32,128]{2,1,0:T(8,128)(2,1)}, bf16[320,32,128]{2,1,0:T(8,128)(2,1)S(1)}, u32[]{:S(2)}) copy-start(bf16[320,32,128]{2,1,0:T(8,128)(2,1)S(1)} %all-to-all-done.tokens_ref) | copy-start | bytes 7864324

commit v2 on v0

v2 whole, which is shorter than its diff:
```python
import functools
import jax
import numpy as np
import jax.numpy as jnp
from jax import lax
from jax.experimental import pallas as pl
from jax.experimental.pallas import tpu as pltpu
from jax.sharding import PartitionSpec as P

G = 16
AXES = ("gx", "gy", "gz")
STAGES = ("gz", "gx", "gy")
LANES = 128
BATCH = 4
norm_eps = 1e-05


def pack_body(cap, slots, groups, prompt_ref, length_ref, level_ref, gain_ref, rows_ref,
              out_ref, spill_ref, table_ref, code_ref,
              rows, wide, tokens, src, dst, count, first, in_sems, out_sem):
    total, pieces = rows.shape[0], in_sems.shape[0]
    piece = total // pieces
    batch = wide.shape[0]
    half = wide.shape[1] // 2
    features = half * LANES
    limit = spill_ref.shape[0]
    owners = count.shape[0]
    for k in range(pieces):
        part = pl.ds(k * piece, piece)
        pltpu.make_async_copy(rows_ref.at[part], rows.at[part], in_sems.at[k]).start()

    for o in range(count.shape[0]):
        count[o] = 0
        first[o] = 0
    for e in range(table_ref.shape[0]):
        table_ref[e] = 0
    for e in range(code_ref.shape[0]):
        code_ref[e] = 0
    gain = gain_ref[...]

    def place(i, spilled):
        p = prompt_ref[i]
        n = length_ref[i]
        o = lax.div(p, groups)
        held = count[o]
        at, nth = held & 255, held >> 8
        count[o] = held + 256 + n
        field = nth * owners + o
        table_ref[field] = p - o * groups + 1
        table_ref[field + slots * owners] = n
        table_ref[field + 2 * slots * owners] = level_ref[i]
        base = o * cap
        head = jnp.where(at == 0, 2 * i, first[o])
        first[o] = head
        ok0 = at < cap
        s0 = jnp.where(ok0, 2 * i, head)
        d0 = base + jnp.where(ok0, at, 0)
        two = n > 1
        ok1 = two & (at + 1 < cap)
        src[2 * i], dst[2 * i] = s0, d0
        src[2 * i + 1] = jnp.where(ok1, 2 * i + 1, s0)
        dst[2 * i + 1] = jnp.where(ok1, d0 + 1, d0)
        if code_ref.shape[0] > limit:
            mark = (o * 256 + at) * 1024
            code_ref[jnp.minimum(spilled, limit)] = mark + 2 * i + 1
            spilled = spilled + jnp.where(ok0, 0, 1)
            code_ref[jnp.minimum(spilled, limit)] = mark + 1024 + 2 * i + 2
            spilled = spilled + jnp.where(two & (at + 1 >= cap), 1, 0)
        return spilled

    def send(i):
        pltpu.make_async_copy(tokens.at[src[i]], out_ref.at[dst[i]], out_sem).start()

    def work(j):
        for b in range(batch):
            i = j * batch + b
            wide[b] = rows[i].astype(jnp.float32)
        for b in range(batch):
            i = j * batch + b
            for t in range(2):
                x = wide[b, pl.ds(t, half, stride=2), :]
                s = jnp.sum((x * x).reshape(half // 8, 8, LANES), axis=0)
                s = jnp.sum(jnp.sum(s, axis=1, keepdims=True), axis=0, keepdims=True)
                r = lax.rsqrt(s * (1.0 / features) + norm_eps)
                tokens[2 * i + t] = (x * r * gain).astype(jnp.bfloat16)

    def step(j, spilled):
        for b in range(2 * batch):
            send((j - 1) * 2 * batch + b)
        for b in range(batch):
            spilled = place(j * batch + b, spilled)
        work(j)
        return spilled

    per = piece // batch

    def load(k):
        part = pl.ds(k * piece, piece)
        pltpu.make_async_copy(rows_ref.at[part], rows.at[part], in_sems.at[k]).wait()

    def chunk(k, spilled):
        load(k)
        return lax.fori_loop(k * per, (k + 1) * per, step, spilled)

    spilled = jnp.int32(0)
    for b in range(batch):
        spilled = place(b, spilled)
    load(0)
    work(0)
    spilled = lax.fori_loop(1, per, step, spilled)
    spilled = lax.fori_loop(1, pieces, chunk, spilled)
    for b in range(2 * batch):
        send(2 * (total - batch) + b)
    for o in range(owners):
        table_ref[3 * slots * owners + o] = jnp.maximum((count[o] & 255) - cap, 0)
    if code_ref.shape[0] > limit:
        for e in range(limit):
            code = jnp.where(e < spilled, code_ref[e], 0)
            code_ref[e] = code
            spill_ref[e] = tokens[jnp.maximum((code & 1023) - 1, 0)]
    else:
        spill_ref[...] = jnp.zeros(spill_ref.shape, spill_ref.dtype)
    pltpu.make_async_copy(rows_ref, rows, out_sem).wait()


def select(parts, near_axes, axis, room, spot_ref, shape):
    f32 = jnp.float32
    size, stride, mine = axis
    moved, offset = None, jnp.zeros((1, LANES), f32)
    for ref in parts:
        p = ref.shape[0]
        info = ref[:, shape[0]:shape[0] + LANES].astype(f32)
        dest = info[:, 1:2].astype(jnp.int32)
        lane = lax.broadcasted_iota(jnp.int32, (p, LANES), 1)
        go = (lane < (size - 1) * room) & (info[:, 0:1] > 0)
        for n, st, at in near_axes:
            go = go & (((dest >> st) & (n - 1)) == spot_ref[at])
        turn = lane & (room - 1)
        to = spot_ref[mine] ^ ((lane >> (room.bit_length() - 1)) + 1)
        go = jnp.where(go & (((dest >> stride) & (size - 1)) == to), 1.0, 0.0)
        row = lax.broadcasted_iota(jnp.int32, (p, p), 0)
        col = lax.broadcasted_iota(jnp.int32, (p, p), 1)
        nth = jnp.dot(jnp.where(col < row, 1.0, 0.0), go, preferred_element_type=f32) + offset
        offset = offset + jnp.sum(go, axis=0, keepdims=True)
        pick = jnp.where(nth == turn.astype(f32), go, 0.0)[:, :(size - 1) * room]
        data = ref[:, :shape[0] + LANES].astype(f32)
        part = lax.dot_general(pick, data, (((0,), (0,)), ((), ())), preferred_element_type=f32)
        moved = part if moved is None else moved + part
    return moved


def crowding(known, owners, fields, near_axes, axis, room, spot_ref):
    f32 = jnp.float32
    size, stride, mine = axis
    o = lax.broadcasted_iota(jnp.int32, (owners, LANES), 0)
    b = lax.broadcasted_iota(jnp.int32, (owners, LANES), 1)
    at = (o >> stride) & (size - 1)
    place = at
    span = size
    for n, st, _ in near_axes:
        place = place + span * ((o >> st) & (n - 1))
        span *= n
    member = jnp.where((place == b) & (at != spot_ref[mine]), 1.0, 0.0)
    total = jnp.zeros((1, LANES), f32)
    for k in known:
        left = jnp.sum(k[:, fields - owners:fields], axis=0, keepdims=True)
        total = total + jnp.dot(left, member, preferred_element_type=f32)
    return jnp.max(jnp.where(total > room, 1.0, 0.0), axis=1, keepdims=True)


def first_body(near_axes, axis, room, owners, fields, spot_ref, code_ref, table_ref, spill_ref, hold_ref, send_ref, table, wide, sem):
    f32 = jnp.float32
    limit, half, _ = spill_ref.shape
    features = half * LANES
    fetch = pltpu.make_async_copy(table_ref, table, sem)
    fetch.start()
    wide[...] = spill_ref[...].astype(f32)
    for c in range(half):
        hold_ref[:, c * LANES:(c + 1) * LANES] = wide[:, c, :].astype(jnp.bfloat16)
    row = lax.broadcasted_iota(jnp.int32, (limit, LANES), 0)
    lane = lax.broadcasted_iota(jnp.int32, (limit, LANES), 1)
    info = jnp.zeros((limit, LANES), jnp.int32)
    for e in range(limit):
        code = code_ref[e]
        used = jnp.where(code > 0, 1, 0)
        mark = code >> 10
        value = jnp.where(lane == 0, used, jnp.where(lane == 1, mark >> 8, jnp.where(lane == 2, spot_ref[3], jnp.where(lane == 3, mark & 255, 0))))
        info = jnp.where((row == e) & (code > 0), value, info)
    hold_ref[:, features:features + LANES] = info.astype(f32).astype(jnp.bfloat16)
    fetch.wait()
    width = table.shape[0] * LANES
    own = jnp.concatenate([table[r:r + 1, :] for r in range(table.shape[0])], axis=1).astype(f32)
    first = lax.broadcasted_iota(jnp.int32, (limit, width), 0) == 0
    known = jnp.where(first, own, 0.0)
    hold_ref[:, features + LANES:] = known.astype(jnp.bfloat16)
    left = jnp.sum(own[:, fields - owners:fields], axis=1, keepdims=True)
    bad = jnp.where(left > limit, 1.0, 0.0)
    bad = jnp.maximum(bad, crowding([known], owners, fields, near_axes, axis, room, spot_ref))
    moved = select([hold_ref], near_axes, axis, room, spot_ref, (features,))
    finish(moved, [known], bad, room, features, send_ref)


def finish(moved, known, bad, room, features, send_ref):
    rows = moved.shape[0]
    lane = lax.broadcasted_iota(jnp.int32, (rows, LANES), 1)
    info = jnp.where(lane == 4, bad, jnp.where(lane < 4, moved[:, features:], 0.0))
    for k in range(send_ref.shape[0]):
        part = slice(k * room, (k + 1) * room)
        send_ref[k, :, :features] = moved[part, :features].astype(jnp.bfloat16)
        send_ref[k, :, features:features + LANES] = info[part].astype(jnp.bfloat16)
        at = features + LANES
        for v in known:
            send_ref[k, :, at:at + v.shape[1]] = v.astype(jnp.bfloat16)
            at += v.shape[1]


def next_body(near_axes, axis, room, owners, fields, width, count, features, parts, recent, spot_ref, *refs):
    f32 = jnp.float32
    holds, own_ref, send_ref = refs[:parts], refs[parts], refs[parts + 1]
    came = holds[parts - recent:]
    at = features + LANES
    blocks = (own_ref.shape[1] - at) // width
    bad = None
    known = []
    for i, ref in enumerate((own_ref, *came)):
        flag = jnp.max(ref[:, features:features + LANES].astype(f32)[:, 4:5], axis=0, keepdims=True)
        bad = flag if bad is None else jnp.maximum(bad, flag)
        for j in range(blocks):
            value = ref[:, at + j * width:at + (j + 1) * width].astype(f32)
            if count >= room:
                known.append(value)
                continue
            rows = ref.shape[0]
            to = lax.broadcasted_iota(jnp.int32, (room, rows), 0)
            source = lax.broadcasted_iota(jnp.int32, (room, rows), 1)
            shift = (i * count) % room
            put = jnp.where((to == source + shift) & (source < count), 1.0, 0.0)
            value = jnp.dot(put, value, preferred_element_type=f32)
            if (i * count) // room == len(known):
                known.append(value)
            else:
                known[-1] = known[-1] + value
    bad = jnp.maximum(bad, crowding(known, owners, fields, near_axes, axis, room, spot_ref))
    moved = select(holds, near_axes, axis, room, spot_ref, (features,))
    finish(moved, known, bad, room, features, send_ref)


def final_body(cap, slots, owners, fields, width, features, groups, parts, spot_ref, id_col_ref, id_row_ref, tokens_ref, *refs):
    f32, i32 = jnp.float32, jnp.int32
    known_refs, holds = refs[:parts[0]], refs[parts[0]:parts[0] + parts[1]]
    out_ref, adv_ref, tokens, wide, out, extra, slot_v, weight_v, slot_s, weight_s, in_sem, table_sems, out_sems = refs[parts[0] + parts[1]:]
    total, pieces = out.shape[0], out_sems.shape[0]
    main = tokens_ref.shape[0]
    half = features // LANES
    fetch = pltpu.make_async_copy(tokens_ref, tokens.at[pl.ds(0, main)], in_sem)
    fetch.start()

    lane = lax.broadcasted_iota(i32, (width, LANES), 0)
    column = lax.broadcasted_iota(i32, (width, LANES), 1)
    mine = jnp.where(((lane >> (owners.bit_length() - 1)) == column) & ((lane & (owners - 1)) == spot_ref[3]) & (lane < fields - owners), 1.0, 0.0)
    entry = []
    for ref in known_refs:
        for j in range((ref.shape[1] - features - LANES) // width):
            at = features + LANES + j * width
            entry.append(jnp.dot(ref[:, at:at + width].astype(f32), mine, preferred_element_type=f32))
    entry = jnp.concatenate(entry, axis=0)
    turned = entry.T
    ids, ids_row = id_col_ref[...], id_row_ref[...]
    label = [entry[:, k:k + 1] for k in range(slots)]
    size = [entry[:, slots + k:slots + k + 1] for k in range(slots)]
    level = [entry[:, 2 * slots + k:2 * slots + k + 1] for k in range(slots)]
    if holds:
        info = jnp.concatenate([ref[:, features:features + LANES].astype(f32) for ref in holds], axis=0)
        there = info.T
        key = jnp.where((there[0:1] > 0) & (there[1:2] == spot_ref[3].astype(f32)), there[2:3] * 256.0 + there[3:4], -1.0)
        held_at = lax.broadcasted_iota(i32, (owners, key.shape[1]), 1).astype(f32)
    q = lax.broadcasted_iota(i32, (owners, total), 1).astype(f32)
    rows = [jnp.zeros((1, total), f32) for _ in range(4)]
    pos = jnp.zeros((owners, 1), f32)
    for k in range(slots):
        rank = jnp.zeros((owners, owners), f32)
        for j in range(slots):
            ahead = (ids_row < ids) if j >= k else (ids_row <= ids)
            rank = rank + jnp.where((label[k] == turned[j:j + 1, :]) & ahead, 1.0, 0.0)
        target = jnp.where(label[k] > 0, (label[k] - 1.0) * G + jnp.sum(rank, axis=1, keepdims=True), -1.0)
        places = []
        for t in range(2):
            p = pos if t == 0 else pos + jnp.where(size[k] > 1, 1.0, 0.0)
            place = ids * cap + p
            if holds:
                hit = jnp.where(key == ids * 256.0 + p, held_at, 0.0)
                place = jnp.where(p < cap, place, main + jnp.sum(hit, axis=1, keepdims=True))
            places.append(place)
        hit = target == q
        for r, v in enumerate((*places, size[k], level[k])):
            rows[r] = rows[r] + jnp.sum(jnp.where(hit, v, 0.0), axis=0, keepdims=True)
        pos = pos + size[k]
    slot_v[0:1, :] = rows[0].astype(i32)
    slot_v[1:2, :] = rows[1].astype(i32)
    n, lv = rows[2], rows[3]
    a = lax.broadcasted_iota(i32, (total, total), 0) // G
    b = lax.broadcasted_iota(i32, (total, total), 1) // G
    group = jnp.where(a == b, 1.0, 0.0)
    mean = jnp.dot(lv, group, preferred_element_type=f32) * (1.0 / G)
    square = jnp.dot(lv * lv, group, preferred_element_type=f32) * (1.0 / G)
    spread = jnp.sqrt(square - mean * mean)
    advantage = (lv - mean) / jnp.maximum(spread, 1.0)
    adv_ref[...] = advantage
    weight_v[0:1, :] = advantage / n
    weight_v[1:2, :] = jnp.where(n > 1, advantage / n, 0.0)
    copy_slot = pltpu.make_async_copy(slot_v, slot_s, table_sems.at[0])
    copy_weight = pltpu.make_async_copy(weight_v, weight_s, table_sems.at[1])
    copy_slot.start()
    copy_weight.start()
    base = 0
    for ref in holds:
        p = ref.shape[0]
        for c in range(half):
            extra[base:base + p, c, :] = ref[:, c * LANES:(c + 1) * LANES].astype(f32)
        base += p
    for h in range(base):
        tokens[main + h] = extra[h].astype(jnp.bfloat16)
    copy_slot.wait()
    copy_weight.wait()
    fetch.wait()

    batch = wide.shape[0]
    piece = total // pieces

    def work(j, _):
        for e in range(batch):
            i = j * batch + e
            for t in range(2):
                x = tokens[slot_s[t, i]].astype(f32)
                wide[e, pl.ds(t, half, stride=2), :] = x * weight_s[t, i]
        for e in range(batch):
            out[j * batch + e] = wide[e].astype(jnp.bfloat16)
        return 0

    def chunk(k, _):
        lax.fori_loop(k * (piece // batch), (k + 1) * (piece // batch), work, 0)
        part = pl.ds(k * piece, piece)
        pltpu.make_async_copy(out.at[part], out_ref.at[part], out_sems.at[k]).start()
        return 0
    lax.fori_loop(0, pieces, chunk, 0)
    for k in range(pieces):
        part = pl.ds(k * piece, piece)
        pltpu.make_async_copy(out.at[part], out_ref.at[part], out_sems.at[k]).wait()


SMEM = pl.BlockSpec(memory_space=pltpu.SMEM)
VMEM = pl.BlockSpec(memory_space=pltpu.VMEM)
HBM = pl.BlockSpec(memory_space=pl.ANY)
COST = pl.CostEstimate(flops=1 << 20, bytes_accessed=1 << 20, transcendentals=0)


def pack(rows, gain, prompt_of, lengths, levels, owners, cap, slots, groups, limit, words):
    total, width, _ = rows.shape
    half = width // 2
    return pl.pallas_call(
        functools.partial(pack_body, cap, slots, groups),
        out_shape=[
            jax.ShapeDtypeStruct((owners * cap, half, LANES), jnp.bfloat16),
            jax.ShapeDtypeStruct((max(limit, 1), half, LANES), jnp.bfloat16),
            jax.ShapeDtypeStruct((words,), jnp.int32),
            jax.ShapeDtypeStruct((limit + 1,), jnp.int32),
        ],
        in_specs=[SMEM, SMEM, SMEM, VMEM, HBM],
        out_specs=[HBM, VMEM, SMEM, SMEM],
        scratch_shapes=[
            pltpu.VMEM(rows.shape, jnp.bfloat16),
            pltpu.VMEM((BATCH, width, LANES), jnp.float32),
            pltpu.VMEM((2 * total, half, LANES), jnp.bfloat16),
            pltpu.SMEM((2 * total,), jnp.int32),
            pltpu.SMEM((2 * total,), jnp.int32),
            pltpu.SMEM((owners,), jnp.int32),
            pltpu.SMEM((owners,), jnp.int32),
            pltpu.SemaphoreType.DMA((8,)),
            pltpu.SemaphoreType.DMA,
        ],
        cost_estimate=COST,
        name="pack",
    )(prompt_of, lengths, levels, gain, rows)


def partner(size, index, step):
    return index ^ step


def log2(n):
    assert n & (n - 1) == 0
    return n.bit_length() - 1


def on_device(hidden, norm_gain, prompt_of, lengths, reward_level):
    f32, i32, bf16 = jnp.float32, jnp.int32, jnp.bfloat16
    count_here, window, features = hidden.shape
    sizes = {a: lax.axis_size(a) for a in AXES}
    owners = sizes["gx"] * sizes["gy"] * sizes["gz"]
    slots = max(2, count_here // owners + 1)
    mean = window * count_here // owners
    full = window * slots
    cap = min(full, max(window, mean - mean // 8))
    limit = 16
    room = {STAGES[0]: limit if (sizes[STAGES[0]] - 1) * limit <= LANES else 8, STAGES[1]: 8, STAGES[2]: 8}
    groups = count_here // G
    half = features // LANES
    stride = {"gx": sizes["gy"] * sizes["gz"], "gy": sizes["gz"], "gz": 1}
    spot_at = {"gx": 0, "gy": 1, "gz": 2}
    coord = {a: lax.axis_index(a) for a in AXES}
    me = sum(coord[a] * stride[a] for a in AXES)
    spot = jnp.stack([coord["gx"], coord["gy"], coord["gz"], me]).astype(i32)
    fields = 3 * slots * owners + owners
    width = -(-fields // LANES) * LANES

    rows = hidden.reshape(count_here, window, half, LANES).transpose(0, 2, 1, 3)
    rows = rows.reshape(count_here, window * half, LANES)
    gain = norm_gain.reshape(half, LANES)
    sent, spill, table, codes = pack(rows, gain, prompt_of, lengths, reward_level, owners, cap, slots, groups, limit, width)
    with jax.named_scope("exchange"):
        came = lax.all_to_all(sent, AXES, split_axis=0, concat_axis=0, tiled=True)

    def axis(a):
        return sizes[a], log2(stride[a]), spot_at[a]

    lanes = features + LANES
    holds, got, own, near, count = [], [], None, [], 1
    steps = {x: np.zeros((1,), np.int32) for x in AXES}
    for n, a in enumerate(STAGES):
        size = sizes[a]
        shape = functools.partial(jax.ShapeDtypeStruct, dtype=bf16)
        with jax.named_scope("stage" + str(n)):
            if n == 0:
                hold, send = pl.pallas_call(
                    functools.partial(first_body, tuple(near), axis(a), room[a], owners, fields),
                    out_shape=[shape((limit, lanes + width)), shape((size - 1, room[a], lanes + width))],
                    in_specs=[SMEM, SMEM, SMEM, VMEM], out_specs=[VMEM, VMEM],
                    scratch_shapes=[pltpu.VMEM((width // LANES, LANES), i32), pltpu.VMEM((limit, half, LANES), f32), pltpu.SemaphoreType.DMA],
                    cost_estimate=COST, name="stage",
                )(spot, codes, table.reshape(width // LANES, LANES), spill)
                holds = [hold]
            else:
                blocks = -(-count // room[a])
                send = pl.pallas_call(
                    functools.partial(next_body, tuple(near), axis(a), room[a], owners, fields, width, before, features, len(holds), len(got)),
                    out_shape=shape((size - 1, room[a], lanes + blocks * width)),
                    in_specs=[SMEM] + [VMEM] * (len(holds) + 1), out_specs=VMEM,
                    cost_estimate=COST, name="stage",
                )(spot, *holds, own)
            got = []
            for k in range(1, size):
                pairs = [(i, partner(size, i, k)) for i in range(size)]
                got.append(lax.ppermute(send[k - 1], a, pairs))
            own = send[0]
            holds = holds + got
        near.append(axis(a))
        before = count
        count *= size
        order = np.arange(size, dtype=np.int32)
        steps = {x: np.concatenate([v + (k if x == a else 0) for k in order]) for x, v in steps.items()}

    ids = sum((coord[a] ^ steps[a]) * stride[a] for a in AXES).astype(f32)
    known = [own, *got]
    bad = jnp.max(jnp.stack([v[0, features + 4] for v in known])) > 0

    def finish_with(tokens, cap_used, extras):
        spare = sum(h.shape[0] for h in extras)
        out, advantages = pl.pallas_call(
            functools.partial(final_body, cap_used, slots, owners, fields, width, features, groups, (len(known), len(extras))),
            out_shape=[jax.ShapeDtypeStruct((count_here, window * half, LANES), bf16), jax.ShapeDtypeStruct((1, count_here), f32)],
            in_specs=[SMEM, VMEM, VMEM, HBM] + [VMEM] * (len(known) + len(extras)), out_specs=[HBM, VMEM],
            scratch_shapes=[
                pltpu.VMEM((tokens.shape[0] + spare, half, LANES), bf16),
                pltpu.VMEM((4, window * half, LANES), f32),
                pltpu.VMEM((count_here, window * half, LANES), bf16),
                pltpu.VMEM((max(spare, 8), half, LANES), f32),
                pltpu.VMEM((window, count_here), i32),
                pltpu.VMEM((window, count_here), f32),
                pltpu.SMEM((window, count_here), i32),
                pltpu.SMEM((window, count_here), f32),
                pltpu.SemaphoreType.DMA,
                pltpu.SemaphoreType.DMA((2,)),
                pltpu.SemaphoreType.DMA((8,)),
            ],
            cost_estimate=COST, name="place",
        )(spot, ids[:, None], ids[None], tokens, *known, *extras)
        out = out.reshape(count_here, half, window, LANES).transpose(0, 2, 1, 3)
        return out.reshape(count_here, window, features), advantages.reshape(count_here)

    def usual():
        return finish_with(came, cap, holds)

    def crowded():
        again = pack(rows, gain, prompt_of, lengths, reward_level, owners, full, slots, groups, 0, width)
        all_came = lax.all_to_all(again[0], AXES, split_axis=0, concat_axis=0, tiled=True)
        return finish_with(all_came, full, [])
    return lax.cond(bad, crowded, usual)


def solution(mesh):
    many = P(AXES)
    return jax.shard_map(
        on_device, mesh=mesh,
        in_specs=(P(AXES, None, None), P(), many, many, many),
        out_specs=(P(AXES, None, None), many), check_vma=False,
    )
```

time: 117 us -> 75 us (0.64)
  local copies, waits for them, and re-layouts: 36.1 us -> 5.03 us
  waiting for transfers between devices: 55.1 us -> 27.8 us
  Pallas kernels: 0 us -> 21.3 us
  other arithmetic: 10.5 us -> 0.08 us
  starting transfers between devices: 13.2 us -> 16.8 us
  between operations: 0.81 us -> 3.43 us
    all_to_all x2 -> x1, waiting for transfers between devices: 55.1 us -> 0.01 us  [on_device(): came = lax.all_to_all(sent, AXES, split_axis=0, concat_axis=0, tiled=True)]
    ppermute x0 -> x7, waiting for transfers between devices: none -> 27.8 us  [on_device(): got.append(lax.ppermute(send[k - 1], a, pairs))]
    pallas_call x0 -> x5, Pallas kernels: none -> 21.3 us  [the longest x1 7.59 us: pack(): pl.pallas_call(functools.partial(pack_body, cap, slots, groups), out_shap...]
    scatter x4 -> x0, local copies, waits for them, and re-layouts: 18.1 us -> none  [the longest x1 15.9 us: on_device(): jnp.zeros((arrived, window, features), jnp.bfloat16).at[slot_index]]
    gather x3 -> x0, local copies, waits for them, and re-layouts: 12.4 us -> none  [the longest x1 9.33 us: on_device(): gathered = incoming[source]]
    ppermute x0 -> x7, starting transfers between devices: none -> 9.28 us  [on_device(): got.append(lax.ppermute(send[k - 1], a, pairs))]
    all_to_all x2 -> x1, starting transfers between devices: 13.2 us -> 7.47 us  [on_device(): came = lax.all_to_all(sent, AXES, split_axis=0, concat_axis=0, tiled=True)]
    convert_element_type x2 -> x1, other arithmetic: 5.38 us -> 0.01 us  [on_device(): ids = sum(((coord[a] ^ steps[a]) * stride[a] for a in AXES)).astype(f32)]
  transfers between devices with their start and end apart: 2 -> 8, of which waited for: 1 -> 5; matrix products, arithmetic and copies ran while one was open for 22% -> 6% of each run, Pallas kernels for 0% -> 10%
where the time goes in v2:
time: 75 us; the launch traced here: 74.5 us
  waiting for transfers between devices  27.8 us (37%)
  Pallas kernels  21.3 us (28%)
  starting transfers between devices  16.8 us (22%)
  local copies, waits for them, and re-layouts  5.03 us (7%)
  between operations  3.43 us (5%)
    ppermute x7, waiting for transfers between devices, on_device(): got.append(lax.ppermute(send[k - 1], a, pairs))  27.8 us
    ppermute x7, starting transfers between devices, on_device(): got.append(lax.ppermute(send[k - 1], a, pairs))  9.28 us
    pallas_call x1, Pallas kernels, pack(): pl.pallas_call(functools.partial(pack_body, cap, slots, groups), out_shap...  7.59 us
    all_to_all x1, starting transfers between devices, on_device(): came = lax.all_to_all(sent, AXES, split_axis=0, concat_axis=0, tiled=True)  7.47 us
    pallas_call x1, Pallas kernels, finish_with(): pl.pallas_call(functools.partial(final_body, cap_used, slots, owners, fie...  6.02 us
    pallas_call x2, Pallas kernels, on_device(): pl.pallas_call(functools.partial(next_body, tuple(near), axis(a), room[a]...  4.99 us
    pallas_call x1, Pallas kernels, on_device(): pl.pallas_call(functools.partial(first_body, tuple(near), axis(a), room[a...  2.74 us
    slice x4, local copies, waits for them, and re-layouts, on_device(): bad = jnp.max(jnp.stack([v[0, features + 4] for v in known])) > 0  2.35 us
  transfers between devices with their start and end apart: 8, of which 5 were waited for; matrix products, arithmetic and copies ran while one was open for 6% of the time, Pallas kernels for 10%

profile of v2, /device:TPU:0, one launch (start us, length us, event | category | flops | bytes accessed | tf_op | source)
XLA Modules:
  0.0 74.5 jit_solution(14984866076341178629)
XLA Ops:
  0.6 7.6 %pack.3 = (bf16[224,32,128]{2,1,0:T(8,128)(2,1)}, bf16[16,32,128]{2,1,0:T(8,128)(2,1)}, s32[512]{0:T(512)}, s32[17]{0:T(128)}) custom-call(s32[128]{0:T(128)} %prompt_ref.1, s32[128]{0:T(128)} %length_ref.1, s32[128]{0:T(128)} %level_ref.1, f32[32,128]{1,0:T(8,128)} %bitcast.45, bf16[128,64,128]{2,1,0:T(8,128)(2,1)} %bitcast.41), custom_call_target="tpu_custom_call" | custom-call | flops 1048576 | bytes 1048576 | tf_op jit(solution)/shard_map/pack/pallas_call | solution.py:360
  8.2 7.5 %all-to-all-start.1 = ((bf16[224,32,128]{2,1,0:T(8,128)(2,1)}), bf16[224,32,128]{2,1,0:T(8,128)(2,1)}, u32[]{:S(2)}, u32[]{:S(2)}) async-start(bf16[224,32,128]{2,1,0:T(8,128)(2,1)} %get-tuple-element.87), calls=%async_computation.1 | async-start | bytes 3670016 | tf_op jit(solution)/shard_map/exchange/all_to_all | solution.py:421
  15.7 0.0 copy-start.7
  15.7 0.0 copy-start.8
  15.7 0.0 copy-start.9
  15.7 0.0 copy-start.1
  15.8 0.0 copy-start.4
  15.8 0.0 copy-start.5
  15.8 0.1 pad_add_fusion.spot_ref
  15.9 2.7 %stage.3 = (bf16[16,4736]{1,0:T(8,128)(2,1)S(1)}, bf16[1,16,4736]{2,1,0:T(8,128)(2,1)}) custom-call(s32[4]{0:T(128)S(1)} %pad_add_fusion.spot_ref, s32[17]{0:T(128)} %get-tuple-element.82.code_ref, s32[4,128]{1,0:T(4,128)} %bitcast.51, bf16[16,32,128]{2,1,0:T(8,128)(2,1)} %get-tuple-element.84.spill_ref), custom_call_target="tpu_custom_call" | custom-call | flops 1048576 | bytes 1048576 | tf_op jit(solution)/shard_map/stage0/stage/pallas_call | solution.py:434
  18.6 0.3 collective-permute-start
  18.9 1.4 %collective-permute-done.refs_1_ = bf16[16,4736]{1,0:T(8,128)(2,1)S(1)} collective-permute-done((bf16[16,4736]{1,0:T(8,128)(2,1)}, bf16[16,4736]{1,0:T(8,128)(2,1)S(1)}, u32[]{:S(2)}, u32[]{:S(2)}) %collective-permute-start) | collective-permute-done | bytes 151584 | tf_op jit(solution)/shard_map/stage0/ppermute | solution.py:453
  20.3 2.1 %stage.4 = bf16[3,8,4736]{2,1,0:T(8,128)(2,1)} custom-call(s32[4]{0:T(128)S(1)} %pad_add_fusion.spot_ref, bf16[16,4736]{1,0:T(8,128)(2,1)S(1)} %get-tuple-element.85.refs_0_, bf16[16,4736]{1,0:T(8,128)(2,1)S(1)} %collective-permute-done.refs_1_, bf16[16,4736]{1,0:T(8,128)(2,1)} %bitcast.44), custom_call_target="tpu_custom_call" | custom-call | flops 1048576 | bytes 1048576 | tf_op jit(solution)/shard_map/stage1/stage/pallas_call | solution.py:444
  22.4 1.0 %slice_bitcast_fusion.3 = (bf16[8,4736]{1,0:T(8,128)(2,1)S(1)}, bf16[8,4736]{1,0:T(8,128)(2,1)S(1)}, bf16[8,4736]{1,0:T(8,128)(2,1)S(1)}) fusion(bf16[3,8,4736]{2,1,0:T(8,128)(2,1)} %stage.4), kind=kLoop, calls=%fused_computation.3 | loop fusion | bytes 454656 | tf_op jit(solution)/shard_map/stage1/squeeze | solution.py:453
  23.4 2.7 %collective-permute-start.3 = (bf16[8,4736]{1,0:T(8,128)(2,1)S(1)}, bf16[8,4736]{1,0:T(8,128)(2,1)S(1)}, u32[]{:S(2)}, u32[]{:S(2)}) collective-permute-start(bf16[8,4736]{1,0:T(8,128)(2,1)S(1)} %get-tuple-element.93), channel_id=1, source_target_pairs={{0,24},{8,16},{16,8},{24,0},{1,25},{9,17},{17,9},{25,1},{2,26},{10... | collective-permute-start | bytes 227336 | tf_op jit(solution)/shard_map/stage1/ppermute | solution.py:453
  26.1 0.6 collective-permute-start.2
  26.6 0.3 collective-permute-start.1
  27.0 4.1 %collective-permute-done.3.refs_4_ = bf16[8,4736]{1,0:T(8,128)(2,1)S(1)} collective-permute-done((bf16[8,4736]{1,0:T(8,128)(2,1)S(1)}, bf16[8,4736]{1,0:T(8,128)(2,1)S(1)}, u32[]{:S(2)}, u32[]{:S(2)}) %collective-permute-start.3) | collective-permute-done | bytes 75808 | tf_op jit(solution)/shard_map/stage1/ppermute | solution.py:453
  31.0 4.0 %collective-permute-done.2.refs_3_ = bf16[8,4736]{1,0:T(8,128)(2,1)S(1)} collective-permute-done((bf16[8,4736]{1,0:T(8,128)(2,1)S(1)}, bf16[8,4736]{1,0:T(8,128)(2,1)S(1)}, u32[]{:S(2)}, u32[]{:S(2)}) %collective-permute-start.2) | collective-permute-done | bytes 75808 | tf_op jit(solution)/shard_map/stage1/ppermute | solution.py:453
  35.0 2.9 %stage.5 = bf16[3,8,4736]{2,1,0:T(8,128)(2,1)} custom-call(s32[4]{0:T(128)S(1)} %pad_add_fusion.spot_ref, bf16[16,4736]{1,0:T(8,128)(2,1)S(1)} %get-tuple-element.85.refs_0_, bf16[16,4736]{1,0:T(8,128)(2,1)S(1)} %collective-permute-done.refs_1_, bf16[8,4736]{1,0:T(8,128)(2,1)S(1)} %collective-permute-done.1.refs_2_, ...), custom_call_target="tpu_custom_call" | custom-call | flops 1048576 | bytes 1048576 | tf_op jit(solution)/shard_map/stage2/stage/pallas_call | solution.py:444
  37.9 1.0 %slice_bitcast_fusion = (bf16[8,4736]{1,0:T(8,128)(2,1)S(1)}, bf16[8,4736]{1,0:T(8,128)(2,1)S(1)}, bf16[8,4736]{1,0:T(8,128)(2,1)S(1)}) fusion(bf16[3,8,4736]{2,1,0:T(8,128)(2,1)} %stage.5), kind=kLoop, calls=%fused_computation | loop fusion | bytes 454656 | tf_op jit(solution)/shard_map/stage2/squeeze | solution.py:453
  38.9 4.8 %collective-permute-start.6 = (bf16[8,4736]{1,0:T(8,128)(2,1)S(1)}, bf16[8,4736]{1,0:T(8,128)(2,1)S(1)}, u32[]{:S(2)}, u32[]{:S(2)}) collective-permute-start(bf16[8,4736]{1,0:T(8,128)(2,1)S(1)} %get-tuple-element.90), channel_id=1, source_target_pairs={{0,6},{2,4},{4,2},{6,0},{1,7},{3,5},{5,3},{7,1},{8,14},{10,12},{12... | collective-permute-start | bytes 227336 | tf_op jit(solution)/shard_map/stage2/ppermute | solution.py:453
  43.7 0.6 collective-permute-start.4
  44.4 0.6 slice.46
  44.9 5.9 %collective-permute-done.4 = bf16[8,4736]{1,0:T(8,128)(2,1)S(1)} collective-permute-done((bf16[8,4736]{1,0:T(8,128)(2,1)S(1)}, bf16[8,4736]{1,0:T(8,128)(2,1)S(1)}, u32[]{:S(2)}, u32[]{:S(2)}) %collective-permute-start.4) | collective-permute-done | bytes 75808 | tf_op jit(solution)/shard_map/stage2/ppermute | solution.py:453
  50.8 0.6 slice.47
  52.7 12.5 %collective-permute-done.5 = bf16[8,4736]{1,0:T(8,128)(2,1)S(1)} collective-permute-done((bf16[8,4736]{1,0:T(8,128)(2,1)S(1)}, bf16[8,4736]{1,0:T(8,128)(2,1)S(1)}, u32[]{:S(2)}, u32[]{:S(2)}) %collective-permute-start.5) | collective-permute-done | bytes 75808 | tf_op jit(solution)/shard_map/stage2/ppermute | solution.py:453
  65.2 0.6 slice.49
  66.4 0.6 slice.51
  67.8 6.7 %conditional.1 = (bf16[128,2,4096]{2,1,0:T(2,128)(2,1)}, f32[128]{0:T(128)}) conditional(s32[]{:T(128)} %bitcast.32, (f32[32]{0:T(128)S(1)}, s32[4]{0:T(128)S(1)}, bf16[224,32,128]{2,1,0:T(8,128)(2,1)}, bf16[8,4736]{1,0:T(8,128)(2,1)S(1)}, bf16[8,4736]{1,0:T(8,128)(2,1)S(1)}, /*index=5*/bf16[8,4736]{1,0:T(8,128)(2,1)S(1)}, ...), branch_computations={%region_0.0_spmd, %region_1.0_spmd} | conditional | flops 2097152 | bytes 20447564 | solution.py:497
  67.8 0.7 copy.14.id_col_ref
  68.4 6.0 %place.2 = (bf16[128,64,128]{2,1,0:T(8,128)(2,1)}, f32[1,128]{1,0:T(1,128)}) custom-call(s32[4]{0:T(128)S(1)} %get-tuple-element.46.spot_ref, f32[32,1]{1,0:T(8,128)} %copy.14.id_col_ref, f32[1,32]{1,0:T(1,128)S(1)} %bitcast.48, bf16[224,32,128]{2,1,0:T(8,128)(2,1)} %get-tuple-element.48.tokens_ref, bf16[8,4736]{1,0:T(8,128)(2,1)S(1)} %get-tuple-element.49.refs_0_, ...), custom_call_target="tpu_custom_call" | custom-call | flops 1048576 | bytes 1048576 | tf_op jit(solution)/shard_map/cond/branch_0_fun/place/pallas_call | solution.py:468
  (17 shorter events, 0.0 us)
Async XLA Ops:
  8.2 59.5 %all-to-all-start.1 = ((bf16[224,32,128]{2,1,0:T(8,128)(2,1)}), bf16[224,32,128]{2,1,0:T(8,128)(2,1)}, u32[]{:S(2)}, u32[]{:S(2)}) async-start(bf16[224,32,128]{2,1,0:T(8,128)(2,1)} %get-tuple-element.87), calls=%async_computation.1 | async-start | bytes 3670016 | tf_op jit(solution)/shard_map/exchange/all_to_all | solution.py:421
  15.7 28.6 %copy-start.7 = (s32[32]{0:T(128)S(1)}, s32[32]{0:T(128)}, u32[]{:S(2)}) copy-start(s32[32]{0:T(128)} %constant.29.clone) | copy-start | bytes 388
  15.7 28.6 %copy-start.8 = (s32[32]{0:T(128)S(1)}, s32[32]{0:T(128)}, u32[]{:S(2)}) copy-start(s32[32]{0:T(128)} %constant.28.clone) | copy-start | bytes 388
  15.7 28.6 %copy-start.9 = (s32[32]{0:T(128)S(1)}, s32[32]{0:T(128)}, u32[]{:S(2)}) copy-start(s32[32]{0:T(128)} %constant.27.clone) | copy-start | bytes 388
  15.7 52.0 %copy-start.1 = (bf16[128,2,4096]{2,1,0:T(2,128)(2,1)S(1)}, bf16[128,2,4096]{2,1,0:T(2,128)(2,1)}, u32[]{:S(2)}) copy-start(bf16[128,2,4096]{2,1,0:T(2,128)(2,1)} %param.10) | copy-start | bytes 6291460
  15.8 52.0 %copy-start.3 = (f32[4096]{0:T(1024)S(1)}, f32[4096]{0:T(1024)}, u32[]{:S(2)}) copy-start(f32[4096]{0:T(1024)} %param.11) | copy-start | bytes 49156
  15.8 52.0 %copy-start.4 = (s32[128]{0:T(128)S(1)}, s32[128]{0:T(128)}, u32[]{:S(2)}) copy-start(s32[128]{0:T(128)} %prompt_ref.1) | copy-start | bytes 1540
  15.8 52.0 %copy-start.5 = (s32[128]{0:T(128)S(1)}, s32[128]{0:T(128)}, u32[]{:S(2)}) copy-start(s32[128]{0:T(128)} %length_ref.1) | copy-start | bytes 1540
  15.8 52.0 %copy-start.6 = (s32[128]{0:T(128)S(1)}, s32[128]{0:T(128)}, u32[]{:S(2)}) copy-start(s32[128]{0:T(128)} %level_ref.1) | copy-start | bytes 1540
  18.6 1.7 %collective-permute-start = (bf16[16,4736]{1,0:T(8,128)(2,1)}, bf16[16,4736]{1,0:T(8,128)(2,1)S(1)}, u32[]{:S(2)}, u32[]{:S(2)}) collective-permute-start(bf16[16,4736]{1,0:T(8,128)(2,1)} %bitcast.43), channel_id=1, source_target_pairs={{0,1},{1,0},{2,3},{3,2},{4,5},{5,4},{6,7},{7,6},{8,9},{9,8},{10,11... | collective-permute-start | bytes 454664 | tf_op jit(solution)/shard_map/stage0/ppermute | solution.py:453
  23.4 11.6 %copy-start.2 = (bf16[8,4736]{1,0:T(8,128)(2,1)}, bf16[8,4736]{1,0:T(8,128)(2,1)S(1)}, u32[]{:S(2)}) copy-start(bf16[8,4736]{1,0:T(8,128)(2,1)S(1)} %get-tuple-element.95.refs_5_) | copy-start | bytes 227332
  23.4 7.6 %collective-permute-start.3 = (bf16[8,4736]{1,0:T(8,128)(2,1)S(1)}, bf16[8,4736]{1,0:T(8,128)(2,1)S(1)}, u32[]{:S(2)}, u32[]{:S(2)}) collective-permute-start(bf16[8,4736]{1,0:T(8,128)(2,1)S(1)} %get-tuple-element.93), channel_id=1, source_target_pairs={{0,24},{8,16},{16,8},{24,0},{1,25},{9,17},{17,9},{25,1},{2,26},{10... | collective-permute-start | bytes 227336 | tf_op jit(solution)/shard_map/stage1/ppermute | solution.py:453
  26.1 8.9 %collective-permute-start.2 = (bf16[8,4736]{1,0:T(8,128)(2,1)S(1)}, bf16[8,4736]{1,0:T(8,128)(2,1)S(1)}, u32[]{:S(2)}, u32[]{:S(2)}) collective-permute-start(bf16[8,4736]{1,0:T(8,128)(2,1)S(1)} %get-tuple-element.94), channel_id=1, source_target_pairs={{0,16},{8,24},{16,0},{24,8},{1,17},{9,25},{17,1},{25,9},{2,18},{10... | collective-permute-start | bytes 227336 | tf_op jit(solution)/shard_map/stage1/ppermute | solution.py:453
  26.6 8.4 %collective-permute-start.1 = (bf16[8,4736]{1,0:T(8,128)(2,1)S(1)}, bf16[8,4736]{1,0:T(8,128)(2,1)S(1)}, u32[]{:S(2)}, u32[]{:S(2)}) collective-permute-start(bf16[8,4736]{1,0:T(8,128)(2,1)S(1)} %get-tuple-element.95.refs_5_), channel_id=1, source_target_pairs={{0,8},{8,0},{16,24},{24,16},{1,9},{9,1},{17,25},{25,17},{2,10},{10... | collective-permute-start | bytes 227336 | tf_op jit(solution)/shard_map/stage1/ppermute | solution.py:453
  38.9 27.6 %collective-permute-start.6 = (bf16[8,4736]{1,0:T(8,128)(2,1)S(1)}, bf16[8,4736]{1,0:T(8,128)(2,1)S(1)}, u32[]{:S(2)}, u32[]{:S(2)}) collective-permute-start(bf16[8,4736]{1,0:T(8,128)(2,1)S(1)} %get-tuple-element.90), channel_id=1, source_target_pairs={{0,6},{2,4},{4,2},{6,0},{1,7},{3,5},{5,3},{7,1},{8,14},{10,12},{12... | collective-permute-start | bytes 227336 | tf_op jit(solution)/shard_map/stage2/ppermute | solution.py:453
  43.7 21.5 %collective-permute-start.5 = (bf16[8,4736]{1,0:T(8,128)(2,1)S(1)}, bf16[8,4736]{1,0:T(8,128)(2,1)S(1)}, u32[]{:S(2)}, u32[]{:S(2)}) collective-permute-start(bf16[8,4736]{1,0:T(8,128)(2,1)S(1)} %get-tuple-element.91), channel_id=1, source_target_pairs={{0,4},{2,6},{4,0},{6,2},{1,5},{3,7},{5,1},{7,3},{8,12},{10,14},{12... | collective-permute-start | bytes 227336 | tf_op jit(solution)/shard_map/stage2/ppermute | solution.py:453
  43.7 7.1 %collective-permute-start.4 = (bf16[8,4736]{1,0:T(8,128)(2,1)S(1)}, bf16[8,4736]{1,0:T(8,128)(2,1)S(1)}, u32[]{:S(2)}, u32[]{:S(2)}) collective-permute-start(bf16[8,4736]{1,0:T(8,128)(2,1)S(1)} %get-tuple-element.92), channel_id=1, source_target_pairs={{0,2},{2,0},{4,6},{6,4},{1,3},{3,1},{5,7},{7,5},{8,10},{10,8},{12,... | collective-permute-start | bytes 227336 | tf_op jit(solution)/shard_map/stage2/ppermute | solution.py:453

commit v3 on v2

v3 whole, which is shorter than its diff:
```python
import functools
import jax
import numpy as np
import jax.numpy as jnp
from jax import lax
from jax.experimental import pallas as pl
from jax.experimental.pallas import tpu as pltpu
from jax.sharding import PartitionSpec as P

G = 16
AXES = ("gx", "gy", "gz")
LANES = 128
BATCH = 16
norm_eps = 1e-05


def pack_body(cap, groups, limit, spot_ref, prompt_ref, length_ref, gain_ref, rows_ref,
              out_ref, spill_ref, mark_ref, nth_ref,
              rows, wide, tokens, way_v, list_v, way, spilled, in_sems, way_sems):
    f32, i32 = jnp.float32, jnp.int32
    total, pieces = rows.shape[0], in_sems.shape[0]
    piece = total // pieces
    batch = wide.shape[0]
    half = wide.shape[1] // 2
    features = half * LANES
    for k in range(pieces):
        part = pl.ds(k * piece, piece)
        pltpu.make_async_copy(rows_ref.at[part], rows.at[part], in_sems.at[k]).start()

    p, n = prompt_ref[...], length_ref[...]
    column = jnp.broadcast_to((p * 4 + n).astype(f32), (total, total)).T.astype(i32)
    before = lax.broadcasted_iota(i32, (total, total), 0) < lax.broadcasted_iota(i32, (total, total), 1)
    owner = p >> log2(groups)
    same = ((column >> (2 + log2(groups))) == owner) & before
    at = jnp.sum(jnp.where(same, column & 3, 0), axis=0, keepdims=True)
    nth_ref[...] = jnp.sum(jnp.where(same, 1, 0), axis=0, keepdims=True)
    lane = lax.broadcasted_iota(i32, (1, total), 1)
    home = jnp.sum(jnp.where(lane == 0, owner, 0), axis=1, keepdims=True) * cap
    d0 = jnp.where(at < cap, owner * cap + at, home)
    way_v[0:1, :] = d0
    way_v[1:2, :] = jnp.where((n > 1) & (at + 1 < cap), d0 + 1, d0)
    pltpu.make_async_copy(way_v, way, way_sems.at[0]).start()
    if limit:
        over = jnp.where(at >= cap, 1, 0)
        more = jnp.where((n > 1) & (at + 1 >= cap), 1, 0)
        start = jnp.dot((over + more).astype(f32), jnp.where(before, 1.0, 0.0), preferred_element_type=f32).astype(i32)
        e = lax.broadcasted_iota(i32, (limit, total), 0)
        hit0 = (over > 0) & (start == e)
        hit1 = (more > 0) & (start + over == e)
        token = jnp.sum(jnp.where(hit0, 2 * lane + 1, jnp.where(hit1, 2 * lane + 2, 0)), axis=1, keepdims=True)
        dest = jnp.sum(jnp.where(hit0 | hit1, owner, 0), axis=1, keepdims=True)
        spot = jnp.sum(jnp.where(hit0, at, jnp.where(hit1, at + 1, 0)), axis=1, keepdims=True)
        lanes = lax.broadcasted_iota(i32, (limit, LANES), 1)
        mark = jnp.where(lanes == 0, 1, jnp.where(lanes == 1, dest, jnp.where(lanes == 2, spot_ref[0], jnp.where(lanes == 3, spot, 0))))
        mark_ref[...] = jnp.where(token > 0, mark, 0).astype(f32).astype(jnp.bfloat16)
        list_v[...] = jnp.broadcast_to(jnp.maximum(token - 1, 0), list_v.shape)
        pltpu.make_async_copy(list_v, spilled, way_sems.at[1]).start()
    else:
        mark_ref[...] = jnp.zeros(mark_ref.shape, mark_ref.dtype)
    gain = gain_ref[...]
    pltpu.make_async_copy(way_v, way, way_sems.at[0]).wait()

    def work(j, _):
        for b in range(batch):
            wide[b] = rows[j * batch + b].astype(f32)
        for b in range(batch):
            i = j * batch + b
            for t in (1, 0):
                x = wide[b, pl.ds(t, half, stride=2), :]
                s = jnp.sum((x * x).reshape(half // 8, 8, LANES), axis=0)
                s = jnp.sum(jnp.sum(s, axis=1, keepdims=True), axis=0, keepdims=True)
                r = lax.rsqrt(s * (1.0 / features) + norm_eps)
                x = (x * r * gain).astype(jnp.bfloat16)
                out_ref[way[t, i]] = x
                tokens[2 * i + t] = x
        return 0

    per = piece // batch

    def chunk(k, _):
        part = pl.ds(k * piece, piece)
        pltpu.make_async_copy(rows_ref.at[part], rows.at[part], in_sems.at[k]).wait()
        return lax.fori_loop(k * per, (k + 1) * per, work, 0)
    lax.fori_loop(0, pieces, chunk, 0)
    out_ref[way[0, 0]] = tokens[0]
    if limit:
        pltpu.make_async_copy(list_v, spilled, way_sems.at[1]).wait()
        for e in range(limit):
            spill_ref[e] = tokens[spilled[e, 0]]
    else:
        spill_ref[...] = jnp.zeros(spill_ref.shape, spill_ref.dtype)


def select(parts, near_axes, axis, room, spot_ref, shape):
    f32 = jnp.float32
    size, stride, mine = axis
    moved, offset = None, jnp.zeros((1, LANES), f32)
    for ref in parts:
        p = ref.shape[0]
        info = ref[:, shape[0]:shape[0] + LANES].astype(f32)
        dest = info[:, 1:2].astype(jnp.int32)
        lane = lax.broadcasted_iota(jnp.int32, (p, LANES), 1)
        go = (lane < (size - 1) * room) & (info[:, 0:1] > 0)
        for n, st, at in near_axes:
            go = go & (((dest >> st) & (n - 1)) == spot_ref[at])
        turn = lane & (room - 1)
        to = spot_ref[mine] ^ ((lane >> (room.bit_length() - 1)) + 1)
        go = jnp.where(go & (((dest >> stride) & (size - 1)) == to), 1.0, 0.0)
        row = lax.broadcasted_iota(jnp.int32, (p, p), 0)
        col = lax.broadcasted_iota(jnp.int32, (p, p), 1)
        nth = jnp.dot(jnp.where(col < row, 1.0, 0.0), go, preferred_element_type=f32) + offset
        offset = offset + jnp.sum(go, axis=0, keepdims=True)
        pick = jnp.where(nth == turn.astype(f32), go, 0.0)[:, :(size - 1) * room]
        data = ref[:, :shape[0] + LANES].astype(f32)
        part = lax.dot_general(pick, data, (((0,), (0,)), ((), ())), preferred_element_type=f32)
        moved = part if moved is None else moved + part
    return moved


def crowding(known, owners, fields, near_axes, axis, room, spot_ref):
    f32 = jnp.float32
    size, stride, mine = axis
    o = lax.broadcasted_iota(jnp.int32, (owners, LANES), 0)
    b = lax.broadcasted_iota(jnp.int32, (owners, LANES), 1)
    at = (o >> stride) & (size - 1)
    place = at
    span = size
    for n, st, _ in near_axes:
        place = place + span * ((o >> st) & (n - 1))
        span *= n
    member = jnp.where((place == b) & (at != spot_ref[mine]), 1.0, 0.0)
    total = jnp.zeros((1, LANES), f32)
    for k in known:
        left = jnp.sum(k[:, fields - owners:fields], axis=0, keepdims=True)
        total = total + jnp.dot(left, member, preferred_element_type=f32)
    return jnp.max(jnp.where(total > room, 1.0, 0.0), axis=1, keepdims=True)


def first_body(near_axes, axis, room, owners, fields, width, cap, groups, spot_ref, prompt_ref, length_ref, level_ref, nth_ref, mark_ref, spill_ref, hold_ref, *rest):
    f32, i32 = jnp.float32, jnp.int32
    limit, half, _ = spill_ref.shape
    features = half * LANES
    send_refs, wide = rest[:-1], rest[-1]
    wide[...] = spill_ref[...].astype(f32)
    for c in range(half):
        hold_ref[:, c * LANES:(c + 1) * LANES] = wide[:, c, :].astype(jnp.bfloat16)
    hold_ref[:, features:features + LANES] = mark_ref[...]
    p, n = prompt_ref[...], length_ref[...]
    total = p.shape[1]
    owner = p >> log2(groups)
    place = nth_ref[...] * owners + owner
    column = jnp.broadcast_to(place.astype(f32), (total, total)).T.astype(i32)[:, :1]
    lane = lax.broadcasted_iota(i32, (total, width), 1)
    block = (fields - owners) // 3
    own = jnp.zeros((1, width), f32)
    for k, v in enumerate(((p & (groups - 1)) + 1, n, level_ref[...])):
        here = jnp.where(lane == column + k * block, 1.0, 0.0)
        own = own + jnp.dot(v.astype(f32), here, preferred_element_type=f32)
    here = jnp.where(lane == (column & (owners - 1)) + 3 * block, 1.0, 0.0)
    tokens = jnp.dot(n.astype(f32), here, preferred_element_type=f32)
    own = own + jnp.maximum(tokens - cap, 0.0)
    first = lax.broadcasted_iota(i32, (limit, width), 0) == 0
    known = jnp.where(first, own, 0.0)
    hold_ref[:, features + LANES:] = known.astype(jnp.bfloat16)
    left = jnp.sum(own[:, fields - owners:fields], axis=1, keepdims=True)
    bad = jnp.where(left > limit, 1.0, 0.0)
    bad = jnp.maximum(bad, crowding([known], owners, fields, near_axes, axis, room, spot_ref))
    moved = select([hold_ref], near_axes, axis, room, spot_ref, (features,))
    finish(moved, [known[:room]], bad, room, features, send_refs)


def finish(moved, known, bad, room, features, send_refs):
    rows = moved.shape[0]
    lane = lax.broadcasted_iota(jnp.int32, (rows, LANES), 1)
    info = jnp.where(lane == 4, bad, jnp.where(lane < 4, moved[:, features:], 0.0))
    for k, send_ref in enumerate(send_refs):
        part = slice(k * room, (k + 1) * room)
        send_ref[:, :features] = moved[part, :features].astype(jnp.bfloat16)
        send_ref[:, features:features + LANES] = info[part].astype(jnp.bfloat16)
        at = features + LANES
        for v in known:
            send_ref[:, at:at + v.shape[1]] = v.astype(jnp.bfloat16)
            at += v.shape[1]


def next_body(near_axes, axis, room, owners, fields, width, count, features, parts, recent, spot_ref, *refs):
    f32 = jnp.float32
    holds, own_ref, send_refs = refs[:parts], refs[parts], refs[parts + 1:]
    came = holds[parts - recent:]
    at = features + LANES
    blocks = (own_ref.shape[1] - at) // width
    bad = None
    known = []
    for i, ref in enumerate((own_ref, *came)):
        flag = jnp.max(ref[:, features:features + LANES].astype(f32)[:, 4:5], axis=0, keepdims=True)
        bad = flag if bad is None else jnp.maximum(bad, flag)
        for j in range(blocks):
            value = ref[:, at + j * width:at + (j + 1) * width].astype(f32)
            if count >= room:
                known.append(value)
                continue
            rows = ref.shape[0]
            to = lax.broadcasted_iota(jnp.int32, (room, rows), 0)
            source = lax.broadcasted_iota(jnp.int32, (room, rows), 1)
            shift = (i * count) % room
            put = jnp.where((to == source + shift) & (source < count), 1.0, 0.0)
            value = jnp.dot(put, value, preferred_element_type=f32)
            if (i * count) // room == len(known):
                known.append(value)
            else:
                known[-1] = known[-1] + value
    bad = jnp.maximum(bad, crowding(known, owners, fields, near_axes, axis, room, spot_ref))
    moved = select(holds, near_axes, axis, room, spot_ref, (features,))
    finish(moved, known, bad, room, features, send_refs)


def final_body(cap, slots, owners, fields, width, features, groups, parts, spot_ref, id_col_ref, id_row_ref, tokens_ref, *refs):
    f32, i32 = jnp.float32, jnp.int32
    known_refs, holds = refs[:parts[0]], refs[parts[0]:parts[0] + parts[1]]
    out_ref, adv_ref, flag_ref, wide, out, extra, more, slot_v, weight_v, slot_s, weight_s, table_sems, out_sems = refs[parts[0] + parts[1]:]
    total, pieces = out.shape[0], out_sems.shape[0]
    main = tokens_ref.shape[0]
    half = features // LANES
    bad = jnp.zeros((1, LANES), f32)
    for ref in known_refs:
        bad = jnp.maximum(bad, jnp.max(ref[:, features:features + LANES].astype(f32), axis=0, keepdims=True))
    bad = jnp.where(lax.broadcasted_iota(i32, (1, LANES), 1) == 4, bad, 0.0)
    flag_ref[0] = jnp.max(bad).astype(i32)
    lane = lax.broadcasted_iota(i32, (width, LANES), 0)
    column = lax.broadcasted_iota(i32, (width, LANES), 1)
    mine = jnp.where(((lane >> (owners.bit_length() - 1)) == column) & ((lane & (owners - 1)) == spot_ref[0]) & (lane < fields - owners), 1.0, 0.0)
    entry = []
    for ref in known_refs:
        for j in range((ref.shape[1] - features - LANES) // width):
            at = features + LANES + j * width
            entry.append(jnp.dot(ref[:, at:at + width].astype(f32), mine, preferred_element_type=f32))
    entry = jnp.concatenate(entry, axis=0)
    turned = entry.T
    ids, ids_row = id_col_ref[...], id_row_ref[...]
    label = [entry[:, k:k + 1] for k in range(slots)]
    size = [entry[:, slots + k:slots + k + 1] for k in range(slots)]
    level = [entry[:, 2 * slots + k:2 * slots + k + 1] for k in range(slots)]
    if holds:
        info = jnp.concatenate([ref[:, features:features + LANES].astype(f32) for ref in holds], axis=0)
        there = info.T
        key = jnp.where((there[0:1] > 0) & (there[1:2] == spot_ref[0].astype(f32)), there[2:3] * 256.0 + there[3:4], -1.0)
        held_at = lax.broadcasted_iota(i32, (owners, key.shape[1]), 1).astype(f32)
    q = lax.broadcasted_iota(i32, (owners, total), 1).astype(f32)
    rows = [jnp.zeros((1, total), f32) for _ in range(4)]
    pos = jnp.zeros((owners, 1), f32)
    for k in range(slots):
        rank = jnp.zeros((owners, owners), f32)
        for j in range(slots):
            ahead = (ids_row < ids) if j >= k else (ids_row <= ids)
            rank = rank + jnp.where((label[k] == turned[j:j + 1, :]) & ahead, 1.0, 0.0)
        target = jnp.where(label[k] > 0, (label[k] - 1.0) * G + jnp.sum(rank, axis=1, keepdims=True), -1.0)
        places = []
        for t in range(2):
            p = pos if t == 0 else pos + jnp.where(size[k] > 1, 1.0, 0.0)
            place = ids * cap + p
            if holds:
                hit = jnp.where(key == ids * 256.0 + p, held_at, 0.0)
                place = jnp.where(p < cap, place, main + jnp.sum(hit, axis=1, keepdims=True))
            places.append(place)
        hit = target == q
        for r, v in enumerate((*places, size[k], level[k])):
            rows[r] = rows[r] + jnp.sum(jnp.where(hit, v, 0.0), axis=0, keepdims=True)
        pos = pos + size[k]
    slot_v[0:1, :] = rows[0].astype(i32)
    slot_v[1:2, :] = rows[1].astype(i32)
    n, lv = rows[2], rows[3]
    a = lax.broadcasted_iota(i32, (total, total), 0) // G
    b = lax.broadcasted_iota(i32, (total, total), 1) // G
    group = jnp.where(a == b, 1.0, 0.0)
    mean = jnp.dot(lv, group, preferred_element_type=f32) * (1.0 / G)
    square = jnp.dot(lv * lv, group, preferred_element_type=f32) * (1.0 / G)
    spread = jnp.sqrt(square - mean * mean)
    advantage = (lv - mean) / jnp.maximum(spread, 1.0)
    adv_ref[...] = advantage
    weight_v[0:1, :] = advantage / n
    weight_v[1:2, :] = jnp.where(n > 1, advantage / n, 0.0)
    copy_slot = pltpu.make_async_copy(slot_v, slot_s, table_sems.at[0])
    copy_weight = pltpu.make_async_copy(weight_v, weight_s, table_sems.at[1])
    copy_slot.start()
    copy_weight.start()
    base = 0
    for ref in holds:
        p = ref.shape[0]
        for c in range(half):
            extra[base:base + p, c, :] = ref[:, c * LANES:(c + 1) * LANES].astype(f32)
        base += p
    for h in range(base):
        more[h] = extra[h].astype(jnp.bfloat16)
    copy_slot.wait()
    copy_weight.wait()

    batch = wide.shape[0]
    piece = total // pieces

    def work(j, _):
        for e in range(batch):
            i = j * batch + e
            for t in range(2):
                at = slot_s[t, i]
                x = tokens_ref[jnp.minimum(at, main - 1)]
                if holds:
                    x = jnp.where(at < main, x, more[jnp.maximum(at - main, 0)])
                x = x.astype(f32)
                wide[e, pl.ds(t, half, stride=2), :] = x * weight_s[t, i]
        for e in range(batch):
            out[j * batch + e] = wide[e].astype(jnp.bfloat16)
        return 0

    def chunk(k, _):
        lax.fori_loop(k * (piece // batch), (k + 1) * (piece // batch), work, 0)
        part = pl.ds(k * piece, piece)
        pltpu.make_async_copy(out.at[part], out_ref.at[part], out_sems.at[k]).start()
        return 0
    lax.fori_loop(0, pieces, chunk, 0)
    for k in range(pieces):
        part = pl.ds(k * piece, piece)
        pltpu.make_async_copy(out.at[part], out_ref.at[part], out_sems.at[k]).wait()


SMEM = pl.BlockSpec(memory_space=pltpu.SMEM)
VMEM = pl.BlockSpec(memory_space=pltpu.VMEM)
HBM = pl.BlockSpec(memory_space=pltpu.HBM)
ROOM = pltpu.CompilerParams(vmem_limit_bytes=20 << 20)
COST = pl.CostEstimate(flops=1 << 20, bytes_accessed=1 << 20, transcendentals=0)


def pack(spot, rows, gain, prompt_of, lengths, owners, cap, groups, limit):
    total, width, _ = rows.shape
    half = width // 2
    few = max(limit, 16)
    return pl.pallas_call(
        functools.partial(pack_body, cap, groups, limit),
        out_shape=[
            jax.ShapeDtypeStruct((owners * cap, half, LANES), jnp.bfloat16),
            jax.ShapeDtypeStruct((few, half, LANES), jnp.bfloat16),
            jax.ShapeDtypeStruct((few, LANES), jnp.bfloat16),
            jax.ShapeDtypeStruct((1, total), jnp.int32),
        ],
        in_specs=[SMEM, VMEM, VMEM, VMEM, HBM],
        out_specs=[VMEM, VMEM, VMEM, VMEM],
        scratch_shapes=[
            pltpu.VMEM(rows.shape, jnp.bfloat16),
            pltpu.VMEM((BATCH, width, LANES), jnp.float32),
            pltpu.VMEM((2 * total, half, LANES), jnp.bfloat16),
            pltpu.VMEM((2, total), jnp.int32),
            pltpu.VMEM((few, LANES), jnp.int32),
            pltpu.SMEM((2, total), jnp.int32),
            pltpu.SMEM((few, LANES), jnp.int32),
            pltpu.SemaphoreType.DMA((8,)),
            pltpu.SemaphoreType.DMA((2,)),
        ],
        cost_estimate=COST, compiler_params=ROOM,
        name="pack",
    )(spot, prompt_of, lengths, gain, rows)


def log2(n):
    assert n & (n - 1) == 0
    return n.bit_length() - 1


def on_device(hidden, norm_gain, prompt_of, lengths, reward_level):
    f32, i32, bf16 = jnp.float32, jnp.int32, jnp.bfloat16
    count_here, window, features = hidden.shape
    sizes = {a: lax.axis_size(a) for a in AXES}
    owners = sizes["gx"] * sizes["gy"] * sizes["gz"]
    slots = max(2, count_here // owners + 1)
    mean = window * count_here // owners
    full = window * slots
    cap = min(full, max(window, mean - mean // 8))
    limit, room = 16, 8
    groups = count_here // G
    half = features // LANES
    stride = {"gx": sizes["gy"] * sizes["gz"], "gy": sizes["gz"], "gz": 1}
    coord = {a: lax.axis_index(a) for a in AXES}
    me = sum(coord[a] * stride[a] for a in AXES)
    stages = [("gz", 0, sizes["gz"]), ("gx", 0, sizes["gx"])]
    stages += [("gy", bit, 2) for bit in range(log2(sizes["gy"]))]
    spot = jnp.stack([me] + [(coord[a] >> bit) & (n - 1) for a, bit, n in stages]).astype(i32)
    fields = 3 * slots * owners + owners
    width = -(-fields // LANES) * LANES

    rows = hidden.reshape(count_here, window, half, LANES).transpose(0, 2, 1, 3)
    rows = rows.reshape(count_here, window * half, LANES)
    gain = norm_gain.reshape(half, LANES)
    prompts, sizes_of, levels = prompt_of[None], lengths[None], reward_level[None]
    sent, spill, marks, nth = pack(spot, rows, gain, prompts, sizes_of, owners, cap, groups, limit)
    came = lax.all_to_all(sent, AXES, split_axis=0, concat_axis=0, tiled=True)

    lanes = features + LANES
    shape = functools.partial(jax.ShapeDtypeStruct, dtype=bf16)
    holds, got, own, near, count, before = [], [], None, [], 1, 0
    steps = {a: np.zeros((1,), np.int32) for a in AXES}
    for n, (a, bit, size) in enumerate(stages):
        axis = (size, log2(stride[a]) + bit, n + 1)
        with jax.named_scope("stage" + str(n)):
            if n == 0:
                hold, *sends = pl.pallas_call(
                    functools.partial(first_body, tuple(near), axis, room, owners, fields, width, cap, groups),
                    out_shape=[shape((limit, lanes + width))] + [shape((room, lanes + width))] * (size - 1),
                    in_specs=[SMEM] + [VMEM] * 6, out_specs=[VMEM] * size,
                    scratch_shapes=[pltpu.VMEM((limit, half, LANES), f32)],
                    cost_estimate=COST, compiler_params=ROOM, name="stage",
                )(spot, prompts, sizes_of, levels, nth, marks, spill)
                holds = [hold]
            else:
                blocks = -(-count // room)
                sends = pl.pallas_call(
                    functools.partial(next_body, tuple(near), axis, room, owners, fields, width, before, features, len(holds), len(got)),
                    out_shape=[shape((room, lanes + blocks * width))] * (size - 1),
                    in_specs=[SMEM] + [VMEM] * (len(holds) + 1), out_specs=[VMEM] * (size - 1),
                    cost_estimate=COST, compiler_params=ROOM, name="stage",
                )(spot, *holds, own)
            got = []
            for k in range(1, size):
                pairs = [(i, i ^ (k << bit)) for i in range(sizes[a])]
                got.append(lax.ppermute(sends[k - 1], a, pairs))
            own = sends[0]
            holds = holds + got
        near.append(axis)
        before = count
        count *= size
        steps = {x: np.concatenate([v + ((k << bit) if x == a else 0) for k in range(size)]).astype(np.int32) for x, v in steps.items()}

    ids = sum((coord[a] ^ steps[a]) * stride[a] for a in AXES).astype(f32)
    known = [own, *got]

    def finish_with(tokens, cap_used, extras):
        spare = sum(h.shape[0] for h in extras)
        return pl.pallas_call(
            functools.partial(final_body, cap_used, slots, owners, fields, width, features, groups, (len(known), len(extras))),
            out_shape=[
                jax.ShapeDtypeStruct((count_here, window * half, LANES), bf16),
                jax.ShapeDtypeStruct((1, count_here), f32),
                jax.ShapeDtypeStruct((1,), i32),
            ],
            in_specs=[SMEM] + [VMEM] * (3 + len(known) + len(extras)), out_specs=[HBM, VMEM, SMEM],
            scratch_shapes=[
                pltpu.VMEM((BATCH, window * half, LANES), f32),
                pltpu.VMEM((count_here, window * half, LANES), bf16),
                pltpu.VMEM((max(spare, 8), half, LANES), f32),
                pltpu.VMEM((max(spare, 8), half, LANES), bf16),
                pltpu.VMEM((window, count_here), i32),
                pltpu.VMEM((window, count_here), f32),
                pltpu.SMEM((window, count_here), i32),
                pltpu.SMEM((window, count_here), f32),
                pltpu.SemaphoreType.DMA((2,)),
                pltpu.SemaphoreType.DMA((8,)),
            ],
            cost_estimate=COST, compiler_params=ROOM, name="place",
        )(spot, ids[:, None], ids[None], tokens, *known, *extras)

    def whole(out):
        out = out.reshape(count_here, half, window, LANES).transpose(0, 2, 1, 3)
        return out.reshape(count_here, window, features)
    out, advantages, bad = finish_with(came, cap, holds)

    def crowded(state):
        again = pack(spot, rows, gain, prompts, sizes_of, owners, full, groups, 0)
        all_came = lax.all_to_all(again[0], AXES, split_axis=0, concat_axis=0, tiled=True)
        return jnp.zeros((1,), i32), whole(finish_with(all_came, full, [])[0])
    _, out = lax.while_loop(lambda state: state[0][0] > 0, crowded, (bad, whole(out)))
    return out, advantages.reshape(count_here)


def solution(mesh):
    many = P(AXES)
    return jax.shard_map(
        on_device, mesh=mesh,
        in_specs=(P(AXES, None, None), P(), many, many, many),
        out_specs=(P(AXES, None, None), many), check_vma=False,
    )
```

time: 75 us -> 66.1 us (0.88)
  Pallas kernels: 21.3 us -> 15 us
  local copies, waits for them, and re-layouts: 5.03 us -> 1.43 us
  between operations: 3.43 us -> 0.76 us
  waiting for transfers between devices: 27.8 us -> 30.2 us
  starting transfers between devices: 16.8 us -> 17.9 us
    pallas_call x4 -> x5, Pallas kernels: 15.3 us -> 9.27 us  [the longest x3 4.44 us: on_device(): pl.pallas_call(functools.partial(next_body, tuple(near), axis, room, owne...]
    ppermute x7 -> x6, waiting for transfers between devices: 27.8 us -> 30.2 us  [on_device(): got.append(lax.ppermute(sends[k - 1], a, pairs))]
    slice x4 -> x0, local copies, waits for them, and re-layouts: 2.35 us -> none  [on_device(): bad = jnp.max(jnp.stack([v[0, features + 4] for v in known])) > 0]
    squeeze x2 -> x0, local copies, waits for them, and re-layouts: 1.95 us -> none  [on_device(): got.append(lax.ppermute(send[k - 1], a, pairs))]
    ppermute x7 -> x6, starting transfers between devices: 9.28 us -> 10.5 us  [on_device(): got.append(lax.ppermute(sends[k - 1], a, pairs))]
    unnamed x18, local copies, waits for them, and re-layouts: 0.06 us -> 1.26 us
  transfers between devices with their start and end apart: 8 -> 7, of which waited for: 5 -> 5; matrix products, arithmetic and copies ran while one was open for 6% -> 0% of each run, Pallas kernels for 10% -> 9%
where the time goes in v3:
time: 66.1 us; the launch traced here: 65.8 us
  waiting for transfers between devices  30.2 us (46%)
  starting transfers between devices  17.9 us (27%)
  Pallas kernels  15 us (23%)
  local copies, waits for them, and re-layouts  1.43 us (2%)
  between operations  0.76 us (1%)
    ppermute x6, waiting for transfers between devices, on_device(): got.append(lax.ppermute(sends[k - 1], a, pairs))  30.2 us
    ppermute x6, starting transfers between devices, on_device(): got.append(lax.ppermute(sends[k - 1], a, pairs))  10.5 us
    all_to_all x1, starting transfers between devices, on_device(): came = lax.all_to_all(sent, AXES, split_axis=0, concat_axis=0, tiled=True)  7.33 us
    pallas_call x1, Pallas kernels, finish_with(): pl.pallas_call(functools.partial(final_body, cap_used, slots, owners, fie...  5.71 us
    pallas_call x3, Pallas kernels, on_device(): pl.pallas_call(functools.partial(next_body, tuple(near), axis, room, owne...  4.44 us
    pallas_call x1, Pallas kernels, pack(): pl.pallas_call(functools.partial(pack_body, cap, groups, limit), out_shap...  3.5 us
    pallas_call x1, Pallas kernels, on_device(): pl.pallas_call(functools.partial(first_body, tuple(near), axis, room, own...  1.33 us
  transfers between devices with their start and end apart: 7, of which 5 were waited for; matrix products, arithmetic and copies ran while one was open for 0% of the time, Pallas kernels for 9%

profile of v3, /device:TPU:0, one launch (start us, length us, event | category | flops | bytes accessed | tf_op | source)
XLA Modules:
  0.0 65.8 jit_solution(2749193730725832438)
XLA Ops:
  0.6 0.1 stack.23.spot_ref
  0.7 3.5 %pack.2 = (bf16[224,32,128]{2,1,0:T(8,128)(2,1)S(1)}, bf16[16,32,128]{2,1,0:T(8,128)(2,1)S(1)}, bf16[16,128]{1,0:T(8,128)(2,1)S(1)}, s32[1,128]{1,0:T(1,128)S(1)}) custom-call(s32[5]{0:T(128)S(1)} %stack.23.spot_ref, s32[1,128]{1,0:T(1,128)} %bitcast.40, s32[1,128]{1,0:T(1,128)} %bitcast.43, f32[32,128]{1,0:T(8,128)} %bitcast.38, bf16[128,64,128]{2,1,0:T(8,128)(2,1)} %bitcast.35), custom_call_target="tpu_custom_call" | custom-call | flops 1048576 | bytes 1048576 | tf_op jit(solution)/shard_map/pack/pallas_call | solution.py:336
  4.2 0.0 copy-start.1
  4.2 1.2 %copy-done.1 = bf16[224,32,128]{2,1,0:T(8,128)(2,1)} copy-done((bf16[224,32,128]{2,1,0:T(8,128)(2,1)}, bf16[224,32,128]{2,1,0:T(8,128)(2,1)S(1)}, u32[]{:S(2)}) %copy-start.1) | copy-done | bytes 1835032
  5.5 0.0 copy-start.12
  5.5 0.0 copy-start.13
  5.5 7.3 %all-to-all-start.1 = ((bf16[224,32,128]{2,1,0:T(8,128)(2,1)}), bf16[224,32,128]{2,1,0:T(8,128)(2,1)S(1)}, u32[]{:S(2)}, u32[]{:S(2)}) async-start(bf16[224,32,128]{2,1,0:T(8,128)(2,1)} %copy-done.1), calls=%async_computation.1 | async-start | bytes 3670016 | tf_op jit(solution)/shard_map/all_to_all | solution.py:393
  12.8 0.0 copy-done.2
  12.8 0.0 copy-done.6
  12.9 0.0 copy-done.7
  12.9 1.3 %stage.4 = (bf16[16,4736]{1,0:T(8,128)(2,1)S(1)}, bf16[8,4736]{1,0:T(8,128)(2,1)S(1)}) custom-call(s32[5]{0:T(128)S(1)} %stack.23.spot_ref, s32[1,128]{1,0:T(1,128)S(1)} %bitcast.41, s32[1,128]{1,0:T(1,128)S(1)} %bitcast.44, s32[1,128]{1,0:T(1,128)S(1)} %bitcast.34, s32[1,128]{1,0:T(1,128)S(1)} %get-tuple-element.67.nth_ref, ...), custom_call_target="tpu_custom_call" | custom-call | flops 1048576 | bytes 1048576 | tf_op jit(solution)/shard_map/stage0/stage/pallas_call | solution.py:403
  14.2 0.3 collective-permute-start
  14.5 1.0 %collective-permute-done.refs_1_.refs_3_ = bf16[8,4736]{1,0:T(8,128)(2,1)S(1)} collective-permute-done((bf16[8,4736]{1,0:T(8,128)(2,1)S(1)}, bf16[8,4736]{1,0:T(8,128)(2,1)S(1)}, u32[]{:S(2)}, u32[]{:S(2)}) %collective-permute-start) | collective-permute-done | bytes 75808 | tf_op jit(solution)/shard_map/stage0/ppermute | solution.py:422
  15.5 1.1 %stage.5 = (bf16[8,4736]{1,0:T(8,128)(2,1)S(1)}, bf16[8,4736]{1,0:T(8,128)(2,1)S(1)}, bf16[8,4736]{1,0:T(8,128)(2,1)S(1)}) custom-call(s32[5]{0:T(128)S(1)} %stack.23.spot_ref, bf16[16,4736]{1,0:T(8,128)(2,1)S(1)} %get-tuple-element.70.refs_0_.refs_2_, bf16[8,4736]{1,0:T(8,128)(2,1)S(1)} %collective-permute-done.refs_1_.refs_3_, ...), custom_call_target="tpu_custom_call" | custom-call | flops 1048576 | bytes 1048576 | tf_op jit(solution)/shard_map/stage1/stage/pallas_call | solution.py:413
  16.6 1.8 %collective-permute-start.1 = (bf16[8,4736]{1,0:T(8,128)(2,1)S(1)}, bf16[8,4736]{1,0:T(8,128)(2,1)S(1)}, u32[]{:S(2)}, u32[]{:S(2)}) collective-permute-start(bf16[8,4736]{1,0:T(8,128)(2,1)S(1)} %get-tuple-element.72.refs_5_), channel_id=1, source_target_pairs={{0,8},{8,0},{16,24},{24,16},{1,9},{9,1},{17,25},{25,17},{2,10},{10... | collective-permute-start | bytes 227336 | tf_op jit(solution)/shard_map/stage1/ppermute | solution.py:422
  18.4 1.5 %collective-permute-start.2 = (bf16[8,4736]{1,0:T(8,128)(2,1)S(1)}, bf16[8,4736]{1,0:T(8,128)(2,1)S(1)}, u32[]{:S(2)}, u32[]{:S(2)}) collective-permute-start(bf16[8,4736]{1,0:T(8,128)(2,1)S(1)} %get-tuple-element.73), channel_id=1, source_target_pairs={{0,16},{8,24},{16,0},{24,8},{1,17},{9,25},{17,1},{25,9},{2,18},{10... | collective-permute-start | bytes 227336 | tf_op jit(solution)/shard_map/stage1/ppermute | solution.py:422
  19.9 0.3 collective-permute-start.3
  20.1 7.0 %collective-permute-done.1.refs_2_.refs_4_ = bf16[8,4736]{1,0:T(8,128)(2,1)S(1)} collective-permute-done((bf16[8,4736]{1,0:T(8,128)(2,1)S(1)}, bf16[8,4736]{1,0:T(8,128)(2,1)S(1)}, u32[]{:S(2)}, u32[]{:S(2)}) %collective-permute-start.1) | collective-permute-done | bytes 75808 | tf_op jit(solution)/shard_map/stage1/ppermute | solution.py:422
  27.1 0.0 collective-permute-done.2.refs_3_.refs_5_
  27.2 3.7 %collective-permute-done.3.refs_4_.refs_6_ = bf16[8,4736]{1,0:T(8,128)(2,1)S(1)} collective-permute-done((bf16[8,4736]{1,0:T(8,128)(2,1)S(1)}, bf16[8,4736]{1,0:T(8,128)(2,1)S(1)}, u32[]{:S(2)}, u32[]{:S(2)}) %collective-permute-start.3) | collective-permute-done | bytes 75808 | tf_op jit(solution)/shard_map/stage1/ppermute | solution.py:422
  30.8 1.6 %stage.6.refs_6_ = bf16[8,4736]{1,0:T(8,128)(2,1)S(1)} custom-call(s32[5]{0:T(128)S(1)} %stack.23.spot_ref, bf16[16,4736]{1,0:T(8,128)(2,1)S(1)} %get-tuple-element.70.refs_0_.refs_2_, bf16[8,4736]{1,0:T(8,128)(2,1)S(1)} %collective-permute-done.refs_1_.refs_3_, bf16[8,4736]{1,0:T(8,128)(2,1)S(1)} %collective-permute-done.1.refs_2_.refs_4_, ...), custom_call_target="tpu_custom_call" | custom-call | flops 1048576 | bytes 1048576 | tf_op jit(solution)/shard_map/stage2/stage/pallas_call | solution.py:413
  32.4 2.0 %collective-permute-start.4 = (bf16[8,4736]{1,0:T(8,128)(2,1)S(1)}, bf16[8,4736]{1,0:T(8,128)(2,1)S(1)}, u32[]{:S(2)}, u32[]{:S(2)}) collective-permute-start(bf16[8,4736]{1,0:T(8,128)(2,1)S(1)} %stage.6.refs_6_), channel_id=1, source_target_pairs={{0,2},{2,0},{4,6},{6,4},{1,3},{3,1},{5,7},{7,5},{8,10},{10,8},{12,... | collective-permute-start | bytes 227336 | tf_op jit(solution)/shard_map/stage2/ppermute | solution.py:422
  34.4 0.0 copy-done.11
  34.4 0.0 copy-done.12
  34.4 10.4 %collective-permute-done.4.refs_5_.refs_7_ = bf16[8,4736]{1,0:T(8,128)(2,1)S(1)} collective-permute-done((bf16[8,4736]{1,0:T(8,128)(2,1)S(1)}, bf16[8,4736]{1,0:T(8,128)(2,1)S(1)}, u32[]{:S(2)}, u32[]{:S(2)}) %collective-permute-start.4) | collective-permute-done | bytes 75808 | tf_op jit(solution)/shard_map/stage2/ppermute | solution.py:422
  44.8 1.8 %stage.7.refs_0_ = bf16[8,5248]{1,0:T(8,128)(2,1)S(1)} custom-call(s32[5]{0:T(128)S(1)} %stack.23.spot_ref, bf16[16,4736]{1,0:T(8,128)(2,1)S(1)} %get-tuple-element.70.refs_0_.refs_2_, bf16[8,4736]{1,0:T(8,128)(2,1)S(1)} %collective-permute-done.refs_1_.refs_3_, bf16[8,4736]{1,0:T(8,128)(2,1)S(1)} %collective-permute-done.1.refs_2_.refs_4_, ...), custom_call_target="tpu_custom_call" | custom-call | flops 1048576 | bytes 1048576 | tf_op jit(solution)/shard_map/stage3/stage/pallas_call | solution.py:413
  46.6 4.7 %collective-permute-start.5 = (bf16[8,5248]{1,0:T(8,128)(2,1)S(1)}, bf16[8,5248]{1,0:T(8,128)(2,1)S(1)}, u32[]{:S(2)}, u32[]{:S(2)}) collective-permute-start(bf16[8,5248]{1,0:T(8,128)(2,1)S(1)} %stage.7.refs_0_), channel_id=1, source_target_pairs={{0,4},{2,6},{4,0},{6,2},{1,5},{3,7},{5,1},{7,3},{8,12},{10,14},{12... | collective-permute-start | bytes 251912 | tf_op jit(solution)/shard_map/stage3/ppermute | solution.py:422
  51.3 0.1 copy.12.id_col_ref
  51.4 8.1 %collective-permute-done.5.refs_1_.refs_8_ = bf16[8,5248]{1,0:T(8,128)(2,1)S(1)} collective-permute-done((bf16[8,5248]{1,0:T(8,128)(2,1)S(1)}, bf16[8,5248]{1,0:T(8,128)(2,1)S(1)}, u32[]{:S(2)}, u32[]{:S(2)}) %collective-permute-start.5) | collective-permute-done | bytes 84000 | tf_op jit(solution)/shard_map/stage3/ppermute | solution.py:422
  59.5 0.0 all-to-all-done.1.tokens_ref
  59.5 5.7 %place.2 = (bf16[128,64,128]{2,1,0:T(8,128)(2,1)}, f32[1,128]{1,0:T(1,128)}, s32[1]{0:T(128)}) custom-call(s32[5]{0:T(128)S(1)} %stack.23.spot_ref, f32[32,1]{1,0:T(8,128)S(1)} %copy.12.id_col_ref, f32[1,32]{1,0:T(1,128)S(1)} %get-tuple-element.134.id_row_ref, bf16[224,32,128]{2,1,0:T(8,128)(2,1)S(1)} %all-to-all-done.1.tokens_ref, ...), custom_call_target="tpu_custom_call" | custom-call | flops 1048576 | bytes 1048576 | tf_op jit(solution)/shard_map/place/pallas_call | solution.py:435
  65.3 0.6 while.10
  (11 shorter events, 0.0 us)
Async XLA Ops:
  4.2 1.2 %copy-start.1 = (bf16[224,32,128]{2,1,0:T(8,128)(2,1)}, bf16[224,32,128]{2,1,0:T(8,128)(2,1)S(1)}, u32[]{:S(2)}) copy-start(bf16[224,32,128]{2,1,0:T(8,128)(2,1)S(1)} %get-tuple-element.66) | copy-start | bytes 5505028
  5.5 7.4 %copy-start.2 = (s32[128]{0:T(128)S(1)}, s32[128]{0:T(128)}, u32[]{:S(2)}) copy-start(s32[128]{0:T(128)} %param.14) | copy-start | bytes 1540
  5.5 7.4 %copy-start.6 = (s32[128]{0:T(128)S(1)}, s32[128]{0:T(128)}, u32[]{:S(2)}) copy-start(s32[128]{0:T(128)} %param.12) | copy-start | bytes 1540
  5.5 7.4 %copy-start.7 = (s32[128]{0:T(128)S(1)}, s32[128]{0:T(128)}, u32[]{:S(2)}) copy-start(s32[128]{0:T(128)} %param.13) | copy-start | bytes 1540
  5.5 28.9 %copy-start.11 = (s32[32]{0:T(128)S(1)}, s32[32]{0:T(128)}, u32[]{:S(2)}) copy-start(s32[32]{0:T(128)} %constant.34.clone) | copy-start | bytes 388
  5.5 28.9 %copy-start.12 = (s32[32]{0:T(128)S(1)}, s32[32]{0:T(128)}, u32[]{:S(2)}) copy-start(s32[32]{0:T(128)} %constant.35.clone) | copy-start | bytes 388
  5.5 28.9 %copy-start.13 = (s32[32]{0:T(128)S(1)}, s32[32]{0:T(128)}, u32[]{:S(2)}) copy-start(s32[32]{0:T(128)} %constant.36.clone) | copy-start | bytes 388
  5.5 54.0 %all-to-all-start.1 = ((bf16[224,32,128]{2,1,0:T(8,128)(2,1)}), bf16[224,32,128]{2,1,0:T(8,128)(2,1)S(1)}, u32[]{:S(2)}, u32[]{:S(2)}) async-start(bf16[224,32,128]{2,1,0:T(8,128)(2,1)} %copy-done.1), calls=%async_computation.1 | async-start | bytes 3670016 | tf_op jit(solution)/shard_map/all_to_all | solution.py:393
  14.2 1.3 %collective-permute-start = (bf16[8,4736]{1,0:T(8,128)(2,1)S(1)}, bf16[8,4736]{1,0:T(8,128)(2,1)S(1)}, u32[]{:S(2)}, u32[]{:S(2)}) collective-permute-start(bf16[8,4736]{1,0:T(8,128)(2,1)S(1)} %get-tuple-element.71.refs_2_), channel_id=1, source_target_pairs={{0,1},{1,0},{2,3},{3,2},{4,5},{5,4},{6,7},{7,6},{8,9},{9,8},{10,11... | collective-permute-start | bytes 227336 | tf_op jit(solution)/shard_map/stage0/ppermute | solution.py:422
  15.5 49.8 %copy-start.5 = (f32[4096]{0:T(1024)S(1)}, f32[4096]{0:T(1024)}, u32[]{:S(2)}) copy-start(f32[4096]{0:T(1024)} %param.11) | copy-start | bytes 49156
  16.6 10.6 %collective-permute-start.1 = (bf16[8,4736]{1,0:T(8,128)(2,1)S(1)}, bf16[8,4736]{1,0:T(8,128)(2,1)S(1)}, u32[]{:S(2)}, u32[]{:S(2)}) collective-permute-start(bf16[8,4736]{1,0:T(8,128)(2,1)S(1)} %get-tuple-element.72.refs_5_), channel_id=1, source_target_pairs={{0,8},{8,0},{16,24},{24,16},{1,9},{9,1},{17,25},{25,17},{2,10},{10... | collective-permute-start | bytes 227336 | tf_op jit(solution)/shard_map/stage1/ppermute | solution.py:422
  18.4 8.7 %collective-permute-start.2 = (bf16[8,4736]{1,0:T(8,128)(2,1)S(1)}, bf16[8,4736]{1,0:T(8,128)(2,1)S(1)}, u32[]{:S(2)}, u32[]{:S(2)}) collective-permute-start(bf16[8,4736]{1,0:T(8,128)(2,1)S(1)} %get-tuple-element.73), channel_id=1, source_target_pairs={{0,16},{8,24},{16,0},{24,8},{1,17},{9,25},{17,1},{25,9},{2,18},{10... | collective-permute-start | bytes 227336 | tf_op jit(solution)/shard_map/stage1/ppermute | solution.py:422
  19.9 10.9 %collective-permute-start.3 = (bf16[8,4736]{1,0:T(8,128)(2,1)S(1)}, bf16[8,4736]{1,0:T(8,128)(2,1)S(1)}, u32[]{:S(2)}, u32[]{:S(2)}) collective-permute-start(bf16[8,4736]{1,0:T(8,128)(2,1)S(1)} %get-tuple-element.74), channel_id=1, source_target_pairs={{0,24},{8,16},{16,8},{24,0},{1,25},{9,17},{17,9},{25,1},{2,26},{10... | collective-permute-start | bytes 227336 | tf_op jit(solution)/shard_map/stage1/ppermute | solution.py:422
  32.4 12.4 %collective-permute-start.4 = (bf16[8,4736]{1,0:T(8,128)(2,1)S(1)}, bf16[8,4736]{1,0:T(8,128)(2,1)S(1)}, u32[]{:S(2)}, u32[]{:S(2)}) collective-permute-start(bf16[8,4736]{1,0:T(8,128)(2,1)S(1)} %stage.6.refs_6_), channel_id=1, source_target_pairs={{0,2},{2,0},{4,6},{6,4},{1,3},{3,1},{5,7},{7,5},{8,10},{10,8},{12,... | collective-permute-start | bytes 227336 | tf_op jit(solution)/shard_map/stage2/ppermute | solution.py:422
  46.6 12.9 %collective-permute-start.5 = (bf16[8,5248]{1,0:T(8,128)(2,1)S(1)}, bf16[8,5248]{1,0:T(8,128)(2,1)S(1)}, u32[]{:S(2)}, u32[]{:S(2)}) collective-permute-start(bf16[8,5248]{1,0:T(8,128)(2,1)S(1)} %stage.7.refs_0_), channel_id=1, source_target_pairs={{0,4},{2,6},{4,0},{6,2},{1,5},{3,7},{5,1},{7,3},{8,12},{10,14},{12... | collective-permute-start | bytes 251912 | tf_op jit(solution)/shard_map/stage3/ppermute | solution.py:422
  59.5 5.7 %copy-start.3 = (bf16[128,2,4096]{2,1,0:T(2,128)(2,1)S(1)}, bf16[128,2,4096]{2,1,0:T(2,128)(2,1)}, u32[]{:S(2)}) copy-start(bf16[128,2,4096]{2,1,0:T(2,128)(2,1)} %param.10) | copy-start | bytes 6291460

commit v4 on v3

--- a/solution.py
+++ b/solution.py
@@ -81,6 +81,7 @@
         part = pl.ds(k * piece, piece)
         pltpu.make_async_copy(rows_ref.at[part], rows.at[part], in_sems.at[k]).wait()
         return lax.fori_loop(k * per, (k + 1) * per, work, 0)
+
     lax.fori_loop(0, pieces, chunk, 0)
     out_ref[way[0, 0]] = tokens[0]
     if limit:
@@ -183,7 +184,7 @@
             at += v.shape[1]
 
 
-def next_body(near_axes, axis, room, owners, fields, width, count, features, parts, recent, spot_ref, *refs):
+def next_body(near_axes, axis, room, owners, fields, width, count, features, parts, recent, last, spot_ref, *refs):
     f32 = jnp.float32
     holds, own_ref, send_refs = refs[:parts], refs[parts], refs[parts + 1:]
     came = holds[parts - recent:]
@@ -211,42 +212,43 @@
                 known[-1] = known[-1] + value
     bad = jnp.maximum(bad, crowding(known, owners, fields, near_axes, axis, room, spot_ref))
     moved = select(holds, near_axes, axis, room, spot_ref, (features,))
-    finish(moved, known, bad, room, features, send_refs)
-
-
-def final_body(cap, slots, owners, fields, width, features, groups, parts, spot_ref, id_col_ref, id_row_ref, tokens_ref, *refs):
+    if not last:
+        finish(moved, known, bad, room, features, send_refs)
+        return
+    token_ref, entry_ref, own_entry_ref = send_refs
+    rows = len(known) * room
+    for ref, who in ((own_entry_ref, spot_ref[0]), (entry_ref, spot_ref[0] ^ (1 << axis[1]))):
+        lane = lax.broadcasted_iota(jnp.int32, (width, LANES), 0)
+        column = lax.broadcasted_iota(jnp.int32, (width, LANES), 1)
+        mine = jnp.where(((lane >> log2(owners)) == column) & ((lane & (owners - 1)) == who) & (lane < fields - owners), 1.0, 0.0)
+        for j, v in enumerate(known):
+            ref[j * room:(j + 1) * room, :] = jnp.dot(v, mine, preferred_element_type=f32).astype(jnp.bfloat16)
+        lane = lax.broadcasted_iota(jnp.int32, (room, LANES), 1)
+        info = jnp.where(lane == 4, bad, jnp.where(lane < 4, moved[:, features:], 0.0))
+        ref[rows:rows + room, :] = info.astype(jnp.bfloat16)
+    token_ref[...] = moved[:, :features].astype(jnp.bfloat16)
+
+
+def plan_body(cap, full, slots, owners, features, main, room, batch, spot_ref, id_col_ref, id_row_ref, own_ref, got_ref, *refs):
     f32, i32 = jnp.float32, jnp.int32
-    known_refs, holds = refs[:parts[0]], refs[parts[0]:parts[0] + parts[1]]
-    out_ref, adv_ref, flag_ref, wide, out, extra, more, slot_v, weight_v, slot_s, weight_s, table_sems, out_sems = refs[parts[0] + parts[1]:]
-    total, pieces = out.shape[0], out_sems.shape[0]
-    main = tokens_ref.shape[0]
-    half = features // LANES
-    bad = jnp.zeros((1, LANES), f32)
-    for ref in known_refs:
-        bad = jnp.maximum(bad, jnp.max(ref[:, features:features + LANES].astype(f32), axis=0, keepdims=True))
+    holds, (slot_ref, weight_ref, adv_ref, flag_ref) = refs[:-4], refs[-4:]
+    rows = owners // 2
+    total = slot_ref.shape[1]
+    info = [ref[:, features:features + LANES].astype(f32) for ref in holds] + [got_ref[rows:rows + room, :].astype(f32)]
+    bad = jnp.max(jnp.maximum(info[-1], own_ref[rows:rows + room, :].astype(f32)), axis=0, keepdims=True)
     bad = jnp.where(lax.broadcasted_iota(i32, (1, LANES), 1) == 4, bad, 0.0)
     flag_ref[0] = jnp.max(bad).astype(i32)
-    lane = lax.broadcasted_iota(i32, (width, LANES), 0)
-    column = lax.broadcasted_iota(i32, (width, LANES), 1)
-    mine = jnp.where(((lane >> (owners.bit_length() - 1)) == column) & ((lane & (owners - 1)) == spot_ref[0]) & (lane < fields - owners), 1.0, 0.0)
-    entry = []
-    for ref in known_refs:
-        for j in range((ref.shape[1] - features - LANES) // width):
-            at = features + LANES + j * width
-            entry.append(jnp.dot(ref[:, at:at + width].astype(f32), mine, preferred_element_type=f32))
-    entry = jnp.concatenate(entry, axis=0)
+    there = jnp.concatenate(info, axis=0).T
+    entry = jnp.concatenate([own_ref[:rows, :].astype(f32), got_ref[:rows, :].astype(f32)], axis=0)
     turned = entry.T
     ids, ids_row = id_col_ref[...], id_row_ref[...]
     label = [entry[:, k:k + 1] for k in range(slots)]
     size = [entry[:, slots + k:slots + k + 1] for k in range(slots)]
     level = [entry[:, 2 * slots + k:2 * slots + k + 1] for k in range(slots)]
-    if holds:
-        info = jnp.concatenate([ref[:, features:features + LANES].astype(f32) for ref in holds], axis=0)
-        there = info.T
-        key = jnp.where((there[0:1] > 0) & (there[1:2] == spot_ref[0].astype(f32)), there[2:3] * 256.0 + there[3:4], -1.0)
-        held_at = lax.broadcasted_iota(i32, (owners, key.shape[1]), 1).astype(f32)
+    key = jnp.where((there[0:1] > 0) & (there[1:2] == spot_ref[0].astype(f32)), there[2:3] * 256.0 + there[3:4], -1.0)
+    held_at = lax.broadcasted_iota(i32, (owners, key.shape[1]), 1).astype(f32)
     q = lax.broadcasted_iota(i32, (owners, total), 1).astype(f32)
-    rows = [jnp.zeros((1, total), f32) for _ in range(4)]
+    found = [jnp.zeros((owners, total), f32) for _ in range(5)]
     pos = jnp.zeros((owners, 1), f32)
     for k in range(slots):
         rank = jnp.zeros((owners, owners), f32)
@@ -258,31 +260,45 @@
         for t in range(2):
             p = pos if t == 0 else pos + jnp.where(size[k] > 1, 1.0, 0.0)
             place = ids * cap + p
-            if holds:
-                hit = jnp.where(key == ids * 256.0 + p, held_at, 0.0)
-                place = jnp.where(p < cap, place, main + jnp.sum(hit, axis=1, keepdims=True))
+            if 2 * k + t >= cap:
+                held = jnp.sum(jnp.where(key == ids * 256.0 + p, held_at, 0.0), axis=1, keepdims=True)
+                place = jnp.where(p < cap, place, main + held)
             places.append(place)
         hit = target == q
-        for r, v in enumerate((*places, size[k], level[k])):
-            rows[r] = rows[r] + jnp.sum(jnp.where(hit, v, 0.0), axis=0, keepdims=True)
+        for r, v in enumerate((*places, size[k], level[k], ids * full + pos)):
+            found[r] = jnp.where(hit, v, found[r])
         pos = pos + size[k]
-    slot_v[0:1, :] = rows[0].astype(i32)
-    slot_v[1:2, :] = rows[1].astype(i32)
-    n, lv = rows[2], rows[3]
-    a = lax.broadcasted_iota(i32, (total, total), 0) // G
-    b = lax.broadcasted_iota(i32, (total, total), 1) // G
-    group = jnp.where(a == b, 1.0, 0.0)
+    one, two, n, lv, far = (jnp.sum(v, axis=0, keepdims=True) for v in found)
+    a = lax.broadcasted_iota(i32, (total, total), 0)
+    b = lax.broadcasted_iota(i32, (total, total), 1)
+    spare = jnp.where(jnp.maximum(one, two) >= main, 1.0, 0.0)
+    near = jnp.where(a >> log2(batch) == b >> log2(batch), 1.0, 0.0)
+    slot_ref[0:1, :] = one.astype(i32)
+    slot_ref[1:2, :] = two.astype(i32)
+    slot_ref[2:3, :] = jnp.dot(spare, near, preferred_element_type=f32).astype(i32)
+    slot_ref[3:4, :] = far.astype(i32)
+    slot_ref[4:5, :] = (far + jnp.where(n > 1, 1.0, 0.0)).astype(i32)
+    slot_ref[5:8, :] = jnp.zeros((3, total), i32)
+    group = jnp.where(a >> log2(G) == b >> log2(G), 1.0, 0.0)
     mean = jnp.dot(lv, group, preferred_element_type=f32) * (1.0 / G)
     square = jnp.dot(lv * lv, group, preferred_element_type=f32) * (1.0 / G)
     spread = jnp.sqrt(square - mean * mean)
     advantage = (lv - mean) / jnp.maximum(spread, 1.0)
     adv_ref[...] = advantage
-    weight_v[0:1, :] = advantage / n
-    weight_v[1:2, :] = jnp.where(n > 1, advantage / n, 0.0)
-    copy_slot = pltpu.make_async_copy(slot_v, slot_s, table_sems.at[0])
-    copy_weight = pltpu.make_async_copy(weight_v, weight_s, table_sems.at[1])
+    weight_ref[0:1, :] = advantage / n
+    weight_ref[1:2, :] = jnp.where(n > 1, advantage / n, 0.0)
+
+
+def place_body(row, slot_ref, weight_ref, tokens_ref, *refs):
+    f32 = jnp.float32
+    holds, (out_ref, wide, out, extra, more, slot_s, weight_s, table_sems, out_sems) = refs[:-9], refs[-9:]
+    copy_slot = pltpu.make_async_copy(slot_ref, slot_s, table_sems.at[0])
+    copy_weight = pltpu.make_async_copy(weight_ref, weight_s, table_sems.at[1])
     copy_slot.start()
     copy_weight.start()
+    pieces = out_sems.shape[0]
+    main = tokens_ref.shape[0]
+    batch, half = wide.shape[0], wide.shape[1] // 2
     base = 0
     for ref in holds:
         p = ref.shape[0]
@@ -294,31 +310,38 @@
     copy_slot.wait()
     copy_weight.wait()
 
-    batch = wide.shape[0]
-    piece = total // pieces
-
-    def work(j, _):
+    def work(j, mixed):
         for e in range(batch):
             i = j * batch + e
             for t in range(2):
-                at = slot_s[t, i]
-                x = tokens_ref[jnp.minimum(at, main - 1)]
-                if holds:
+                at = slot_s[row + t, i]
+                if mixed:
+                    x = tokens_ref[jnp.minimum(at, main - 1)]
                     x = jnp.where(at < main, x, more[jnp.maximum(at - main, 0)])
-                x = x.astype(f32)
-                wide[e, pl.ds(t, half, stride=2), :] = x * weight_s[t, i]
+                else:
+                    x = tokens_ref[at]
+                wide[e, pl.ds(t, half, stride=2), :] = x.astype(f32) * weight_s[t, i]
         for e in range(batch):
             out[j * batch + e] = wide[e].astype(jnp.bfloat16)
-        return 0
 
     def chunk(k, _):
-        lax.fori_loop(k * (piece // batch), (k + 1) * (piece // batch), work, 0)
-        part = pl.ds(k * piece, piece)
+        if holds:
+            @pl.when(slot_s[2, k * batch] == 0)
+            def _():
+                work(k, False)
+
+            @pl.when(slot_s[2, k * batch] > 0)
+            def _():
+                work(k, True)
+        else:
+            work(k, False)
+        part = pl.ds(k * batch, batch)
         pltpu.make_async_copy(out.at[part], out_ref.at[part], out_sems.at[k]).start()
         return 0
+
     lax.fori_loop(0, pieces, chunk, 0)
     for k in range(pieces):
-        part = pl.ds(k * piece, piece)
+        part = pl.ds(k * batch, batch)
         pltpu.make_async_copy(out.at[part], out_ref.at[part], out_sems.at[k]).wait()
 
 
@@ -398,72 +421,81 @@
     steps = {a: np.zeros((1,), np.int32) for a in AXES}
     for n, (a, bit, size) in enumerate(stages):
         axis = (size, log2(stride[a]) + bit, n + 1)
-        with jax.named_scope("stage" + str(n)):
-            if n == 0:
-                hold, *sends = pl.pallas_call(
-                    functools.partial(first_body, tuple(near), axis, room, owners, fields, width, cap, groups),
-                    out_shape=[shape((limit, lanes + width))] + [shape((room, lanes + width))] * (size - 1),
-                    in_specs=[SMEM] + [VMEM] * 6, out_specs=[VMEM] * size,
-                    scratch_shapes=[pltpu.VMEM((limit, half, LANES), f32)],
-                    cost_estimate=COST, compiler_params=ROOM, name="stage",
-                )(spot, prompts, sizes_of, levels, nth, marks, spill)
-                holds = [hold]
-            else:
-                blocks = -(-count // room)
-                sends = pl.pallas_call(
-                    functools.partial(next_body, tuple(near), axis, room, owners, fields, width, before, features, len(holds), len(got)),
-                    out_shape=[shape((room, lanes + blocks * width))] * (size - 1),
-                    in_specs=[SMEM] + [VMEM] * (len(holds) + 1), out_specs=[VMEM] * (size - 1),
-                    cost_estimate=COST, compiler_params=ROOM, name="stage",
-                )(spot, *holds, own)
-            got = []
-            for k in range(1, size):
-                pairs = [(i, i ^ (k << bit)) for i in range(sizes[a])]
-                got.append(lax.ppermute(sends[k - 1], a, pairs))
+        if n == 0:
+            hold, *sends = pl.pallas_call(
+                functools.partial(first_body, tuple(near), axis, room, owners, fields, width, cap, groups),
+                out_shape=[shape((limit, lanes + width))] + [shape((room, lanes + width))] * (size - 1),
+                in_specs=[SMEM] + [VMEM] * 6, out_specs=[VMEM] * size,
+                scratch_shapes=[pltpu.VMEM((limit, half, LANES), f32)],
+                cost_estimate=COST, compiler_params=ROOM, name="stage",
+            )(spot, prompts, sizes_of, levels, nth, marks, spill)
+            holds = [hold]
+        else:
+            blocks = -(-count // room)
+            last = n + 1 == len(stages)
+            outs = [shape((room, lanes + blocks * width))] * (size - 1)
+            if last:
+                outs = [shape((room, features)), shape((count + room, LANES)), shape((count + room, LANES))]
+            sends = pl.pallas_call(
+                functools.partial(next_body, tuple(near), axis, room, owners, fields, width, before, features, len(holds), len(got), last),
+                out_shape=outs,
+                in_specs=[SMEM] + [VMEM] * (len(holds) + 1), out_specs=[VMEM] * len(outs),
+                cost_estimate=COST, compiler_params=ROOM, name="stage",
+            )(spot, *holds, own)
+        pairs = [[(i, i ^ (k << bit)) for i in range(sizes[a])] for k in range(size)]
+        if n + 1 < len(stages):
+            got = [lax.ppermute(sends[k - 1], a, pairs[k]) for k in range(1, size)]
             own = sends[0]
             holds = holds + got
+        else:
+            own = sends[2]
+            entries = lax.ppermute(sends[1], a, pairs[1])
+            landed = lax.ppermute(sends[0], a, pairs[1])
         near.append(axis)
         before = count
         count *= size
         steps = {x: np.concatenate([v + ((k << bit) if x == a else 0) for k in range(size)]).astype(np.int32) for x, v in steps.items()}
 
     ids = sum((coord[a] ^ steps[a]) * stride[a] for a in AXES).astype(f32)
-    known = [own, *got]
-
-    def finish_with(tokens, cap_used, extras):
-        spare = sum(h.shape[0] for h in extras)
+    batch = min(BATCH, count_here)
+    vmem_i32 = functools.partial(jax.ShapeDtypeStruct, dtype=i32)
+    slot_of, weight, advantages, bad = pl.pallas_call(
+        functools.partial(plan_body, cap, full, slots, owners, features, owners * cap, room, batch),
+        out_shape=[vmem_i32((8, count_here)), jax.ShapeDtypeStruct((window, count_here), f32), jax.ShapeDtypeStruct((1, count_here), f32), vmem_i32((1,))],
+        in_specs=[SMEM] + [VMEM] * (4 + len(holds)), out_specs=[VMEM, VMEM, VMEM, SMEM],
+        cost_estimate=COST, compiler_params=ROOM, name="plan",
+    )(spot, ids[:, None], ids[None], own, entries, *holds)
+
+    def place(tokens, row, extras):
+        spare = max(sum(h.shape[0] for h in extras), 8)
         return pl.pallas_call(
-            functools.partial(final_body, cap_used, slots, owners, fields, width, features, groups, (len(known), len(extras))),
-            out_shape=[
-                jax.ShapeDtypeStruct((count_here, window * half, LANES), bf16),
-                jax.ShapeDtypeStruct((1, count_here), f32),
-                jax.ShapeDtypeStruct((1,), i32),
-            ],
-            in_specs=[SMEM] + [VMEM] * (3 + len(known) + len(extras)), out_specs=[HBM, VMEM, SMEM],
+            functools.partial(place_body, row),
+            out_shape=jax.ShapeDtypeStruct((count_here, window * half, LANES), bf16),
+            in_specs=[VMEM] * (3 + len(extras)), out_specs=HBM,
             scratch_shapes=[
-                pltpu.VMEM((BATCH, window * half, LANES), f32),
+                pltpu.VMEM((batch, window * half, LANES), f32),
                 pltpu.VMEM((count_here, window * half, LANES), bf16),
-                pltpu.VMEM((max(spare, 8), half, LANES), f32),
-                pltpu.VMEM((max(spare, 8), half, LANES), bf16),
-                pltpu.VMEM((window, count_here), i32),
-                pltpu.VMEM((window, count_here), f32),
-                pltpu.SMEM((window, count_here), i32),
+                pltpu.VMEM((spare, half, LANES), f32),
+                pltpu.VMEM((spare, half, LANES), bf16),
+                pltpu.SMEM((8, count_here), i32),
                 pltpu.SMEM((window, count_here), f32),
                 pltpu.SemaphoreType.DMA((2,)),
-                pltpu.SemaphoreType.DMA((8,)),
+                pltpu.SemaphoreType.DMA((count_here // batch,)),
             ],
             cost_estimate=COST, compiler_params=ROOM, name="place",
-        )(spot, ids[:, None], ids[None], tokens, *known, *extras)
+        )(slot_of, weight, tokens, *extras)
 
     def whole(out):
         out = out.reshape(count_here, half, window, LANES).transpose(0, 2, 1, 3)
         return out.reshape(count_here, window, features)
-    out, advantages, bad = finish_with(came, cap, holds)
+
+    out = place(came, 0, [*holds, landed])
 
     def crowded(state):
         again = pack(spot, rows, gain, prompts, sizes_of, owners, full, groups, 0)
         all_came = lax.all_to_all(again[0], AXES, split_axis=0, concat_axis=0, tiled=True)
-        return jnp.zeros((1,), i32), whole(finish_with(all_came, full, [])[0])
+        return jnp.zeros((1,), i32), whole(place(all_came, 3, []))
+
     _, out = lax.while_loop(lambda state: state[0][0] > 0, crowded, (bad, whole(out)))
     return out, advantages.reshape(count_here)
 

time: 66.1 us -> 65 us (0.983)
  Pallas kernels: 15 us -> 14.3 us
    pallas_call x1 -> x2, Pallas kernels: 5.71 us -> 4.96 us  [the longest x1 2.73 us: place(): pl.pallas_call(functools.partial(place_body, row), out_shape=jax.ShapeDty...]
    ppermute x6 -> x7, waiting for transfers between devices: 30.2 us -> 29.6 us  [the longest x5 22.1 us: on_device(): got = [lax.ppermute(sends[k - 1], a, pairs[k]) for k in range(1, size)]]
    ppermute x6 -> x7, starting transfers between devices: 10.5 us -> 10.6 us  [the longest x5 5.85 us: on_device(): got = [lax.ppermute(sends[k - 1], a, pairs[k]) for k in range(1, size)]]
  transfers between devices with their start and end apart: 7 -> 8, of which waited for: 5 -> 5; matrix products, arithmetic and copies ran while one was open for 0% -> 0% of each run, Pallas kernels for 9% -> 13%
where the time goes in v4:
time: 65 us; the launch traced here: 64.7 us
  waiting for transfers between devices  29.6 us (46%)
  starting transfers between devices  17.9 us (28%)
  Pallas kernels  14.3 us (22%)
  local copies, waits for them, and re-layouts  1.44 us (2%)
  between operations  0.8 us (1%)
  loops' own time  0.69 us (1%)
    ppermute x5, waiting for transfers between devices, on_device(): got = [lax.ppermute(sends[k - 1], a, pairs[k]) for k in range(1, size)]  22.1 us
    ppermute x1, waiting for transfers between devices, on_device(): entries = lax.ppermute(sends[1], a, pairs[1])  7.44 us
    all_to_all x1, starting transfers between devices, on_device(): came = lax.all_to_all(sent, AXES, split_axis=0, concat_axis=0, tiled=True)  7.33 us
    ppermute x5, starting transfers between devices, on_device(): got = [lax.ppermute(sends[k - 1], a, pairs[k]) for k in range(1, size)]  5.85 us
    ppermute x1, starting transfers between devices, on_device(): landed = lax.ppermute(sends[0], a, pairs[1])  4.66 us
    pallas_call x3, Pallas kernels, on_device(): pl.pallas_call(functools.partial(next_body, tuple(near), axis, room, owne...  4.54 us
    pallas_call x1, Pallas kernels, pack(): pl.pallas_call(functools.partial(pack_body, cap, groups, limit), out_shap...  3.5 us
    pallas_call x1, Pallas kernels, place(): pl.pallas_call(functools.partial(place_body, row), out_shape=jax.ShapeDty...  2.73 us
  transfers between devices with their start and end apart: 8, of which 5 were waited for; matrix products, arithmetic and copies ran while one was open for 0% of the time, Pallas kernels for 13%

profile of v4, /device:TPU:0, one launch (start us, length us, event | category | flops | bytes accessed | tf_op | source)
XLA Modules:
  0.0 64.7 jit_solution(12591868332983029760)
XLA Ops:
  0.6 0.1 stack.23.spot_ref
  0.7 3.5 %pack.3 = (bf16[224,32,128]{2,1,0:T(8,128)(2,1)S(1)}, bf16[16,32,128]{2,1,0:T(8,128)(2,1)S(1)}, bf16[16,128]{1,0:T(8,128)(2,1)S(1)}, s32[1,128]{1,0:T(1,128)S(1)}) custom-call(s32[5]{0:T(128)S(1)} %stack.23.spot_ref, s32[1,128]{1,0:T(1,128)} %bitcast.38, s32[1,128]{1,0:T(1,128)} %bitcast.41, f32[32,128]{1,0:T(8,128)} %bitcast.36, bf16[128,64,128]{2,1,0:T(8,128)(2,1)} %bitcast.31), custom_call_target="tpu_custom_call" | custom-call | flops 1048576 | bytes 1048576 | tf_op jit(solution)/shard_map/pack/pallas_call | solution.py:359
  4.2 0.0 copy-start.1
  4.2 1.2 %copy-done.1 = bf16[224,32,128]{2,1,0:T(8,128)(2,1)} copy-done((bf16[224,32,128]{2,1,0:T(8,128)(2,1)}, bf16[224,32,128]{2,1,0:T(8,128)(2,1)S(1)}, u32[]{:S(2)}) %copy-start.1) | copy-done | bytes 1835032
  5.5 0.0 copy-start.9
  5.5 0.0 copy-start.10
  5.5 7.3 %all-to-all-start.1 = ((bf16[224,32,128]{2,1,0:T(8,128)(2,1)}), bf16[224,32,128]{2,1,0:T(8,128)(2,1)S(1)}, u32[]{:S(2)}, u32[]{:S(2)}) async-start(bf16[224,32,128]{2,1,0:T(8,128)(2,1)} %copy-done.1), calls=%async_computation.1 | async-start | bytes 3670016 | tf_op jit(solution)/shard_map/all_to_all | solution.py:416
  12.9 1.3 %stage.4 = (bf16[16,4736]{1,0:T(8,128)(2,1)S(1)}, bf16[8,4736]{1,0:T(8,128)(2,1)S(1)}) custom-call(s32[5]{0:T(128)S(1)} %stack.23.spot_ref, s32[1,128]{1,0:T(1,128)S(1)} %bitcast.39, s32[1,128]{1,0:T(1,128)S(1)} %bitcast.42, s32[1,128]{1,0:T(1,128)S(1)} %bitcast.30, s32[1,128]{1,0:T(1,128)S(1)} %get-tuple-element.64.nth_ref, ...), custom_call_target="tpu_custom_call" | custom-call | flops 1048576 | bytes 1048576 | tf_op jit(solution)/shard_map/stage/pallas_call | solution.py:425
  14.2 0.3 collective-permute-start
  14.5 1.0 %collective-permute-done.refs_1_ = bf16[8,4736]{1,0:T(8,128)(2,1)S(1)} collective-permute-done((bf16[8,4736]{1,0:T(8,128)(2,1)S(1)}, bf16[8,4736]{1,0:T(8,128)(2,1)S(1)}, u32[]{:S(2)}, u32[]{:S(2)}) %collective-permute-start) | collective-permute-done | bytes 75808 | tf_op jit(solution)/shard_map/ppermute | solution.py:447
  15.5 1.1 %stage.5 = (bf16[8,4736]{1,0:T(8,128)(2,1)S(1)}, bf16[8,4736]{1,0:T(8,128)(2,1)S(1)}, bf16[8,4736]{1,0:T(8,128)(2,1)S(1)}) custom-call(s32[5]{0:T(128)S(1)} %stack.23.spot_ref, bf16[16,4736]{1,0:T(8,128)(2,1)S(1)} %get-tuple-element.67.refs_0_, bf16[8,4736]{1,0:T(8,128)(2,1)S(1)} %collective-permute-done.refs_1_, bf16[8,4736]{1,0:T(8,128)(2,1)S(1)} %get-tuple-element.68.refs_2_), custom_call_target="tpu_custom_call" | custom-call | flops 1048576 | bytes 1048576 | tf_op jit(solution)/shard_map/stage/pallas_call | solution.py:439
  16.6 1.8 %collective-permute-start.1 = (bf16[8,4736]{1,0:T(8,128)(2,1)S(1)}, bf16[8,4736]{1,0:T(8,128)(2,1)S(1)}, u32[]{:S(2)}, u32[]{:S(2)}) collective-permute-start(bf16[8,4736]{1,0:T(8,128)(2,1)S(1)} %get-tuple-element.69.refs_5_), channel_id=1, source_target_pairs={{0,8},{8,0},{16,24},{24,16},{1,9},{9,1},{17,25},{25,17},{2,10},{10... | collective-permute-start | bytes 227336 | tf_op jit(solution)/shard_map/ppermute | solution.py:447
  18.4 1.5 %collective-permute-start.2 = (bf16[8,4736]{1,0:T(8,128)(2,1)S(1)}, bf16[8,4736]{1,0:T(8,128)(2,1)S(1)}, u32[]{:S(2)}, u32[]{:S(2)}) collective-permute-start(bf16[8,4736]{1,0:T(8,128)(2,1)S(1)} %get-tuple-element.70), channel_id=1, source_target_pairs={{0,16},{8,24},{16,0},{24,8},{1,17},{9,25},{17,1},{25,9},{2,18},{10... | collective-permute-start | bytes 227336 | tf_op jit(solution)/shard_map/ppermute | solution.py:447
  19.9 0.3 collective-permute-start.3
  20.1 7.0 %collective-permute-done.1.refs_2_ = bf16[8,4736]{1,0:T(8,128)(2,1)S(1)} collective-permute-done((bf16[8,4736]{1,0:T(8,128)(2,1)S(1)}, bf16[8,4736]{1,0:T(8,128)(2,1)S(1)}, u32[]{:S(2)}, u32[]{:S(2)}) %collective-permute-start.1) | collective-permute-done | bytes 75808 | tf_op jit(solution)/shard_map/ppermute | solution.py:447
  27.1 0.0 collective-permute-done.2.refs_3_
  27.2 3.7 %collective-permute-done.3.refs_4_ = bf16[8,4736]{1,0:T(8,128)(2,1)S(1)} collective-permute-done((bf16[8,4736]{1,0:T(8,128)(2,1)S(1)}, bf16[8,4736]{1,0:T(8,128)(2,1)S(1)}, u32[]{:S(2)}, u32[]{:S(2)}) %collective-permute-start.3) | collective-permute-done | bytes 75808 | tf_op jit(solution)/shard_map/ppermute | solution.py:447
  30.8 1.6 %stage.6.refs_6_ = bf16[8,4736]{1,0:T(8,128)(2,1)S(1)} custom-call(s32[5]{0:T(128)S(1)} %stack.23.spot_ref, bf16[16,4736]{1,0:T(8,128)(2,1)S(1)} %get-tuple-element.67.refs_0_, bf16[8,4736]{1,0:T(8,128)(2,1)S(1)} %collective-permute-done.refs_1_, bf16[8,4736]{1,0:T(8,128)(2,1)S(1)} %collective-permute-done.1.refs_2_, ...), custom_call_target="tpu_custom_call" | custom-call | flops 1048576 | bytes 1048576 | tf_op jit(solution)/shard_map/stage/pallas_call | solution.py:439
  32.4 2.0 %collective-permute-start.4 = (bf16[8,4736]{1,0:T(8,128)(2,1)S(1)}, bf16[8,4736]{1,0:T(8,128)(2,1)S(1)}, u32[]{:S(2)}, u32[]{:S(2)}) collective-permute-start(bf16[8,4736]{1,0:T(8,128)(2,1)S(1)} %stage.6.refs_6_), channel_id=1, source_target_pairs={{0,2},{2,0},{4,6},{6,4},{1,3},{3,1},{5,7},{7,5},{8,10},{10,8},{12,... | collective-permute-start | bytes 227336 | tf_op jit(solution)/shard_map/ppermute | solution.py:447
  34.4 10.4 %collective-permute-done.4.refs_5_ = bf16[8,4736]{1,0:T(8,128)(2,1)S(1)} collective-permute-done((bf16[8,4736]{1,0:T(8,128)(2,1)S(1)}, bf16[8,4736]{1,0:T(8,128)(2,1)S(1)}, u32[]{:S(2)}, u32[]{:S(2)}) %collective-permute-start.4) | collective-permute-done | bytes 75808 | tf_op jit(solution)/shard_map/ppermute | solution.py:447
  44.8 1.9 %stage.7 = (bf16[8,4096]{1,0:T(8,128)(2,1)S(1)}, bf16[24,128]{1,0:T(8,128)(2,1)S(1)}, bf16[24,128]{1,0:T(8,128)(2,1)S(1)}) custom-call(s32[5]{0:T(128)S(1)} %stack.23.spot_ref, bf16[16,4736]{1,0:T(8,128)(2,1)S(1)} %get-tuple-element.67.refs_0_, bf16[8,4736]{1,0:T(8,128)(2,1)S(1)} %collective-permute-done.refs_1_, ...), custom_call_target="tpu_custom_call" | custom-call | flops 1048576 | bytes 1048576 | tf_op jit(solution)/shard_map/stage/pallas_call | solution.py:439
  46.7 4.7 %collective-permute-start.6 = (bf16[8,4096]{1,0:T(8,128)(2,1)S(1)}, bf16[8,4096]{1,0:T(8,128)(2,1)S(1)}, u32[]{:S(2)}, u32[]{:S(2)}) collective-permute-start(bf16[8,4096]{1,0:T(8,128)(2,1)S(1)} %get-tuple-element.78), channel_id=1, source_target_pairs={{0,4},{2,6},{4,0},{6,2},{1,5},{3,7},{5,1},{7,3},{8,12},{10,14},{12... | collective-permute-start | bytes 196616 | tf_op jit(solution)/shard_map/ppermute | solution.py:453
  51.4 0.1 collective-permute-start.5
  51.5 0.1 copy.11.id_col_ref
  51.6 7.4 %collective-permute-done.5.got_ref = bf16[24,128]{1,0:T(8,128)(2,1)S(1)} collective-permute-done((bf16[24,128]{1,0:T(8,128)(2,1)S(1)}, bf16[24,128]{1,0:T(8,128)(2,1)S(1)}, u32[]{:S(2)}, u32[]{:S(2)}) %collective-permute-start.5) | collective-permute-done | bytes 6176 | tf_op jit(solution)/shard_map/ppermute | solution.py:452
  59.0 2.2 %plan.1 = (s32[8,128]{1,0:T(8,128)S(1)}, f32[2,128]{1,0:T(2,128)S(1)}, f32[1,128]{1,0:T(1,128)}, s32[1]{0:T(128)}) custom-call(s32[5]{0:T(128)S(1)} %stack.23.spot_ref, f32[32,1]{1,0:T(8,128)S(1)} %copy.11.id_col_ref, f32[1,32]{1,0:T(1,128)S(1)} %get-tuple-element.99.id_row_ref, bf16[24,128]{1,0:T(8,128)(2,1)S(1)} %get-tuple-element.72.own_ref, ...), custom_call_target="tpu_custom_call" | custom-call | flops 1048576 | bytes 1048576 | tf_op jit(solution)/shard_map/plan/pallas_call | solution.py:462
  61.2 0.0 collective-permute-done.6.refs_6_
  61.3 0.0 all-to-all-done.1.tokens_ref
  61.3 0.0 copy-start.3
  61.3 0.0 copy-start.5
  61.3 2.7 %place.3 = bf16[128,64,128]{2,1,0:T(8,128)(2,1)} custom-call(s32[8,128]{1,0:T(8,128)S(1)} %get-tuple-element.117.slot_ref, f32[2,128]{1,0:T(2,128)S(1)} %get-tuple-element.118.weight_ref, bf16[224,32,128]{2,1,0:T(8,128)(2,1)S(1)} %all-to-all-done.1.tokens_ref, bf16[16,4736]{1,0:T(8,128)(2,1)S(1)} %get-tuple-element.67.refs_0_, ...), custom_call_target="tpu_custom_call" | custom-call | flops 1048576 | bytes 1048576 | tf_op jit(solution)/shard_map/place/pallas_call | solution.py:471
  64.1 0.7 %while.9 = (s32[1]{0:T(128)}, bf16[128,2,4096]{2,1,0:T(2,128)(2,1)}, s32[5]{0:T(128)S(1)}, s32[1,128]{1,0:T(1,128)S(1)}, s32[1,128]{1,0:T(1,128)S(1)}, /*index=5...) while((s32[1]{0:T(128)}, ...), condition=%region_1.0_spmd, body=%region_0.0_spmd | while | flops 2097153 | bytes 28836024 | solution.py:499
  (14 shorter events, 0.0 us)
Async XLA Ops:
  4.2 1.2 %copy-start.1 = (bf16[224,32,128]{2,1,0:T(8,128)(2,1)}, bf16[224,32,128]{2,1,0:T(8,128)(2,1)S(1)}, u32[]{:S(2)}) copy-start(bf16[224,32,128]{2,1,0:T(8,128)(2,1)S(1)} %get-tuple-element.77) | copy-start | bytes 5505028
  5.5 7.4 %copy-start.2 = (s32[128]{0:T(128)S(1)}, s32[128]{0:T(128)}, u32[]{:S(2)}) copy-start(s32[128]{0:T(128)} %param.14) | copy-start | bytes 1540
  5.5 7.4 %copy-start.6 = (s32[128]{0:T(128)S(1)}, s32[128]{0:T(128)}, u32[]{:S(2)}) copy-start(s32[128]{0:T(128)} %param.12) | copy-start | bytes 1540
  5.5 7.4 %copy-start.7 = (s32[128]{0:T(128)S(1)}, s32[128]{0:T(128)}, u32[]{:S(2)}) copy-start(s32[128]{0:T(128)} %param.13) | copy-start | bytes 1540
  5.5 28.9 %copy-start.8 = (s32[32]{0:T(128)S(1)}, s32[32]{0:T(128)}, u32[]{:S(2)}) copy-start(s32[32]{0:T(128)} %constant.34.clone) | copy-start | bytes 388
  5.5 28.9 %copy-start.9 = (s32[32]{0:T(128)S(1)}, s32[32]{0:T(128)}, u32[]{:S(2)}) copy-start(s32[32]{0:T(128)} %constant.35.clone) | copy-start | bytes 388
  5.5 28.9 %copy-start.10 = (s32[32]{0:T(128)S(1)}, s32[32]{0:T(128)}, u32[]{:S(2)}) copy-start(s32[32]{0:T(128)} %constant.36.clone) | copy-start | bytes 388
  5.5 55.8 %all-to-all-start.1 = ((bf16[224,32,128]{2,1,0:T(8,128)(2,1)}), bf16[224,32,128]{2,1,0:T(8,128)(2,1)S(1)}, u32[]{:S(2)}, u32[]{:S(2)}) async-start(bf16[224,32,128]{2,1,0:T(8,128)(2,1)} %copy-done.1), calls=%async_computation.1 | async-start | bytes 3670016 | tf_op jit(solution)/shard_map/all_to_all | solution.py:416
  14.2 1.3 %collective-permute-start = (bf16[8,4736]{1,0:T(8,128)(2,1)S(1)}, bf16[8,4736]{1,0:T(8,128)(2,1)S(1)}, u32[]{:S(2)}, u32[]{:S(2)}) collective-permute-start(bf16[8,4736]{1,0:T(8,128)(2,1)S(1)} %get-tuple-element.68.refs_2_), channel_id=1, source_target_pairs={{0,1},{1,0},{2,3},{3,2},{4,5},{5,4},{6,7},{7,6},{8,9},{9,8},{10,11... | collective-permute-start | bytes 227336 | tf_op jit(solution)/shard_map/ppermute | solution.py:447
  16.6 10.6 %collective-permute-start.1 = (bf16[8,4736]{1,0:T(8,128)(2,1)S(1)}, bf16[8,4736]{1,0:T(8,128)(2,1)S(1)}, u32[]{:S(2)}, u32[]{:S(2)}) collective-permute-start(bf16[8,4736]{1,0:T(8,128)(2,1)S(1)} %get-tuple-element.69.refs_5_), channel_id=1, source_target_pairs={{0,8},{8,0},{16,24},{24,16},{1,9},{9,1},{17,25},{25,17},{2,10},{10... | collective-permute-start | bytes 227336 | tf_op jit(solution)/shard_map/ppermute | solution.py:447
  18.4 8.7 %collective-permute-start.2 = (bf16[8,4736]{1,0:T(8,128)(2,1)S(1)}, bf16[8,4736]{1,0:T(8,128)(2,1)S(1)}, u32[]{:S(2)}, u32[]{:S(2)}) collective-permute-start(bf16[8,4736]{1,0:T(8,128)(2,1)S(1)} %get-tuple-element.70), channel_id=1, source_target_pairs={{0,16},{8,24},{16,0},{24,8},{1,17},{9,25},{17,1},{25,9},{2,18},{10... | collective-permute-start | bytes 227336 | tf_op jit(solution)/shard_map/ppermute | solution.py:447
  19.9 10.9 %collective-permute-start.3 = (bf16[8,4736]{1,0:T(8,128)(2,1)S(1)}, bf16[8,4736]{1,0:T(8,128)(2,1)S(1)}, u32[]{:S(2)}, u32[]{:S(2)}) collective-permute-start(bf16[8,4736]{1,0:T(8,128)(2,1)S(1)} %get-tuple-element.71), channel_id=1, source_target_pairs={{0,24},{8,16},{16,8},{24,0},{1,25},{9,17},{17,9},{25,1},{2,26},{10... | collective-permute-start | bytes 227336 | tf_op jit(solution)/shard_map/ppermute | solution.py:447
  32.4 12.4 %collective-permute-start.4 = (bf16[8,4736]{1,0:T(8,128)(2,1)S(1)}, bf16[8,4736]{1,0:T(8,128)(2,1)S(1)}, u32[]{:S(2)}, u32[]{:S(2)}) collective-permute-start(bf16[8,4736]{1,0:T(8,128)(2,1)S(1)} %stage.6.refs_6_), channel_id=1, source_target_pairs={{0,2},{2,0},{4,6},{6,4},{1,3},{3,1},{5,7},{7,5},{8,10},{10,8},{12,... | collective-permute-start | bytes 227336 | tf_op jit(solution)/shard_map/ppermute | solution.py:447
  46.7 14.5 %collective-permute-start.6 = (bf16[8,4096]{1,0:T(8,128)(2,1)S(1)}, bf16[8,4096]{1,0:T(8,128)(2,1)S(1)}, u32[]{:S(2)}, u32[]{:S(2)}) collective-permute-start(bf16[8,4096]{1,0:T(8,128)(2,1)S(1)} %get-tuple-element.78), channel_id=1, source_target_pairs={{0,4},{2,6},{4,0},{6,2},{1,5},{3,7},{5,1},{7,3},{8,12},{10,14},{12... | collective-permute-start | bytes 196616 | tf_op jit(solution)/shard_map/ppermute | solution.py:453
  51.4 7.6 %collective-permute-start.5 = (bf16[24,128]{1,0:T(8,128)(2,1)S(1)}, bf16[24,128]{1,0:T(8,128)(2,1)S(1)}, u32[]{:S(2)}, u32[]{:S(2)}) collective-permute-start(bf16[24,128]{1,0:T(8,128)(2,1)S(1)} %get-tuple-element.73), channel_id=1, source_target_pairs={{0,4},{2,6},{4,0},{6,2},{1,5},{3,7},{5,1},{7,3},{8,12},{10,14},{12... | collective-permute-start | bytes 18440 | tf_op jit(solution)/shard_map/ppermute | solution.py:452
  61.3 2.8 %copy-start.3 = (bf16[128,2,4096]{2,1,0:T(2,128)(2,1)S(1)}, bf16[128,2,4096]{2,1,0:T(2,128)(2,1)}, u32[]{:S(2)}) copy-start(bf16[128,2,4096]{2,1,0:T(2,128)(2,1)} %param.10) | copy-start | bytes 6291460
  61.3 2.8 %copy-start.5 = (f32[4096]{0:T(1024)S(1)}, f32[4096]{0:T(1024)}, u32[]{:S(2)}) copy-start(f32[4096]{0:T(1024)} %param.11) | copy-start | bytes 49156

commit v5 on v4

--- a/solution.py
+++ b/solution.py
@@ -10,7 +10,7 @@
 G = 16
 AXES = ("gx", "gy", "gz")
 LANES = 128
-BATCH = 16
+BATCH = 32
 norm_eps = 1e-05
 
 
@@ -374,7 +374,7 @@
             pltpu.VMEM((few, LANES), jnp.int32),
             pltpu.SMEM((2, total), jnp.int32),
             pltpu.SMEM((few, LANES), jnp.int32),
-            pltpu.SemaphoreType.DMA((8,)),
+            pltpu.SemaphoreType.DMA((4,)),
             pltpu.SemaphoreType.DMA((2,)),
         ],
         cost_estimate=COST, compiler_params=ROOM,
@@ -457,7 +457,7 @@
         steps = {x: np.concatenate([v + ((k << bit) if x == a else 0) for k in range(size)]).astype(np.int32) for x, v in steps.items()}
 
     ids = sum((coord[a] ^ steps[a]) * stride[a] for a in AXES).astype(f32)
-    batch = min(BATCH, count_here)
+    batch = min(16, count_here)
     vmem_i32 = functools.partial(jax.ShapeDtypeStruct, dtype=i32)
     slot_of, weight, advantages, bad = pl.pallas_call(
         functools.partial(plan_body, cap, full, slots, owners, features, owners * cap, room, batch),

time: 65 us -> 64.6 us (level)
  no operation moved by 1% of the time
where the time goes in v5:
time: 64.6 us; the launch traced here: 64.4 us
  waiting for transfers between devices  29.6 us (46%)
  starting transfers between devices  17.9 us (28%)
  Pallas kernels  14 us (22%)
  local copies, waits for them, and re-layouts  1.44 us (2%)
  between operations  0.8 us (1%)
  loops' own time  0.69 us (1%)
    ppermute x5, waiting for transfers between devices, on_device(): got = [lax.ppermute(sends[k - 1], a, pairs[k]) for k in range(1, size)]  22.1 us
    ppermute x1, waiting for transfers between devices, on_device(): entries = lax.ppermute(sends[1], a, pairs[1])  7.44 us
    all_to_all x1, starting transfers between devices, on_device(): came = lax.all_to_all(sent, AXES, split_axis=0, concat_axis=0, tiled=True)  7.33 us
    ppermute x5, starting transfers between devices, on_device(): got = [lax.ppermute(sends[k - 1], a, pairs[k]) for k in range(1, size)]  5.86 us
    ppermute x1, starting transfers between devices, on_device(): landed = lax.ppermute(sends[0], a, pairs[1])  4.65 us
    pallas_call x3, Pallas kernels, on_device(): pl.pallas_call(functools.partial(next_body, tuple(near), axis, room, owne...  4.54 us
    pallas_call x1, Pallas kernels, pack(): pl.pallas_call(functools.partial(pack_body, cap, groups, limit), out_shap...  3.13 us
    pallas_call x1, Pallas kernels, place(): pl.pallas_call(functools.partial(place_body, row), out_shape=jax.ShapeDty...  2.73 us
  transfers between devices with their start and end apart: 8, of which 5 were waited for; matrix products, arithmetic and copies ran while one was open for 0% of the time, Pallas kernels for 13%

profile of v5, /device:TPU:0, one launch (start us, length us, event | category | flops | bytes accessed | tf_op | source)
XLA Modules:
  0.0 64.4 jit_solution(14742135257612212029)
XLA Ops:
  0.6 0.1 stack.23.spot_ref
  0.7 3.1 %pack.3 = (bf16[224,32,128]{2,1,0:T(8,128)(2,1)S(1)}, bf16[16,32,128]{2,1,0:T(8,128)(2,1)S(1)}, bf16[16,128]{1,0:T(8,128)(2,1)S(1)}, s32[1,128]{1,0:T(1,128)S(1)}) custom-call(s32[5]{0:T(128)S(1)} %stack.23.spot_ref, s32[1,128]{1,0:T(1,128)} %bitcast.38, s32[1,128]{1,0:T(1,128)} %bitcast.41, f32[32,128]{1,0:T(8,128)} %bitcast.36, bf16[128,64,128]{2,1,0:T(8,128)(2,1)} %bitcast.31), custom_call_target="tpu_custom_call" | custom-call | flops 1048576 | bytes 1048576 | tf_op jit(solution)/shard_map/pack/pallas_call | solution.py:359
  3.9 0.0 copy-start.1
  3.9 1.2 %copy-done.1 = bf16[224,32,128]{2,1,0:T(8,128)(2,1)} copy-done((bf16[224,32,128]{2,1,0:T(8,128)(2,1)}, bf16[224,32,128]{2,1,0:T(8,128)(2,1)S(1)}, u32[]{:S(2)}) %copy-start.1) | copy-done | bytes 1835032
  5.1 0.0 copy-start.9
  5.1 0.0 copy-start.10
  5.1 7.3 %all-to-all-start.1 = ((bf16[224,32,128]{2,1,0:T(8,128)(2,1)}), bf16[224,32,128]{2,1,0:T(8,128)(2,1)S(1)}, u32[]{:S(2)}, u32[]{:S(2)}) async-start(bf16[224,32,128]{2,1,0:T(8,128)(2,1)} %copy-done.1), calls=%async_computation.1 | async-start | bytes 3670016 | tf_op jit(solution)/shard_map/all_to_all | solution.py:416
  12.5 1.3 %stage.4 = (bf16[16,4736]{1,0:T(8,128)(2,1)S(1)}, bf16[8,4736]{1,0:T(8,128)(2,1)S(1)}) custom-call(s32[5]{0:T(128)S(1)} %stack.23.spot_ref, s32[1,128]{1,0:T(1,128)S(1)} %bitcast.39, s32[1,128]{1,0:T(1,128)S(1)} %bitcast.42, s32[1,128]{1,0:T(1,128)S(1)} %bitcast.30, s32[1,128]{1,0:T(1,128)S(1)} %get-tuple-element.64.nth_ref, ...), custom_call_target="tpu_custom_call" | custom-call | flops 1048576 | bytes 1048576 | tf_op jit(solution)/shard_map/stage/pallas_call | solution.py:425
  13.8 0.3 collective-permute-start
  14.1 1.0 %collective-permute-done.refs_1_ = bf16[8,4736]{1,0:T(8,128)(2,1)S(1)} collective-permute-done((bf16[8,4736]{1,0:T(8,128)(2,1)S(1)}, bf16[8,4736]{1,0:T(8,128)(2,1)S(1)}, u32[]{:S(2)}, u32[]{:S(2)}) %collective-permute-start) | collective-permute-done | bytes 75808 | tf_op jit(solution)/shard_map/ppermute | solution.py:447
  15.1 1.1 %stage.5 = (bf16[8,4736]{1,0:T(8,128)(2,1)S(1)}, bf16[8,4736]{1,0:T(8,128)(2,1)S(1)}, bf16[8,4736]{1,0:T(8,128)(2,1)S(1)}) custom-call(s32[5]{0:T(128)S(1)} %stack.23.spot_ref, bf16[16,4736]{1,0:T(8,128)(2,1)S(1)} %get-tuple-element.67.refs_0_, bf16[8,4736]{1,0:T(8,128)(2,1)S(1)} %collective-permute-done.refs_1_, bf16[8,4736]{1,0:T(8,128)(2,1)S(1)} %get-tuple-element.68.refs_2_), custom_call_target="tpu_custom_call" | custom-call | flops 1048576 | bytes 1048576 | tf_op jit(solution)/shard_map/stage/pallas_call | solution.py:439
  16.2 1.8 %collective-permute-start.1 = (bf16[8,4736]{1,0:T(8,128)(2,1)S(1)}, bf16[8,4736]{1,0:T(8,128)(2,1)S(1)}, u32[]{:S(2)}, u32[]{:S(2)}) collective-permute-start(bf16[8,4736]{1,0:T(8,128)(2,1)S(1)} %get-tuple-element.69.refs_5_), channel_id=1, source_target_pairs={{0,8},{8,0},{16,24},{24,16},{1,9},{9,1},{17,25},{25,17},{2,10},{10... | collective-permute-start | bytes 227336 | tf_op jit(solution)/shard_map/ppermute | solution.py:447
  18.0 1.5 %collective-permute-start.2 = (bf16[8,4736]{1,0:T(8,128)(2,1)S(1)}, bf16[8,4736]{1,0:T(8,128)(2,1)S(1)}, u32[]{:S(2)}, u32[]{:S(2)}) collective-permute-start(bf16[8,4736]{1,0:T(8,128)(2,1)S(1)} %get-tuple-element.70), channel_id=1, source_target_pairs={{0,16},{8,24},{16,0},{24,8},{1,17},{9,25},{17,1},{25,9},{2,18},{10... | collective-permute-start | bytes 227336 | tf_op jit(solution)/shard_map/ppermute | solution.py:447
  19.5 0.3 collective-permute-start.3
  19.8 7.0 %collective-permute-done.1.refs_2_ = bf16[8,4736]{1,0:T(8,128)(2,1)S(1)} collective-permute-done((bf16[8,4736]{1,0:T(8,128)(2,1)S(1)}, bf16[8,4736]{1,0:T(8,128)(2,1)S(1)}, u32[]{:S(2)}, u32[]{:S(2)}) %collective-permute-start.1) | collective-permute-done | bytes 75808 | tf_op jit(solution)/shard_map/ppermute | solution.py:447
  26.8 0.0 collective-permute-done.2.refs_3_
  26.8 3.7 %collective-permute-done.3.refs_4_ = bf16[8,4736]{1,0:T(8,128)(2,1)S(1)} collective-permute-done((bf16[8,4736]{1,0:T(8,128)(2,1)S(1)}, bf16[8,4736]{1,0:T(8,128)(2,1)S(1)}, u32[]{:S(2)}, u32[]{:S(2)}) %collective-permute-start.3) | collective-permute-done | bytes 75808 | tf_op jit(solution)/shard_map/ppermute | solution.py:447
  30.4 1.6 %stage.6.refs_6_ = bf16[8,4736]{1,0:T(8,128)(2,1)S(1)} custom-call(s32[5]{0:T(128)S(1)} %stack.23.spot_ref, bf16[16,4736]{1,0:T(8,128)(2,1)S(1)} %get-tuple-element.67.refs_0_, bf16[8,4736]{1,0:T(8,128)(2,1)S(1)} %collective-permute-done.refs_1_, bf16[8,4736]{1,0:T(8,128)(2,1)S(1)} %collective-permute-done.1.refs_2_, ...), custom_call_target="tpu_custom_call" | custom-call | flops 1048576 | bytes 1048576 | tf_op jit(solution)/shard_map/stage/pallas_call | solution.py:439
  32.0 2.0 %collective-permute-start.4 = (bf16[8,4736]{1,0:T(8,128)(2,1)S(1)}, bf16[8,4736]{1,0:T(8,128)(2,1)S(1)}, u32[]{:S(2)}, u32[]{:S(2)}) collective-permute-start(bf16[8,4736]{1,0:T(8,128)(2,1)S(1)} %stage.6.refs_6_), channel_id=1, source_target_pairs={{0,2},{2,0},{4,6},{6,4},{1,3},{3,1},{5,7},{7,5},{8,10},{10,8},{12,... | collective-permute-start | bytes 227336 | tf_op jit(solution)/shard_map/ppermute | solution.py:447
  34.0 10.4 %collective-permute-done.4.refs_5_ = bf16[8,4736]{1,0:T(8,128)(2,1)S(1)} collective-permute-done((bf16[8,4736]{1,0:T(8,128)(2,1)S(1)}, bf16[8,4736]{1,0:T(8,128)(2,1)S(1)}, u32[]{:S(2)}, u32[]{:S(2)}) %collective-permute-start.4) | collective-permute-done | bytes 75808 | tf_op jit(solution)/shard_map/ppermute | solution.py:447
  44.5 1.9 %stage.7 = (bf16[8,4096]{1,0:T(8,128)(2,1)S(1)}, bf16[24,128]{1,0:T(8,128)(2,1)S(1)}, bf16[24,128]{1,0:T(8,128)(2,1)S(1)}) custom-call(s32[5]{0:T(128)S(1)} %stack.23.spot_ref, bf16[16,4736]{1,0:T(8,128)(2,1)S(1)} %get-tuple-element.67.refs_0_, bf16[8,4736]{1,0:T(8,128)(2,1)S(1)} %collective-permute-done.refs_1_, ...), custom_call_target="tpu_custom_call" | custom-call | flops 1048576 | bytes 1048576 | tf_op jit(solution)/shard_map/stage/pallas_call | solution.py:439
  46.4 4.7 %collective-permute-start.6 = (bf16[8,4096]{1,0:T(8,128)(2,1)S(1)}, bf16[8,4096]{1,0:T(8,128)(2,1)S(1)}, u32[]{:S(2)}, u32[]{:S(2)}) collective-permute-start(bf16[8,4096]{1,0:T(8,128)(2,1)S(1)} %get-tuple-element.78), channel_id=1, source_target_pairs={{0,4},{2,6},{4,0},{6,2},{1,5},{3,7},{5,1},{7,3},{8,12},{10,14},{12... | collective-permute-start | bytes 196616 | tf_op jit(solution)/shard_map/ppermute | solution.py:453
  51.0 0.1 collective-permute-start.5
  51.1 0.1 copy.11.id_col_ref
  51.2 7.4 %collective-permute-done.5.got_ref = bf16[24,128]{1,0:T(8,128)(2,1)S(1)} collective-permute-done((bf16[24,128]{1,0:T(8,128)(2,1)S(1)}, bf16[24,128]{1,0:T(8,128)(2,1)S(1)}, u32[]{:S(2)}, u32[]{:S(2)}) %collective-permute-start.5) | collective-permute-done | bytes 6176 | tf_op jit(solution)/shard_map/ppermute | solution.py:452
  58.6 2.2 %plan.1 = (s32[8,128]{1,0:T(8,128)S(1)}, f32[2,128]{1,0:T(2,128)S(1)}, f32[1,128]{1,0:T(1,128)}, s32[1]{0:T(128)}) custom-call(s32[5]{0:T(128)S(1)} %stack.23.spot_ref, f32[32,1]{1,0:T(8,128)S(1)} %copy.11.id_col_ref, f32[1,32]{1,0:T(1,128)S(1)} %get-tuple-element.99.id_row_ref, bf16[24,128]{1,0:T(8,128)(2,1)S(1)} %get-tuple-element.72.own_ref, ...), custom_call_target="tpu_custom_call" | custom-call | flops 1048576 | bytes 1048576 | tf_op jit(solution)/shard_map/plan/pallas_call | solution.py:462
  60.9 0.0 collective-permute-done.6.refs_6_
  60.9 0.0 all-to-all-done.1.tokens_ref
  60.9 0.0 copy-start.3
  60.9 0.0 copy-start.5
  60.9 2.7 %place.3 = bf16[128,64,128]{2,1,0:T(8,128)(2,1)} custom-call(s32[8,128]{1,0:T(8,128)S(1)} %get-tuple-element.117.slot_ref, f32[2,128]{1,0:T(2,128)S(1)} %get-tuple-element.118.weight_ref, bf16[224,32,128]{2,1,0:T(8,128)(2,1)S(1)} %all-to-all-done.1.tokens_ref, bf16[16,4736]{1,0:T(8,128)(2,1)S(1)} %get-tuple-element.67.refs_0_, ...), custom_call_target="tpu_custom_call" | custom-call | flops 1048576 | bytes 1048576 | tf_op jit(solution)/shard_map/place/pallas_call | solution.py:471
  63.7 0.7 %while.9 = (s32[1]{0:T(128)}, bf16[128,2,4096]{2,1,0:T(2,128)(2,1)}, s32[5]{0:T(128)S(1)}, s32[1,128]{1,0:T(1,128)S(1)}, s32[1,128]{1,0:T(1,128)S(1)}, /*index=5...) while((s32[1]{0:T(128)}, ...), condition=%region_1.0_spmd, body=%region_0.0_spmd | while | flops 2097153 | bytes 28836024 | solution.py:499
  (14 shorter events, 0.0 us)
Async XLA Ops:
  3.9 1.2 %copy-start.1 = (bf16[224,32,128]{2,1,0:T(8,128)(2,1)}, bf16[224,32,128]{2,1,0:T(8,128)(2,1)S(1)}, u32[]{:S(2)}) copy-start(bf16[224,32,128]{2,1,0:T(8,128)(2,1)S(1)} %get-tuple-element.77) | copy-start | bytes 5505028
  5.1 7.4 %copy-start.2 = (s32[128]{0:T(128)S(1)}, s32[128]{0:T(128)}, u32[]{:S(2)}) copy-start(s32[128]{0:T(128)} %param.14) | copy-start | bytes 1540
  5.1 7.4 %copy-start.6 = (s32[128]{0:T(128)S(1)}, s32[128]{0:T(128)}, u32[]{:S(2)}) copy-start(s32[128]{0:T(128)} %param.12) | copy-start | bytes 1540
  5.1 7.4 %copy-start.7 = (s32[128]{0:T(128)S(1)}, s32[128]{0:T(128)}, u32[]{:S(2)}) copy-start(s32[128]{0:T(128)} %param.13) | copy-start | bytes 1540
  5.1 28.9 %copy-start.8 = (s32[32]{0:T(128)S(1)}, s32[32]{0:T(128)}, u32[]{:S(2)}) copy-start(s32[32]{0:T(128)} %constant.34.clone) | copy-start | bytes 388
  5.1 28.9 %copy-start.9 = (s32[32]{0:T(128)S(1)}, s32[32]{0:T(128)}, u32[]{:S(2)}) copy-start(s32[32]{0:T(128)} %constant.35.clone) | copy-start | bytes 388
  5.1 28.9 %copy-start.10 = (s32[32]{0:T(128)S(1)}, s32[32]{0:T(128)}, u32[]{:S(2)}) copy-start(s32[32]{0:T(128)} %constant.36.clone) | copy-start | bytes 388
  5.1 55.8 %all-to-all-start.1 = ((bf16[224,32,128]{2,1,0:T(8,128)(2,1)}), bf16[224,32,128]{2,1,0:T(8,128)(2,1)S(1)}, u32[]{:S(2)}, u32[]{:S(2)}) async-start(bf16[224,32,128]{2,1,0:T(8,128)(2,1)} %copy-done.1), calls=%async_computation.1 | async-start | bytes 3670016 | tf_op jit(solution)/shard_map/all_to_all | solution.py:416
  13.8 1.3 %collective-permute-start = (bf16[8,4736]{1,0:T(8,128)(2,1)S(1)}, bf16[8,4736]{1,0:T(8,128)(2,1)S(1)}, u32[]{:S(2)}, u32[]{:S(2)}) collective-permute-start(bf16[8,4736]{1,0:T(8,128)(2,1)S(1)} %get-tuple-element.68.refs_2_), channel_id=1, source_target_pairs={{0,1},{1,0},{2,3},{3,2},{4,5},{5,4},{6,7},{7,6},{8,9},{9,8},{10,11... | collective-permute-start | bytes 227336 | tf_op jit(solution)/shard_map/ppermute | solution.py:447
  16.2 10.6 %collective-permute-start.1 = (bf16[8,4736]{1,0:T(8,128)(2,1)S(1)}, bf16[8,4736]{1,0:T(8,128)(2,1)S(1)}, u32[]{:S(2)}, u32[]{:S(2)}) collective-permute-start(bf16[8,4736]{1,0:T(8,128)(2,1)S(1)} %get-tuple-element.69.refs_5_), channel_id=1, source_target_pairs={{0,8},{8,0},{16,24},{24,16},{1,9},{9,1},{17,25},{25,17},{2,10},{10... | collective-permute-start | bytes 227336 | tf_op jit(solution)/shard_map/ppermute | solution.py:447
  18.0 8.7 %collective-permute-start.2 = (bf16[8,4736]{1,0:T(8,128)(2,1)S(1)}, bf16[8,4736]{1,0:T(8,128)(2,1)S(1)}, u32[]{:S(2)}, u32[]{:S(2)}) collective-permute-start(bf16[8,4736]{1,0:T(8,128)(2,1)S(1)} %get-tuple-element.70), channel_id=1, source_target_pairs={{0,16},{8,24},{16,0},{24,8},{1,17},{9,25},{17,1},{25,9},{2,18},{10... | collective-permute-start | bytes 227336 | tf_op jit(solution)/shard_map/ppermute | solution.py:447
  19.5 10.9 %collective-permute-start.3 = (bf16[8,4736]{1,0:T(8,128)(2,1)S(1)}, bf16[8,4736]{1,0:T(8,128)(2,1)S(1)}, u32[]{:S(2)}, u32[]{:S(2)}) collective-permute-start(bf16[8,4736]{1,0:T(8,128)(2,1)S(1)} %get-tuple-element.71), channel_id=1, source_target_pairs={{0,24},{8,16},{16,8},{24,0},{1,25},{9,17},{17,9},{25,1},{2,26},{10... | collective-permute-start | bytes 227336 | tf_op jit(solution)/shard_map/ppermute | solution.py:447
  32.0 12.4 %collective-permute-start.4 = (bf16[8,4736]{1,0:T(8,128)(2,1)S(1)}, bf16[8,4736]{1,0:T(8,128)(2,1)S(1)}, u32[]{:S(2)}, u32[]{:S(2)}) collective-permute-start(bf16[8,4736]{1,0:T(8,128)(2,1)S(1)} %stage.6.refs_6_), channel_id=1, source_target_pairs={{0,2},{2,0},{4,6},{6,4},{1,3},{3,1},{5,7},{7,5},{8,10},{10,8},{12,... | collective-permute-start | bytes 227336 | tf_op jit(solution)/shard_map/ppermute | solution.py:447
  46.4 14.5 %collective-permute-start.6 = (bf16[8,4096]{1,0:T(8,128)(2,1)S(1)}, bf16[8,4096]{1,0:T(8,128)(2,1)S(1)}, u32[]{:S(2)}, u32[]{:S(2)}) collective-permute-start(bf16[8,4096]{1,0:T(8,128)(2,1)S(1)} %get-tuple-element.78), channel_id=1, source_target_pairs={{0,4},{2,6},{4,0},{6,2},{1,5},{3,7},{5,1},{7,3},{8,12},{10,14},{12... | collective-permute-start | bytes 196616 | tf_op jit(solution)/shard_map/ppermute | solution.py:453
  51.0 7.6 %collective-permute-start.5 = (bf16[24,128]{1,0:T(8,128)(2,1)S(1)}, bf16[24,128]{1,0:T(8,128)(2,1)S(1)}, u32[]{:S(2)}, u32[]{:S(2)}) collective-permute-start(bf16[24,128]{1,0:T(8,128)(2,1)S(1)} %get-tuple-element.73), channel_id=1, source_target_pairs={{0,4},{2,6},{4,0},{6,2},{1,5},{3,7},{5,1},{7,3},{8,12},{10,14},{12... | collective-permute-start | bytes 18440 | tf_op jit(solution)/shard_map/ppermute | solution.py:452
  60.9 2.8 %copy-start.3 = (bf16[128,2,4096]{2,1,0:T(2,128)(2,1)S(1)}, bf16[128,2,4096]{2,1,0:T(2,128)(2,1)}, u32[]{:S(2)}) copy-start(bf16[128,2,4096]{2,1,0:T(2,128)(2,1)} %param.10) | copy-start | bytes 6291460
  60.9 2.8 %copy-start.5 = (f32[4096]{0:T(1024)S(1)}, f32[4096]{0:T(1024)}, u32[]{:S(2)}) copy-start(f32[4096]{0:T(1024)} %param.11) | copy-start | bytes 49156

commit v6 on v5

--- a/solution.py
+++ b/solution.py
@@ -210,7 +210,8 @@
                 known.append(value)
             else:
                 known[-1] = known[-1] + value
-    bad = jnp.maximum(bad, crowding(known, owners, fields, near_axes, axis, room, spot_ref))
+    seats = 2 * send_refs[0].shape[0] if last else room
+    bad = jnp.maximum(bad, crowding(known, owners, fields, near_axes, axis, seats, spot_ref))
     moved = select(holds, near_axes, axis, room, spot_ref, (features,))
     if not last:
         finish(moved, known, bad, room, features, send_refs)
@@ -226,7 +227,8 @@
         lane = lax.broadcasted_iota(jnp.int32, (room, LANES), 1)
         info = jnp.where(lane == 4, bad, jnp.where(lane < 4, moved[:, features:], 0.0))
         ref[rows:rows + room, :] = info.astype(jnp.bfloat16)
-    token_ref[...] = moved[:, :features].astype(jnp.bfloat16)
+    for i in range(token_ref.shape[0]):
+        token_ref[i] = moved[2 * i:2 * i + 2, :features].astype(jnp.bfloat16)
 
 
 def plan_body(cap, full, slots, owners, features, main, room, batch, spot_ref, id_col_ref, id_row_ref, own_ref, got_ref, *refs):
@@ -301,10 +303,11 @@
     batch, half = wide.shape[0], wide.shape[1] // 2
     base = 0
     for ref in holds:
-        p = ref.shape[0]
-        for c in range(half):
-            extra[base:base + p, c, :] = ref[:, c * LANES:(c + 1) * LANES].astype(f32)
-        base += p
+        for piece in ([ref] if len(ref.shape) == 2 else [ref.at[i] for i in range(ref.shape[0])]):
+            p = piece.shape[0]
+            for c in range(half):
+                extra[base:base + p, c, :] = piece[:, c * LANES:(c + 1) * LANES].astype(f32)
+            base += p
     for h in range(base):
         more[h] = extra[h].astype(jnp.bfloat16)
     copy_slot.wait()
@@ -435,7 +438,7 @@
             last = n + 1 == len(stages)
             outs = [shape((room, lanes + blocks * width))] * (size - 1)
             if last:
-                outs = [shape((room, features)), shape((count + room, LANES)), shape((count + room, LANES))]
+                outs = [shape((room // 2 - room // 8, 2, features)), shape((count + room, LANES)), shape((count + room, LANES))]
             sends = pl.pallas_call(
                 functools.partial(next_body, tuple(near), axis, room, owners, fields, width, before, features, len(holds), len(got), last),
                 out_shape=outs,
@@ -467,7 +470,7 @@
     )(spot, ids[:, None], ids[None], own, entries, *holds)
 
     def place(tokens, row, extras):
-        spare = max(sum(h.shape[0] for h in extras), 8)
+        spare = max(sum(h.size // features if h.ndim == 3 else h.shape[0] for h in extras), 8)
         return pl.pallas_call(
             functools.partial(place_body, row),
             out_shape=jax.ShapeDtypeStruct((count_here, window * half, LANES), bf16),

time: 64.6 us -> 63.9 us (0.989)
  waiting for transfers between devices: 29.6 us -> 28.9 us
    ppermute x1, waiting for transfers between devices: 7.44 us -> 6.74 us  [on_device(): entries = lax.ppermute(sends[1], a, pairs[1])]
where the time goes in v6:
time: 63.9 us; the launch traced here: 63.7 us
  waiting for transfers between devices  28.9 us (45%)
  starting transfers between devices  17.9 us (28%)
  Pallas kernels  13.9 us (22%)
  local copies, waits for them, and re-layouts  1.44 us (2%)
  between operations  0.8 us (1%)
  loops' own time  0.69 us (1%)
    ppermute x5, waiting for transfers between devices, on_device(): got = [lax.ppermute(sends[k - 1], a, pairs[k]) for k in range(1, size)]  22.1 us
    all_to_all x1, starting transfers between devices, on_device(): came = lax.all_to_all(sent, AXES, split_axis=0, concat_axis=0, tiled=True)  7.33 us
    ppermute x1, waiting for transfers between devices, on_device(): entries = lax.ppermute(sends[1], a, pairs[1])  6.74 us
    ppermute x5, starting transfers between devices, on_device(): got = [lax.ppermute(sends[k - 1], a, pairs[k]) for k in range(1, size)]  5.86 us
    ppermute x1, starting transfers between devices, on_device(): landed = lax.ppermute(sends[0], a, pairs[1])  4.65 us
    pallas_call x3, Pallas kernels, on_device(): pl.pallas_call(functools.partial(next_body, tuple(near), axis, room, owne...  4.54 us
    pallas_call x1, Pallas kernels, pack(): pl.pallas_call(functools.partial(pack_body, cap, groups, limit), out_shap...  3.13 us
    pallas_call x1, Pallas kernels, place(): pl.pallas_call(functools.partial(place_body, row), out_shape=jax.ShapeDty...  2.73 us
  transfers between devices with their start and end apart: 8, of which 5 were waited for; matrix products, arithmetic and copies ran while one was open for 0% of the time, Pallas kernels for 13%

profile of v6, /device:TPU:0, one launch (start us, length us, event | category | flops | bytes accessed | tf_op | source)
XLA Modules:
  0.0 63.7 jit_solution(3443437863917574019)
XLA Ops:
  0.6 0.1 stack.23.spot_ref
  0.7 3.1 %pack.3 = (bf16[224,32,128]{2,1,0:T(8,128)(2,1)S(1)}, bf16[16,32,128]{2,1,0:T(8,128)(2,1)S(1)}, bf16[16,128]{1,0:T(8,128)(2,1)S(1)}, s32[1,128]{1,0:T(1,128)S(1)}) custom-call(s32[5]{0:T(128)S(1)} %stack.23.spot_ref, s32[1,128]{1,0:T(1,128)} %bitcast.38, s32[1,128]{1,0:T(1,128)} %bitcast.41, f32[32,128]{1,0:T(8,128)} %bitcast.36, bf16[128,64,128]{2,1,0:T(8,128)(2,1)} %bitcast.31), custom_call_target="tpu_custom_call" | custom-call | flops 1048576 | bytes 1048576 | tf_op jit(solution)/shard_map/pack/pallas_call | solution.py:362
  3.9 0.0 copy-start.1
  3.9 1.2 %copy-done.1 = bf16[224,32,128]{2,1,0:T(8,128)(2,1)} copy-done((bf16[224,32,128]{2,1,0:T(8,128)(2,1)}, bf16[224,32,128]{2,1,0:T(8,128)(2,1)S(1)}, u32[]{:S(2)}) %copy-start.1) | copy-done | bytes 1835032
  5.1 0.0 copy-start.9
  5.1 0.0 copy-start.10
  5.1 7.3 %all-to-all-start.1 = ((bf16[224,32,128]{2,1,0:T(8,128)(2,1)}), bf16[224,32,128]{2,1,0:T(8,128)(2,1)S(1)}, u32[]{:S(2)}, u32[]{:S(2)}) async-start(bf16[224,32,128]{2,1,0:T(8,128)(2,1)} %copy-done.1), calls=%async_computation.1 | async-start | bytes 3670016 | tf_op jit(solution)/shard_map/all_to_all | solution.py:419
  12.5 1.3 %stage.4 = (bf16[16,4736]{1,0:T(8,128)(2,1)S(1)}, bf16[8,4736]{1,0:T(8,128)(2,1)S(1)}) custom-call(s32[5]{0:T(128)S(1)} %stack.23.spot_ref, s32[1,128]{1,0:T(1,128)S(1)} %bitcast.39, s32[1,128]{1,0:T(1,128)S(1)} %bitcast.42, s32[1,128]{1,0:T(1,128)S(1)} %bitcast.30, s32[1,128]{1,0:T(1,128)S(1)} %get-tuple-element.64.nth_ref, ...), custom_call_target="tpu_custom_call" | custom-call | flops 1048576 | bytes 1048576 | tf_op jit(solution)/shard_map/stage/pallas_call | solution.py:428
  13.8 0.3 collective-permute-start
  14.1 1.0 %collective-permute-done.refs_1_ = bf16[8,4736]{1,0:T(8,128)(2,1)S(1)} collective-permute-done((bf16[8,4736]{1,0:T(8,128)(2,1)S(1)}, bf16[8,4736]{1,0:T(8,128)(2,1)S(1)}, u32[]{:S(2)}, u32[]{:S(2)}) %collective-permute-start) | collective-permute-done | bytes 75808 | tf_op jit(solution)/shard_map/ppermute | solution.py:450
  15.1 1.1 %stage.5 = (bf16[8,4736]{1,0:T(8,128)(2,1)S(1)}, bf16[8,4736]{1,0:T(8,128)(2,1)S(1)}, bf16[8,4736]{1,0:T(8,128)(2,1)S(1)}) custom-call(s32[5]{0:T(128)S(1)} %stack.23.spot_ref, bf16[16,4736]{1,0:T(8,128)(2,1)S(1)} %get-tuple-element.67.refs_0_, bf16[8,4736]{1,0:T(8,128)(2,1)S(1)} %collective-permute-done.refs_1_, bf16[8,4736]{1,0:T(8,128)(2,1)S(1)} %get-tuple-element.68.refs_2_), custom_call_target="tpu_custom_call" | custom-call | flops 1048576 | bytes 1048576 | tf_op jit(solution)/shard_map/stage/pallas_call | solution.py:442
  16.2 1.8 %collective-permute-start.1 = (bf16[8,4736]{1,0:T(8,128)(2,1)S(1)}, bf16[8,4736]{1,0:T(8,128)(2,1)S(1)}, u32[]{:S(2)}, u32[]{:S(2)}) collective-permute-start(bf16[8,4736]{1,0:T(8,128)(2,1)S(1)} %get-tuple-element.69.refs_5_), channel_id=1, source_target_pairs={{0,8},{8,0},{16,24},{24,16},{1,9},{9,1},{17,25},{25,17},{2,10},{10... | collective-permute-start | bytes 227336 | tf_op jit(solution)/shard_map/ppermute | solution.py:450
  18.0 1.5 %collective-permute-start.2 = (bf16[8,4736]{1,0:T(8,128)(2,1)S(1)}, bf16[8,4736]{1,0:T(8,128)(2,1)S(1)}, u32[]{:S(2)}, u32[]{:S(2)}) collective-permute-start(bf16[8,4736]{1,0:T(8,128)(2,1)S(1)} %get-tuple-element.70), channel_id=1, source_target_pairs={{0,16},{8,24},{16,0},{24,8},{1,17},{9,25},{17,1},{25,9},{2,18},{10... | collective-permute-start | bytes 227336 | tf_op jit(solution)/shard_map/ppermute | solution.py:450
  19.5 0.3 collective-permute-start.3
  19.8 7.0 %collective-permute-done.1.refs_2_ = bf16[8,4736]{1,0:T(8,128)(2,1)S(1)} collective-permute-done((bf16[8,4736]{1,0:T(8,128)(2,1)S(1)}, bf16[8,4736]{1,0:T(8,128)(2,1)S(1)}, u32[]{:S(2)}, u32[]{:S(2)}) %collective-permute-start.1) | collective-permute-done | bytes 75808 | tf_op jit(solution)/shard_map/ppermute | solution.py:450
  26.8 0.0 collective-permute-done.2.refs_3_
  26.8 3.7 %collective-permute-done.3.refs_4_ = bf16[8,4736]{1,0:T(8,128)(2,1)S(1)} collective-permute-done((bf16[8,4736]{1,0:T(8,128)(2,1)S(1)}, bf16[8,4736]{1,0:T(8,128)(2,1)S(1)}, u32[]{:S(2)}, u32[]{:S(2)}) %collective-permute-start.3) | collective-permute-done | bytes 75808 | tf_op jit(solution)/shard_map/ppermute | solution.py:450
  30.4 1.6 %stage.6.refs_6_ = bf16[8,4736]{1,0:T(8,128)(2,1)S(1)} custom-call(s32[5]{0:T(128)S(1)} %stack.23.spot_ref, bf16[16,4736]{1,0:T(8,128)(2,1)S(1)} %get-tuple-element.67.refs_0_, bf16[8,4736]{1,0:T(8,128)(2,1)S(1)} %collective-permute-done.refs_1_, bf16[8,4736]{1,0:T(8,128)(2,1)S(1)} %collective-permute-done.1.refs_2_, ...), custom_call_target="tpu_custom_call" | custom-call | flops 1048576 | bytes 1048576 | tf_op jit(solution)/shard_map/stage/pallas_call | solution.py:442
  32.0 2.0 %collective-permute-start.4 = (bf16[8,4736]{1,0:T(8,128)(2,1)S(1)}, bf16[8,4736]{1,0:T(8,128)(2,1)S(1)}, u32[]{:S(2)}, u32[]{:S(2)}) collective-permute-start(bf16[8,4736]{1,0:T(8,128)(2,1)S(1)} %stage.6.refs_6_), channel_id=1, source_target_pairs={{0,2},{2,0},{4,6},{6,4},{1,3},{3,1},{5,7},{7,5},{8,10},{10,8},{12,... | collective-permute-start | bytes 227336 | tf_op jit(solution)/shard_map/ppermute | solution.py:450
  34.0 10.4 %collective-permute-done.4.refs_5_ = bf16[8,4736]{1,0:T(8,128)(2,1)S(1)} collective-permute-done((bf16[8,4736]{1,0:T(8,128)(2,1)S(1)}, bf16[8,4736]{1,0:T(8,128)(2,1)S(1)}, u32[]{:S(2)}, u32[]{:S(2)}) %collective-permute-start.4) | collective-permute-done | bytes 75808 | tf_op jit(solution)/shard_map/ppermute | solution.py:450
  44.5 1.9 %stage.7 = (bf16[3,2,4096]{2,1,0:T(2,128)(2,1)S(1)}, bf16[24,128]{1,0:T(8,128)(2,1)S(1)}, bf16[24,128]{1,0:T(8,128)(2,1)S(1)}) custom-call(s32[5]{0:T(128)S(1)} %stack.23.spot_ref, bf16[16,4736]{1,0:T(8,128)(2,1)S(1)} %get-tuple-element.67.refs_0_, bf16[8,4736]{1,0:T(8,128)(2,1)S(1)} %collective-permute-done.refs_1_, ...), custom_call_target="tpu_custom_call" | custom-call | flops 1048576 | bytes 1048576 | tf_op jit(solution)/shard_map/stage/pallas_call | solution.py:442
  46.4 4.7 %collective-permute-start.6 = (bf16[3,2,4096]{2,1,0:T(2,128)(2,1)S(1)}, bf16[3,2,4096]{2,1,0:T(2,128)(2,1)S(1)}, u32[]{:S(2)}, u32[]{:S(2)}) collective-permute-start(bf16[3,2,4096]{2,1,0:T(2,128)(2,1)S(1)} %get-tuple-element.78), channel_id=1, source_target_pairs={{0,4},{2,6},{4,0},{6,2},{1,5},{3,7},{5,1},{7,3},{8,12},{10,14},{12... | collective-permute-start | bytes 147464 | tf_op jit(solution)/shard_map/ppermute | solution.py:456
  51.0 0.1 collective-permute-start.5
  51.1 0.1 copy.11.id_col_ref
  51.2 6.7 %collective-permute-done.5.got_ref = bf16[24,128]{1,0:T(8,128)(2,1)S(1)} collective-permute-done((bf16[24,128]{1,0:T(8,128)(2,1)S(1)}, bf16[24,128]{1,0:T(8,128)(2,1)S(1)}, u32[]{:S(2)}, u32[]{:S(2)}) %collective-permute-start.5) | collective-permute-done | bytes 6176 | tf_op jit(solution)/shard_map/ppermute | solution.py:455
  57.9 2.2 %plan.1 = (s32[8,128]{1,0:T(8,128)S(1)}, f32[2,128]{1,0:T(2,128)S(1)}, f32[1,128]{1,0:T(1,128)}, s32[1]{0:T(128)}) custom-call(s32[5]{0:T(128)S(1)} %stack.23.spot_ref, f32[32,1]{1,0:T(8,128)S(1)} %copy.11.id_col_ref, f32[1,32]{1,0:T(1,128)S(1)} %get-tuple-element.99.id_row_ref, bf16[24,128]{1,0:T(8,128)(2,1)S(1)} %get-tuple-element.72.own_ref, ...), custom_call_target="tpu_custom_call" | custom-call | flops 1048576 | bytes 1048576 | tf_op jit(solution)/shard_map/plan/pallas_call | solution.py:465
  60.2 0.0 collective-permute-done.6.refs_6_
  60.2 0.0 all-to-all-done.1.tokens_ref
  60.2 0.0 copy-start.3
  60.2 0.0 copy-start.5
  60.2 2.7 %place.3 = bf16[128,64,128]{2,1,0:T(8,128)(2,1)} custom-call(s32[8,128]{1,0:T(8,128)S(1)} %get-tuple-element.117.slot_ref, f32[2,128]{1,0:T(2,128)S(1)} %get-tuple-element.118.weight_ref, bf16[224,32,128]{2,1,0:T(8,128)(2,1)S(1)} %all-to-all-done.1.tokens_ref, bf16[16,4736]{1,0:T(8,128)(2,1)S(1)} %get-tuple-element.67.refs_0_, ...), custom_call_target="tpu_custom_call" | custom-call | flops 1048576 | bytes 1048576 | tf_op jit(solution)/shard_map/place/pallas_call | solution.py:474
  63.0 0.7 %while.9 = (s32[1]{0:T(128)}, bf16[128,2,4096]{2,1,0:T(2,128)(2,1)}, s32[5]{0:T(128)S(1)}, s32[1,128]{1,0:T(1,128)S(1)}, s32[1,128]{1,0:T(1,128)S(1)}, /*index=5...) while((s32[1]{0:T(128)}, ...), condition=%region_1.0_spmd, body=%region_0.0_spmd | while | flops 2097153 | bytes 28836024 | solution.py:502
  (14 shorter events, 0.0 us)
Async XLA Ops:
  3.9 1.2 %copy-start.1 = (bf16[224,32,128]{2,1,0:T(8,128)(2,1)}, bf16[224,32,128]{2,1,0:T(8,128)(2,1)S(1)}, u32[]{:S(2)}) copy-start(bf16[224,32,128]{2,1,0:T(8,128)(2,1)S(1)} %get-tuple-element.77) | copy-start | bytes 5505028
  5.1 7.4 %copy-start.2 = (s32[128]{0:T(128)S(1)}, s32[128]{0:T(128)}, u32[]{:S(2)}) copy-start(s32[128]{0:T(128)} %param.14) | copy-start | bytes 1540
  5.1 7.4 %copy-start.6 = (s32[128]{0:T(128)S(1)}, s32[128]{0:T(128)}, u32[]{:S(2)}) copy-start(s32[128]{0:T(128)} %param.12) | copy-start | bytes 1540
  5.1 7.4 %copy-start.7 = (s32[128]{0:T(128)S(1)}, s32[128]{0:T(128)}, u32[]{:S(2)}) copy-start(s32[128]{0:T(128)} %param.13) | copy-start | bytes 1540
  5.1 28.9 %copy-start.8 = (s32[32]{0:T(128)S(1)}, s32[32]{0:T(128)}, u32[]{:S(2)}) copy-start(s32[32]{0:T(128)} %constant.34.clone) | copy-start | bytes 388
  5.1 28.9 %copy-start.9 = (s32[32]{0:T(128)S(1)}, s32[32]{0:T(128)}, u32[]{:S(2)}) copy-start(s32[32]{0:T(128)} %constant.35.clone) | copy-start | bytes 388
  5.1 28.9 %copy-start.10 = (s32[32]{0:T(128)S(1)}, s32[32]{0:T(128)}, u32[]{:S(2)}) copy-start(s32[32]{0:T(128)} %constant.36.clone) | copy-start | bytes 388
  5.1 55.1 %all-to-all-start.1 = ((bf16[224,32,128]{2,1,0:T(8,128)(2,1)}), bf16[224,32,128]{2,1,0:T(8,128)(2,1)S(1)}, u32[]{:S(2)}, u32[]{:S(2)}) async-start(bf16[224,32,128]{2,1,0:T(8,128)(2,1)} %copy-done.1), calls=%async_computation.1 | async-start | bytes 3670016 | tf_op jit(solution)/shard_map/all_to_all | solution.py:419
  13.8 1.3 %collective-permute-start = (bf16[8,4736]{1,0:T(8,128)(2,1)S(1)}, bf16[8,4736]{1,0:T(8,128)(2,1)S(1)}, u32[]{:S(2)}, u32[]{:S(2)}) collective-permute-start(bf16[8,4736]{1,0:T(8,128)(2,1)S(1)} %get-tuple-element.68.refs_2_), channel_id=1, source_target_pairs={{0,1},{1,0},{2,3},{3,2},{4,5},{5,4},{6,7},{7,6},{8,9},{9,8},{10,11... | collective-permute-start | bytes 227336 | tf_op jit(solution)/shard_map/ppermute | solution.py:450
  16.2 10.6 %collective-permute-start.1 = (bf16[8,4736]{1,0:T(8,128)(2,1)S(1)}, bf16[8,4736]{1,0:T(8,128)(2,1)S(1)}, u32[]{:S(2)}, u32[]{:S(2)}) collective-permute-start(bf16[8,4736]{1,0:T(8,128)(2,1)S(1)} %get-tuple-element.69.refs_5_), channel_id=1, source_target_pairs={{0,8},{8,0},{16,24},{24,16},{1,9},{9,1},{17,25},{25,17},{2,10},{10... | collective-permute-start | bytes 227336 | tf_op jit(solution)/shard_map/ppermute | solution.py:450
  18.0 8.7 %collective-permute-start.2 = (bf16[8,4736]{1,0:T(8,128)(2,1)S(1)}, bf16[8,4736]{1,0:T(8,128)(2,1)S(1)}, u32[]{:S(2)}, u32[]{:S(2)}) collective-permute-start(bf16[8,4736]{1,0:T(8,128)(2,1)S(1)} %get-tuple-element.70), channel_id=1, source_target_pairs={{0,16},{8,24},{16,0},{24,8},{1,17},{9,25},{17,1},{25,9},{2,18},{10... | collective-permute-start | bytes 227336 | tf_op jit(solution)/shard_map/ppermute | solution.py:450
  19.5 10.9 %collective-permute-start.3 = (bf16[8,4736]{1,0:T(8,128)(2,1)S(1)}, bf16[8,4736]{1,0:T(8,128)(2,1)S(1)}, u32[]{:S(2)}, u32[]{:S(2)}) collective-permute-start(bf16[8,4736]{1,0:T(8,128)(2,1)S(1)} %get-tuple-element.71), channel_id=1, source_target_pairs={{0,24},{8,16},{16,8},{24,0},{1,25},{9,17},{17,9},{25,1},{2,26},{10... | collective-permute-start | bytes 227336 | tf_op jit(solution)/shard_map/ppermute | solution.py:450
  32.0 12.4 %collective-permute-start.4 = (bf16[8,4736]{1,0:T(8,128)(2,1)S(1)}, bf16[8,4736]{1,0:T(8,128)(2,1)S(1)}, u32[]{:S(2)}, u32[]{:S(2)}) collective-permute-start(bf16[8,4736]{1,0:T(8,128)(2,1)S(1)} %stage.6.refs_6_), channel_id=1, source_target_pairs={{0,2},{2,0},{4,6},{6,4},{1,3},{3,1},{5,7},{7,5},{8,10},{10,8},{12,... | collective-permute-start | bytes 227336 | tf_op jit(solution)/shard_map/ppermute | solution.py:450
  46.4 13.8 %collective-permute-start.6 = (bf16[3,2,4096]{2,1,0:T(2,128)(2,1)S(1)}, bf16[3,2,4096]{2,1,0:T(2,128)(2,1)S(1)}, u32[]{:S(2)}, u32[]{:S(2)}) collective-permute-start(bf16[3,2,4096]{2,1,0:T(2,128)(2,1)S(1)} %get-tuple-element.78), channel_id=1, source_target_pairs={{0,4},{2,6},{4,0},{6,2},{1,5},{3,7},{5,1},{7,3},{8,12},{10,14},{12... | collective-permute-start | bytes 147464 | tf_op jit(solution)/shard_map/ppermute | solution.py:456
  51.0 6.9 %collective-permute-start.5 = (bf16[24,128]{1,0:T(8,128)(2,1)S(1)}, bf16[24,128]{1,0:T(8,128)(2,1)S(1)}, u32[]{:S(2)}, u32[]{:S(2)}) collective-permute-start(bf16[24,128]{1,0:T(8,128)(2,1)S(1)} %get-tuple-element.73), channel_id=1, source_target_pairs={{0,4},{2,6},{4,0},{6,2},{1,5},{3,7},{5,1},{7,3},{8,12},{10,14},{12... | collective-permute-start | bytes 18440 | tf_op jit(solution)/shard_map/ppermute | solution.py:455
  60.2 2.8 %copy-start.3 = (bf16[128,2,4096]{2,1,0:T(2,128)(2,1)S(1)}, bf16[128,2,4096]{2,1,0:T(2,128)(2,1)}, u32[]{:S(2)}) copy-start(bf16[128,2,4096]{2,1,0:T(2,128)(2,1)} %param.10) | copy-start | bytes 6291460
  60.2 2.8 %copy-start.5 = (f32[4096]{0:T(1024)S(1)}, f32[4096]{0:T(1024)}, u32[]{:S(2)}) copy-start(f32[4096]{0:T(1024)} %param.11) | copy-start | bytes 49156
